TPU v7x, 32 devices: a whole 2x2x4 slice. The times are simulated.
32 devices in a mesh: rows: 32 (over z, y, x, core).
Axes of the slice: x: 2, y: 2, z: 4, core: 2. Of those that a mesh axis runs over, the one named last changes fastest.
Arguments:
- stiffness: float32 [9, 128, 512], P(None, 'rows'), may hold values from -400 to 806.1, as said below
- mass: float32 [9, 128, 512], P(None, 'rows'), may hold values from 0.05 to 3, as said below
- shifts: float32 [3], replicated, may hold values from 0.05 to 2
- factor: float32 [128, 32, 512], P('rows'), may hold values from -6 to 6
Outputs:
- lowrank: float32 [3, 128, 32, 512], P(None, 'rows')
- residual_factor: float32 [128, 32, 512], P('rows')
Inputs may be any that keep to these rules, and one draw needn't show every extreme that they name: `stiffness`: entry 4 along the first dimension exceeds the sum of the magnitudes of the other eight, which are negative. `mass`: entry 4 along the first dimension exceeds the sum of the other eight, which are positive.
All inputs are finite; a program needn't handle non-finite values.
Results may differ from a plain program's by a relative error of at most 0.0003.
Values sent between devices are 32-bit elements; how exact they have to be, the bound alone decides.
No kernel may reach another device: no remote copies, remote signals or barrier semaphores. Data moves between devices by JAX's collectives and lax.ppermute only.
A program may use at most 128 MiB of HBM per device.

v0:
```python
import jax
import jax.numpy as jnp
from jax import lax
from jax.sharding import PartitionSpec as P

STEPS = 3
ITERS = 4


OFFSETS = ((-1, -1), (-1, 0), (-1, 1), (0, -1), (0, 0), (0, 1), (1, -1), (1, 0), (1, 1))


def padded_2(block, sides, width):
    for axis, dim in sides:
        count = lax.axis_size(axis)
        forward = [(i, i + 1) for i in range(count - 1)]
        backward = [(target, source) for source, target in forward]
        low = lax.ppermute(
            lax.slice_in_dim(block, block.shape[dim] - width, None, axis=dim), axis, forward
        )
        high = lax.ppermute(lax.slice_in_dim(block, 0, width, axis=dim), axis, backward)
        block = jnp.concatenate([low, block, high], axis=dim)
    return block


def apply_stencil(coeffs, padded):
    height = coeffs.shape[1]
    breadth = padded.shape[2]
    framed = jnp.pad(padded, ((0, 0), (0, 0), (1, 1)))
    summed = jnp.zeros((height, padded.shape[1], breadth), padded.dtype)
    for stencil_entry, offset in enumerate(OFFSETS):
        shifted = framed[
            1 + offset[0] : 1 + offset[0] + height, :, 1 + offset[1] : 1 + offset[1] + breadth
        ]
        summed = summed + coeffs[stencil_entry][:, None, :] * shifted
    return summed


def shift_later(field, stride, filler):
    widths = [(0, 0)] * (field.ndim - 1) + [(stride, 0)]
    return jnp.pad(field[..., :-stride], widths, constant_values=filler)


def shift_earlier(field, stride, filler):
    widths = [(0, 0)] * (field.ndim - 1) + [(0, stride)]
    return jnp.pad(field[..., stride:], widths, constant_values=filler)


def line_factors(coeffs):
    breadth = coeffs.shape[2]
    column = lax.broadcasted_iota(jnp.int32, (1, breadth), 1)
    below_diag = jnp.where(column == 0, 0.0, coeffs[3])
    above_diag = jnp.where(column == breadth - 1, 0.0, coeffs[5])
    center = coeffs[4]
    levels = []
    stride = 1
    while stride < breadth:
        from_below = -below_diag / shift_later(center, stride, 1.0)
        from_above = -above_diag / shift_earlier(center, stride, 1.0)
        center = (
            center
            + from_below * shift_later(above_diag, stride, 0.0)
            + from_above * shift_earlier(below_diag, stride, 0.0)
        )
        next_below = from_below * shift_later(below_diag, stride, 0.0)
        next_above = from_above * shift_earlier(above_diag, stride, 0.0)
        below_diag = next_below
        above_diag = next_above
        levels.append((stride, from_below, from_above))
        stride = stride * 2
    return (levels, center)


def line_apply(solver_parts, vector):
    levels, center = solver_parts
    for stride, from_below, from_above in levels:
        vector = (
            vector
            + from_below[:, None, :] * shift_later(vector, stride, 0.0)
            + from_above[:, None, :] * shift_earlier(vector, stride, 0.0)
        )
    return vector / center[:, None, :]


def row_sums(field):
    return jnp.sum(field, axis=(0, 2))


def least_squares(columns, initial):
    count = len(columns)
    cosines = []
    sines = []
    rhs_list = [initial] + [jnp.zeros_like(initial) for onward in range(count)]
    upper_cols = []
    for position in range(count):
        column = list(columns[position])
        for earlier in range(position):
            first = cosines[earlier] * column[earlier] + sines[earlier] * column[earlier + 1]
            second = -sines[earlier] * column[earlier] + cosines[earlier] * column[earlier + 1]
            column[earlier] = first
            column[earlier + 1] = second
        radius = jnp.sqrt(
            column[position] * column[position] + column[position + 1] * column[position + 1]
        )
        cosine = column[position] / radius
        sine = column[position + 1] / radius
        cosines.append(cosine)
        sines.append(sine)
        column[position] = radius
        rhs_list[position + 1] = -sine * rhs_list[position]
        rhs_list[position] = cosine * rhs_list[position]
        upper_cols.append(column[: position + 1])
    solution = [None] * count
    for position in reversed(range(count)):
        accum = rhs_list[position]
        for onward in range(position + 1, count):
            accum = accum - upper_cols[onward][position] * solution[onward]
        solution[position] = accum / upper_cols[position][position]
    return solution


def shards(stiffness, mass, shifts, factor):
    current = factor
    pieces = []
    for adi_step in range(STEPS):
        shift_now = shifts[adi_step]
        coeffs = stiffness + shift_now * mass
        solver_parts = line_factors(coeffs)
        initial = jnp.sqrt(lax.psum(row_sums(current * current), "rows"))
        latest = current / initial[None, :, None]
        krylov = []
        directions = []
        columns = []
        for krylov_step in range(ITERS):
            direction = line_apply(solver_parts, latest)
            framed_direction = padded_2(direction, (("rows", 0),), 1)
            mapped = apply_stencil(coeffs, framed_direction)
            local_heights = jnp.stack([row_sums(vector * mapped) for vector in krylov + [latest]])
            dots, squares = lax.psum((local_heights, row_sums(latest * latest)), "rows")
            if krylov_step > 0:
                norm_prev = jnp.sqrt(squares)
                columns[-1].append(norm_prev)
                scale_back = 1.0 / norm_prev
                latest = latest * scale_back[None, :, None]
                mapped = mapped * scale_back[None, :, None]
                framed_direction = framed_direction * scale_back[None, :, None]
                heights = dots * scale_back[None, :]
                heights = heights.at[krylov_step].set(heights[krylov_step] * scale_back)
            else:
                heights = dots
            krylov.append(latest)
            directions.append(framed_direction)
            for earlier in range(krylov_step + 1):
                mapped = mapped - heights[earlier][None, :, None] * krylov[earlier]
            columns.append([heights[earlier] for earlier in range(krylov_step + 1)])
            divisor = jnp.ones((mapped.shape[1],), jnp.float32)
            if krylov_step + 1 == ITERS:
                remainder = jnp.sqrt(lax.psum(row_sums(mapped * mapped), "rows"))
                columns[-1].append(remainder)
            if krylov_step + 1 < ITERS:
                latest = mapped / divisor[None, :, None]
        weights = least_squares(columns, initial)
        framed_result = weights[0][None, :, None] * directions[0]
        for onward in range(1, ITERS):
            framed_result = framed_result + weights[onward][None, :, None] * directions[onward]
        result = framed_result[1:-1]
        framed_result = padded_2(result, (("rows", 0),), 1)
        pieces.append(jnp.sqrt(2.0 * shift_now) * result)
        current = current - 2.0 * shift_now * apply_stencil(mass, framed_result)
    return (jnp.stack(pieces), current)


def solution(mesh):
    in_specs = (P(None, "rows", None), P(None, "rows", None), P(), P("rows", None, None))
    out_specs = (P(None, "rows", None, None), P("rows", None, None))
    return jax.shard_map(shards, mesh=mesh, in_specs=in_specs, out_specs=out_specs, check_vma=False)
```

profile of v0, /device:TPU:0, one launch (start us, length us, event | category | flops | bytes accessed | tf_op | source)
XLA Modules:
  0.0 921.5 jit_solution(9883211213438943753)
XLA Ops:
  1.9 2.8 multiply_add_fusion.99
  8.1 42.0 %psum.189 = f32[32]{0:T(128)S(1)} all-reduce(f32[32]{0:T(128)S(1)} %multiply_reduce_fusion.44), channel_id=1, replica_groups=mesh['rows'=32] {'rows'}, use_global_device_ids=true, to_apply=%region_1.2 | all-reduce | flops 32 | bytes 256 | tf_op jit(solution)/shard_map/psum | solution.py:129
  62.8 44.0 %psum.190 = f32[32]{0:T(128)S(1)} all-reduce(f32[32]{0:T(128)S(1)} %get-tuple-element.263), channel_id=1, replica_groups=mesh['rows'=32] {'rows'}, use_global_device_ids=true, to_apply=%region_3.4 | all-reduce | flops 32 | bytes 256 | tf_op jit(solution)/shard_map/psum | solution.py:139
  112.3 4.3 collective-permute-done.3
  117.3 41.5 %all-reduce.395 = (f32[32]{0:T(128)S(1)}, f32[2,32]{1,0:T(2,128)S(1)}) all-reduce(f32[32]{0:T(128)S(1)} %get-tuple-element.145, f32[2,32]{1,0:T(2,128)S(1)} %pad_maximum_fusion.49), channel_id=1, replica_groups=mesh['rows'=32] {'rows'}, use_global_device_ids=true, to_apply=%region_5.6 | all-reduce | flops 96 | bytes 768 | tf_op jit(solution)/shard_map/psum | solution.py:139
  166.0 3.3 collective-permute-done.5
  170.0 42.5 %all-reduce.394 = (f32[32]{0:T(128)S(1)}, f32[3,32]{1,0:T(4,128)S(1)}) all-reduce(f32[32]{0:T(128)S(1)} %get-tuple-element.141, f32[3,32]{1,0:T(4,128)S(1)} %pad_maximum_fusion.43), channel_id=1, replica_groups=mesh['rows'=32] {'rows'}, use_global_device_ids=true, to_apply=%region_10.11 | all-reduce | flops 128 | bytes 1024 | tf_op jit(solution)/shard_map/psum | solution.py:139
  218.7 3.7 collective-permute-done.7
  223.2 41.5 %all-reduce.393 = (f32[32]{0:T(128)S(1)}, f32[4,32]{1,0:T(4,128)S(1)}) all-reduce(f32[32]{0:T(128)S(1)} %get-tuple-element.136, f32[4,32]{1,0:T(4,128)S(1)} %pad_maximum_fusion.44), channel_id=1, replica_groups=mesh['rows'=32] {'rows'}, use_global_device_ids=true, to_apply=%region_16.17 | all-reduce | flops 160 | bytes 1280 | tf_op jit(solution)/shard_map/psum | solution.py:139
  265.2 40.1 %psum.197 = f32[32]{0:T(128)S(1)} all-reduce(f32[32]{0:T(128)S(1)} %multiply_reduce_fusion.30), channel_id=1, replica_groups=mesh['rows'=32] {'rows'}, use_global_device_ids=true, to_apply=%region_23.24 | all-reduce | flops 32 | bytes 256 | tf_op jit(solution)/shard_map/psum | solution.py:158
  308.3 4.3 collective-permute-done.9
  313.4 42.4 %psum.198 = f32[32]{0:T(128)S(1)} all-reduce(f32[32]{0:T(128)S(1)} %get-tuple-element.254), channel_id=1, replica_groups=mesh['rows'=32] {'rows'}, use_global_device_ids=true, to_apply=%region_25.26 | all-reduce | flops 32 | bytes 256 | tf_op jit(solution)/shard_map/psum | solution.py:129
  361.4 4.3 collective-permute-done.11
  366.3 41.7 %psum.199 = f32[32]{0:T(128)S(1)} all-reduce(f32[32]{0:T(128)S(1)} %get-tuple-element.217), channel_id=1, replica_groups=mesh['rows'=32] {'rows'}, use_global_device_ids=true, to_apply=%region_27.28 | all-reduce | flops 32 | bytes 256 | tf_op jit(solution)/shard_map/psum | solution.py:139
  413.6 4.3 collective-permute-done.13
  418.6 42.4 %all-reduce.392 = (f32[32]{0:T(128)S(1)}, f32[2,32]{1,0:T(2,128)S(1)}) all-reduce(f32[32]{0:T(128)S(1)} %get-tuple-element.133, f32[2,32]{1,0:T(2,128)S(1)} %pad_maximum_fusion.50), channel_id=1, replica_groups=mesh['rows'=32] {'rows'}, use_global_device_ids=true, to_apply=%region_29.30 | all-reduce | flops 96 | bytes 768 | tf_op jit(solution)/shard_map/psum | solution.py:139
  472.2 41.6 %all-reduce.391 = (f32[32]{0:T(128)S(1)}, f32[3,32]{1,0:T(4,128)S(1)}) all-reduce(f32[32]{0:T(128)S(1)} %get-tuple-element.129, f32[3,32]{1,0:T(4,128)S(1)} %pad_maximum_fusion.45), channel_id=1, replica_groups=mesh['rows'=32] {'rows'}, use_global_device_ids=true, to_apply=%region_34.35 | all-reduce | flops 128 | bytes 1024 | tf_op jit(solution)/shard_map/psum | solution.py:139
  520.8 3.6 collective-permute-done.17
  525.2 42.4 %all-reduce.390 = (f32[32]{0:T(128)S(1)}, f32[4,32]{1,0:T(4,128)S(1)}) all-reduce(f32[32]{0:T(128)S(1)} %get-tuple-element.124, f32[4,32]{1,0:T(4,128)S(1)} %pad_maximum_fusion.46), channel_id=1, replica_groups=mesh['rows'=32] {'rows'}, use_global_device_ids=true, to_apply=%region_40.41 | all-reduce | flops 160 | bytes 1280 | tf_op jit(solution)/shard_map/psum | solution.py:139
  568.1 40.2 %psum.206 = f32[32]{0:T(128)S(1)} all-reduce(f32[32]{0:T(128)S(1)} %multiply_reduce_fusion.15), channel_id=1, replica_groups=mesh['rows'=32] {'rows'}, use_global_device_ids=true, to_apply=%region_47.48 | all-reduce | flops 32 | bytes 256 | tf_op jit(solution)/shard_map/psum | solution.py:158
  611.4 4.3 collective-permute-done.19
  617.0 42.2 %psum.207 = f32[32]{0:T(128)S(1)} all-reduce(f32[32]{0:T(128)S(1)} %get-tuple-element.208), channel_id=1, replica_groups=mesh['rows'=32] {'rows'}, use_global_device_ids=true, to_apply=%region_49.50 | all-reduce | flops 32 | bytes 256 | tf_op jit(solution)/shard_map/psum | solution.py:129
  664.8 4.3 collective-permute-done.21
  669.8 41.7 %psum.208 = f32[32]{0:T(128)S(1)} all-reduce(f32[32]{0:T(128)S(1)} %get-tuple-element.171), channel_id=1, replica_groups=mesh['rows'=32] {'rows'}, use_global_device_ids=true, to_apply=%region_51.52 | all-reduce | flops 32 | bytes 256 | tf_op jit(solution)/shard_map/psum | solution.py:139
  717.0 4.3 collective-permute-done.23
  722.0 42.2 %all-reduce.389 = (f32[32]{0:T(128)S(1)}, f32[2,32]{1,0:T(2,128)S(1)}) all-reduce(f32[32]{0:T(128)S(1)} %get-tuple-element.121, f32[2,32]{1,0:T(2,128)S(1)} %pad_maximum_fusion.51), channel_id=1, replica_groups=mesh['rows'=32] {'rows'}, use_global_device_ids=true, to_apply=%region_53.54 | all-reduce | flops 96 | bytes 768 | tf_op jit(solution)/shard_map/psum | solution.py:139
  770.3 4.3 collective-permute-done.25
  775.3 42.0 %all-reduce.388 = (f32[32]{0:T(128)S(1)}, f32[3,32]{1,0:T(4,128)S(1)}) all-reduce(f32[32]{0:T(128)S(1)} %get-tuple-element.117, f32[3,32]{1,0:T(4,128)S(1)} %pad_maximum_fusion.47), channel_id=1, replica_groups=mesh['rows'=32] {'rows'}, use_global_device_ids=true, to_apply=%region_58.59 | all-reduce | flops 128 | bytes 1024 | tf_op jit(solution)/shard_map/psum | solution.py:139
  824.7 3.7 collective-permute-done.27
  829.2 42.2 %all-reduce.387 = (f32[32]{0:T(128)S(1)}, f32[4,32]{1,0:T(4,128)S(1)}) all-reduce(f32[32]{0:T(128)S(1)} %get-tuple-element.112, f32[4,32]{1,0:T(4,128)S(1)} %pad_maximum_fusion.48), channel_id=1, replica_groups=mesh['rows'=32] {'rows'}, use_global_device_ids=true, to_apply=%region_64.65 | all-reduce | flops 160 | bytes 1280 | tf_op jit(solution)/shard_map/psum | solution.py:139
  871.9 40.1 %psum.215 = f32[32]{0:T(128)S(1)} all-reduce(f32[32]{0:T(128)S(1)} %multiply_reduce_fusion), channel_id=1, replica_groups=mesh['rows'=32] {'rows'}, use_global_device_ids=true, to_apply=%region_71.72 | all-reduce | flops 32 | bytes 256 | tf_op jit(solution)/shard_map/psum | solution.py:158
  916.0 3.4 collective-permute-done.29
  (732 shorter events, 106.9 us)
Async XLA Ops:
  53.0 9.2 collective-permute-start
  54.3 7.9 collective-permute-start.1
  56.5 415.0 %copy-start.2 = (f32[4,512]{1,0:T(4,128)}, f32[4,512]{1,0:T(4,128)S(1)}, u32[]{:S(2)}) copy-start(f32[4,512]{1,0:T(4,128)S(1)} %get-tuple-element.574) | copy-start | bytes 24580
  56.5 256.3 %copy-start.8 = (f32[4,512]{1,0:T(4,128)}, f32[4,512]{1,0:T(4,128)S(1)}, u32[]{:S(2)}) copy-start(f32[4,512]{1,0:T(4,128)S(1)} %get-tuple-element.577) | copy-start | bytes 24580
  109.7 2.6 collective-permute-start.2
  111.0 5.7 collective-permute-start.3
  162.3 3.7 collective-permute-start.4
  163.6 5.7 collective-permute-start.5
  215.5 3.2 collective-permute-start.6
  216.8 5.7 collective-permute-start.7
  305.7 2.7 collective-permute-start.8
  307.0 5.7 collective-permute-start.9
  358.8 2.6 collective-permute-start.10
  360.1 5.7 collective-permute-start.11
  411.0 2.6 collective-permute-start.12
  412.3 5.7 collective-permute-start.13
  464.5 4.4 collective-permute-start.14
  465.8 5.7 collective-permute-start.15
  517.5 3.3 collective-permute-start.16
  518.8 5.7 collective-permute-start.17
  608.8 2.7 collective-permute-start.18
  610.1 5.7 collective-permute-start.19
  662.2 2.6 collective-permute-start.20
  663.5 5.7 collective-permute-start.21
  714.4 2.6 collective-permute-start.22
  715.7 5.7 collective-permute-start.23
  767.7 2.6 collective-permute-start.24
  769.0 5.7 collective-permute-start.25
  821.5 3.2 collective-permute-start.26
  822.8 5.7 collective-permute-start.27
  912.4 3.6 collective-permute-start.28
  913.7 5.7 collective-permute-start.29
  (93 other events, 4091.0 us)
where the time goes:
time: 936 us; the launch traced here: 922 us
  blocking collectives  753 us (80%)
  waiting for transfers between devices  54.9 us (6%)
  starting transfers between devices  39.2 us (4%)
  other arithmetic  36.1 us (4%)
  local copies, waits for them, and re-layouts  31.7 us (3%)
    psum x12, blocking collectives, shards(): dots, squares = lax.psum((local_heights, row_sums(latest * latest)), 'rows')  506 us
    psum x3, blocking collectives, shards(): initial = jnp.sqrt(lax.psum(row_sums(current * current), 'rows'))  127 us
    psum x3, blocking collectives, shards(): remainder = jnp.sqrt(lax.psum(row_sums(mapped * mapped), 'rows'))  120 us
    ppermute x15, waiting for transfers between devices, padded_2(): lax.ppermute(lax.slice_in_dim(block, 0, width, axis=dim), axis, backward)  54.9 us
    ppermute x15, starting transfers between devices, padded_2(): lax.ppermute(lax.slice_in_dim(block, 0, width, axis=dim), axis, backward)  19.8 us
    ppermute x15, starting transfers between devices, padded_2(): lax.ppermute(lax.slice_in_dim(block, block.shape[dim] - width, None, axis...  19.4 us
  transfers between devices with their start and end apart: 30, of which 14 were waited for; matrix products, arithmetic and copies ran while one was open for 1% of the time, Pallas kernels for 0%

commit v1 on v0

v1 whole, which is shorter than its diff:
```python
import functools

import jax
import jax.numpy as jnp
from jax import lax
from jax.experimental import pallas as pl
from jax.experimental.pallas import tpu as pltpu
from jax.sharding import PartitionSpec as P

ITERS = 4
CELLS = 4
LANES = 128
PIVOT_TOL = 3e-7
OFFSETS = ((-1, -1), (-1, 0), (-1, 1), (0, -1), (0, 0), (0, 1), (1, -1), (1, 0), (1, 1))
OFF_ROW = (0, 1, 2, 6, 7, 8)
PAIRS = [(i, j) for i in range(ITERS + 1) for j in range(i, ITERS + 1)]


E1, E2, G0, G1, G2, C0, C1, A3, C3, L0, L1, L2, R0, R1, R2, INV = range(16)
LEVELS = 16


def roll(x, shift, axis=-1):
    axis = axis % x.ndim
    return pltpu.roll(x, shift % x.shape[axis], axis)


def params():
    return pltpu.CompilerParams(vmem_limit_bytes=40 * 1024 * 1024)


def to_chunks(natural, stage):
    tiles = natural.shape[1] // LANES
    for tile in range(tiles):
        stage[tile * LANES : (tile + 1) * LANES, :] = natural[:, tile * LANES : (tile + 1) * LANES].T
    return [stage[pl.ds(cell, LANES, stride=CELLS), :].T for cell in range(CELLS)]


def from_chunks(planes, stage):
    for cell in range(CELLS):
        stage[pl.ds(cell, LANES, stride=CELLS), :] = planes[cell].T
    return [stage[tile * LANES : (tile + 1) * LANES, :].T for tile in range(CELLS)]


def pack_kernel(stiff_ref, mass_ref, factor_ref, out_ref, stage, gather):
    rows, cols, width = factor_ref.shape
    planes = to_chunks(factor_ref[...].reshape(rows * cols, width), stage)
    for cell in range(CELLS):
        out_ref[cell, 0 : rows * cols, :] = planes[cell]
    entries = len(OFFSETS)
    gather[...] = jnp.zeros(gather.shape, jnp.float32)
    for which, ref in enumerate((stiff_ref, mass_ref)):
        for entry in range(entries):
            at = (which * entries + entry) * rows
            gather[at : at + rows, :] = ref[entry]
    planes = to_chunks(gather[...], stage)
    count = 2 * entries * rows
    lane = lax.broadcasted_iota(jnp.int32, (count, LANES), 1)
    line = lax.broadcasted_iota(jnp.int32, (count, LANES), 0)
    column = (line // rows) % 3
    for cell in range(CELLS):
        plane = planes[cell][0:count, :]
        if cell == 0:
            plane = jnp.where((lane == 0) & (column == 0), 0.0, plane)
        if cell == CELLS - 1:
            plane = jnp.where((lane == LANES - 1) & (column == 2), 0.0, plane)
        out_ref[cell, rows * cols : rows * cols + count, :] = plane


def build_line_factors(diag, factors, rows_ext):
    def put(index, value):
        factors[index, 0:rows_ext, :] = value

    a = [diag(3, cell) for cell in range(CELLS)]
    d = [diag(4, cell) for cell in range(CELLS)]
    c = [diag(5, cell) for cell in range(CELLS)]
    d = [jnp.where(x <= 0.0, 1.0, x) for x in d]
    g0 = 1.0 / d[0]
    e1 = a[1] * g0
    g1 = 1.0 / (d[1] - e1 * c[0])
    e2 = a[2] * g1
    g2 = 1.0 / (d[2] - e2 * c[1])
    f0 = -a[0]
    f1 = -e1 * f0
    f2 = -e2 * f1
    l2 = f2 * g2
    l1 = (f1 - c[1] * l2) * g1
    l0 = (f0 - c[0] * l1) * g0
    r2 = -c[2] * g2
    r1 = -c[1] * r2 * g1
    r0 = -c[0] * r1 * g0
    below = a[3] * l2
    center = d[3] + a[3] * r2 + c[3] * roll(l0, -1)
    above = c[3] * roll(r0, -1)
    for index, value in (
        (E1, e1), (E2, e2), (G0, g0), (G1, g1), (G2, g2), (C0, c[0]), (C1, c[1]), (A3, a[3]),
        (C3, c[3]), (L0, l0), (L1, l1), (L2, l2), (R0, r0), (R1, r1), (R2, r2),
    ):
        put(index, value)
    stride = 1
    slot = LEVELS
    while stride < LANES:
        inverse = 1.0 / center
        from_below = -below * roll(inverse, stride)
        from_above = -above * roll(inverse, -stride)
        center = center + from_below * roll(above, stride) + from_above * roll(below, -stride)
        below = from_below * roll(below, stride)
        above = from_above * roll(above, -stride)
        put(slot, from_below)
        put(slot + 1, from_above)
        slot += 2
        stride *= 2
    put(INV, 1.0 / center)


def level_count():
    return LANES.bit_length() - 1


def line_solve(factors, read, rows, cols, write):
    def coef(index, row):
        return factors[index, row : row + 1, :]

    p0, p1, p2, s = [], [], [], []
    for row in rows:
        v0, v1, v2, v3 = (read(cell, row) for cell in range(CELLS))
        f1 = v1 - coef(E1, row) * v0
        f2 = v2 - coef(E2, row) * f1
        x2 = f2 * coef(G2, row)
        x1 = (f1 - coef(C1, row) * x2) * coef(G1, row)
        x0 = (v0 - coef(C0, row) * x1) * coef(G0, row)
        p0.append(x0)
        p1.append(x1)
        p2.append(x2)
        s.append(v3 - coef(A3, row) * x2 - coef(C3, row) * roll(x0, -1))
    stride = 1
    slot = LEVELS
    while stride < LANES:
        for at, row in enumerate(rows):
            if 2 * stride == LANES:
                both = coef(slot, row) + coef(slot + 1, row)
                s[at] = s[at] + both * roll(s[at], stride)
            else:
                s[at] = (
                    s[at]
                    + coef(slot, row) * roll(s[at], stride)
                    + coef(slot + 1, row) * roll(s[at], -stride)
                )
        slot += 2
        stride *= 2
    for at, row in enumerate(rows):
        x3 = s[at] * coef(INV, row)
        before = roll(x3, 1)
        x0 = p0[at] + coef(L0, row) * before + coef(R0, row) * x3
        x1 = p1[at] + coef(L1, row) * before + coef(R1, row) * x3
        x2 = p2[at] + coef(L2, row) * before + coef(R2, row) * x3
        write(row, (before, x0, x1, x2, x3, roll(x0, -1)))


def stencil_rows(coef, entries, read, row):
    out = []
    for cell in range(CELLS):
        total = None
        for entry in entries:
            offset = OFFSETS[entry]
            term = coef(entry, cell) * read(1 + cell + offset[1], row + offset[0])
            total = term if total is None else total + term
        out.append(total)
    return out


def krylov_kernel(
    parity_ref, shift_ref, mine_ref, even_ref, odd_ref, coefs_in, *refs, step, first, rows, cols, peers
):
    if first:
        coefs_ref, z_out, gram_out, wx, zx, line, factors = refs
    else:
        z_out, gram_out, wx, zx, line, factors = refs
        coefs_ref = coefs_in
    ext = 3 * rows
    entries = len(OFFSETS)
    block = rows * cols
    parity = parity_ref[0]
    at_even = jnp.where(parity == 0, 2 * rows, 0)
    at_odd = 2 * rows - at_even
    wx[0, :, pl.ds(rows * cols, block), :] = mine_ref[:, 0:block, :]
    wx[0, :, pl.ds(pl.multiple_of(at_even * cols, cols), block), :] = even_ref[:, 0:block, :]
    wx[0, :, pl.ds(pl.multiple_of(at_odd * cols, cols), block), :] = odd_ref[:, 0:block, :]
    if first:
        low_is_even = parity == 1
        for which in range(2):
            for entry in range(entries):
                at = block + (which * entries + entry) * rows
                for cell in range(CELLS):
                    even = even_ref[cell, at : at + rows, :]
                    odd = odd_ref[cell, at : at + rows, :]
                    coefs_ref[which, entry, cell, 0:rows, :] = jnp.where(low_is_even, even, odd)
                    coefs_ref[which, entry, cell, rows : 2 * rows, :] = mine_ref[cell, at : at + rows, :]
                    coefs_ref[which, entry, cell, 2 * rows : ext, :] = jnp.where(low_is_even, odd, even)
    shift = shift_ref[step]
    for entry in range(entries):
        for cell in range(CELLS):
            line[entry, cell, 0:ext, :] = (
                coefs_ref[0, entry, cell, 0:ext, :] + shift * coefs_ref[1, entry, cell, 0:ext, :]
            )
    build_line_factors(lambda entry, cell: line[entry, cell, 0:ext, :], factors, ext)

    for k in range(ITERS):
        low, high = k, ext - k

        def read_w(cell, row):
            return wx[k, cell, row * cols : (row + 1) * cols, :]

        def write_z(row, slots):
            for slot, value in enumerate(slots):
                zx[slot, row * cols : (row + 1) * cols, :] = value
            if rows - 1 <= row <= 2 * rows:
                at = (row - rows + 1) * cols
                for cell in range(CELLS):
                    z_out[k, cell, at : at + cols, :] = slots[1 + cell]

        for row in range(low, high, 2):
            line_solve(factors, read_w, list(range(row, min(row + 2, high))), cols, write_z)

        def read_z(slot, row):
            return zx[slot, row * cols : (row + 1) * cols, :]

        for row in range(low + 1, high - 1):
            image = stencil_rows(lambda entry, cell: line[entry, cell, row : row + 1, :], OFF_ROW, read_z, row)
            for cell in range(CELLS):
                wx[k + 1, cell, row * cols : (row + 1) * cols, :] = image[cell]

    lane = lax.broadcasted_iota(jnp.int32, (8, LANES), 1)
    packed = jnp.zeros((8, LANES), jnp.float32)
    for tile in range(cols // 8):
        sums = [None] * 16
        for row in range(rows, 2 * rows):
            for cell in range(CELLS):
                at = row * cols + tile * 8
                w = [wx[k, cell, at : at + 8, :] for k in range(ITERS + 1)]
                for index, (i, j) in enumerate(PAIRS):
                    term = w[i] * w[j]
                    sums[index] = term if sums[index] is None else sums[index] + term
        sums[15] = jnp.zeros((8, LANES), jnp.float32)
        half = LANES // 2
        while len(sums) > 1:
            mask = (lane % (2 * half)) < half
            count = len(sums) // 2
            sums = [
                jnp.where(
                    mask,
                    sums[i] + roll(sums[i], -half),
                    sums[i + count] + roll(sums[i + count], half),
                )
                for i in range(count)
            ]
            half //= 2
        total = sums[0]
        while half >= 1:
            total = total + roll(total, -half)
            half //= 2
        packed = jnp.where(lane % 8 == tile, roll(total, tile), packed)
    lower = roll(roll(packed, 4, 0), 4)
    packed = jnp.where(lane % 8 < 4, packed, lower)[0:4, :]
    gram_out[...] = jnp.broadcast_to(packed[None], (peers, 4, LANES))


def weights_of(gram):
    g = {}
    for index, (i, j) in enumerate(PAIRS):
        value = roll(gram, -8 * index)
        g[i, j] = value
        g[j, i] = value
    upper = [
        [(g[i, j] + g[i + 1, j + 1]) + (g[i, j + 1] + g[i + 1, j]) for j in range(ITERS)] for i in range(ITERS)
    ]
    diag = [upper[i][i] for i in range(ITERS)]
    right = [g[0, i] + g[0, i + 1] for i in range(ITERS)]
    inverse = [None] * ITERS
    for k in range(ITERS):
        good = upper[k][k] > PIVOT_TOL * diag[k]
        inverse[k] = jnp.where(good, 1.0 / jnp.where(good, upper[k][k], 1.0), 0.0)
        for i in range(k + 1, ITERS):
            scale = upper[k][i] * inverse[k]
            for j in range(i, ITERS):
                upper[i][j] = upper[i][j] - scale * upper[k][j]
            right[i] = right[i] - scale * right[k]
    y = [None] * ITERS
    for k in reversed(range(ITERS)):
        value = right[k]
        for j in range(k + 1, ITERS):
            value = value - upper[k][j] * y[j]
        y[k] = value * inverse[k]
    return y


def update_kernel(shift_ref, gram_ref, z_ref, mine_ref, coefs_ref, *refs, step, first, last, rows, cols):
    if not first:
        refs = refs[1:]
    low_out, next_out, ux, yx, own, stage = refs
    total = gram_ref[0]
    for peer in range(1, gram_ref.shape[0]):
        total = total + gram_ref[peer]
    gram = jnp.concatenate([total, roll(total, -4)], axis=0)
    y = weights_of(gram)
    for k in range(ITERS):
        for tile in range(cols // 8):
            yx[k, tile * 8 : tile * 8 + 8, :] = jnp.broadcast_to(y[k][:, tile : tile + 1], (8, LANES))
    shift = shift_ref[step]
    for row in range(rows + 2):
        at = slice(row * cols, (row + 1) * cols)
        u = []
        for cell in range(CELLS):
            value = yx[0] * z_ref[0, cell, at, :]
            for k in range(1, ITERS):
                value = value + yx[k] * z_ref[k, cell, at, :]
            u.append(value)
        for slot, value in enumerate((roll(u[CELLS - 1], 1), *u, roll(u[0], -1))):
            ux[slot, at, :] = value

    def read_u(slot, row):
        return ux[slot, row * cols : (row + 1) * cols, :]

    double = 2.0 * shift
    for row in range(rows):
        image = stencil_rows(
            lambda entry, cell: coefs_ref[1, entry, cell, rows + row : rows + row + 1, :],
            range(len(OFFSETS)), read_u, row + 1,
        )
        for cell in range(CELLS):
            at = slice(row * cols, (row + 1) * cols)
            value = mine_ref[cell, at, :] - double * image[cell]
            if last:
                own[cell, at, :] = value
            else:
                next_out[cell, at, :] = value

    width = CELLS * LANES
    root = jnp.sqrt(jnp.broadcast_to(double, (1, LANES)))
    block = rows * cols
    tiles = from_chunks([root * ux[1 + cell, cols : cols + block, :] for cell in range(CELLS)], stage)
    for tile in range(len(tiles)):
        low_out[0, :, :, tile * LANES : (tile + 1) * LANES] = tiles[tile].reshape(rows, cols, LANES)
    if last:
        tiles = from_chunks([own[cell] for cell in range(CELLS)], stage)
        for tile in range(len(tiles)):
            next_out[:, :, tile * LANES : (tile + 1) * LANES] = tiles[tile].reshape(rows, cols, LANES)


def vmem():
    return pl.BlockSpec(memory_space=pltpu.VMEM)


def smem():
    return pl.BlockSpec(memory_space=pltpu.SMEM)


def shards(stiffness, mass, shifts, factor):
    rows, cols, width = factor.shape
    steps = shifts.shape[0]
    entries = len(OFFSETS)
    peers = lax.axis_size("rows")
    parity = (lax.axis_index("rows") % 2).astype(jnp.int32).reshape(1)
    block = rows * cols
    ext = 3 * rows
    ext_pad = -(-ext // 8) * 8
    f32 = jnp.float32

    within = [(i, i ^ 1) for i in range(peers) if i ^ 1 < peers]
    across = [(i, i + 1) for i in range(1, peers - 1, 2)]
    across = across + [(b, a) for a, b in across]

    def exchange(x):
        return lax.ppermute(x, "rows", within), lax.ppermute(x, "rows", across)

    mine = pl.pallas_call(
        pack_kernel,
        in_specs=[vmem(), vmem(), vmem()],
        out_specs=vmem(),
        out_shape=jax.ShapeDtypeStruct((CELLS, block + 2 * entries * rows, LANES), f32),
        scratch_shapes=[pltpu.VMEM((width, LANES), f32), pltpu.VMEM((LANES, width), f32)],
        compiler_params=params(),
        name="pack",
    )(stiffness, mass, factor)

    coefs = None
    lowrank = None
    for step in range(steps):
        even, odd = exchange(mine)
        coef_shape = jax.ShapeDtypeStruct((2, entries, CELLS, ext_pad, LANES), f32)
        out_shape = [
            jax.ShapeDtypeStruct((ITERS, CELLS, (rows + 2) * cols, LANES), f32),
            jax.ShapeDtypeStruct((peers, 4, LANES), f32),
        ]
        if step == 0:
            out_shape = [coef_shape] + out_shape
        outs = pl.pallas_call(
            functools.partial(
                krylov_kernel, step=step, first=step == 0, rows=rows, cols=cols, peers=peers
            ),
            in_specs=[smem(), smem(), vmem(), vmem(), vmem(), vmem()],
            out_specs=[vmem() for shape in out_shape],
            out_shape=out_shape,
            scratch_shapes=[
                pltpu.VMEM((ITERS + 1, CELLS, ext * cols, LANES), f32),
                pltpu.VMEM((CELLS + 2, ext * cols, LANES), f32),
                pltpu.VMEM((entries, CELLS, ext_pad, LANES), f32),
                pltpu.VMEM((LEVELS + 2 * level_count(), ext_pad, LANES), f32),
            ],
            compiler_params=params(),
            name=f"krylov{step}",
        )(parity, shifts, mine, even, odd, shifts.reshape(1, -1) if step == 0 else coefs)
        if step == 0:
            coefs = outs[0]
            outs = outs[1:]
        z, gram = outs
        gram = lax.all_to_all(gram, "rows", 0, 0)
        last = step + 1 == steps
        next_shape = (rows, cols, width) if last else (CELLS, block, LANES)
        out = pl.pallas_call(
            functools.partial(
                update_kernel, step=step, first=step == 0, last=last, rows=rows, cols=cols
            ),
            grid=(1,),
            in_specs=[smem(), vmem(), vmem(), vmem(), vmem()]
            + ([] if step == 0 else [pl.BlockSpec(memory_space=pl.ANY)]),
            out_specs=[
                pl.BlockSpec((1, rows, cols, width), lambda i, step=step: (step, 0, 0, 0)),
                vmem(),
            ],
            out_shape=[
                jax.ShapeDtypeStruct((steps, rows, cols, width), f32),
                jax.ShapeDtypeStruct(next_shape, f32),
            ],
            scratch_shapes=[
                pltpu.VMEM((CELLS + 2, (rows + 2) * cols, LANES), f32),
                pltpu.VMEM((ITERS, cols, LANES), f32),
                pltpu.VMEM((CELLS, block, LANES), f32),
                pltpu.VMEM((width, LANES), f32),
            ],
            input_output_aliases={} if step == 0 else {5: 0},
            compiler_params=params(),
            name=f"update{step}",
        )(*((shifts, gram, z, mine, coefs) + (() if step == 0 else (lowrank,))))
        lowrank, mine = out
    return lowrank, mine


def solution(mesh):
    in_specs = (P(None, "rows", None), P(None, "rows", None), P(), P("rows", None, None))
    out_specs = (P(None, "rows", None, None), P("rows", None, None))
    return jax.shard_map(shards, mesh=mesh, in_specs=in_specs, out_specs=out_specs, check_vma=False)
```

time: 936 us -> 102 us (0.11); the launches traced: 922 us -> 102 us
  blocking collectives: 753 us -> 53.9 us
  waiting for transfers between devices: 54.9 us -> 3.7 us
  other arithmetic: 36.1 us -> 0 us
  Pallas kernels: 0 us -> 29.7 us
  starting transfers between devices: 39.2 us -> 10.3 us
  local copies, waits for them, and re-layouts: 31.7 us -> 3.37 us
    psum x18 -> x0, blocking collectives: 753 us -> none  [the longest x12 506 us: shards(): dots, squares = lax.psum((local_heights, row_sums(latest * latest)), 'rows')]
    all_to_all x0 -> x3, blocking collectives: none -> 53.9 us  [shards(): gram = lax.all_to_all(gram, 'rows', 0, 0)]
    ppermute x30 -> x6, waiting for transfers between devices: 54.9 us -> 3.7 us  [exchange(): return (lax.ppermute(x, 'rows', within), lax.ppermute(x, 'rows', across))]
    pallas_call x0 -> x7, Pallas kernels: none -> 29.7 us  [the longest x3 23 us: shards(): pl.pallas_call(functools.partial(krylov_kernel, step=step, first=step ==...]
    ppermute x30 -> x6, starting transfers between devices: 39.2 us -> 10.3 us  [exchange(): return (lax.ppermute(x, 'rows', within), lax.ppermute(x, 'rows', across))]
    slice x203 -> x0, local copies, waits for them, and re-layouts: 18.7 us -> none  [the longest x159 15.3 us: shift_later(): return jnp.pad(field[..., :-stride], widths, constant_values=filler)]
    add x126 -> x0, other arithmetic: 18 us -> none  [the longest x96 12.8 us: line_apply(): vector + from_below[:, None, :] * shift_later(vector, stride, 0.0)]
    reduce_sum x18 -> x0, other arithmetic: 9.81 us -> none  [row_sums(): return jnp.sum(field, axis=(0, 2))]
  transfers between devices with their start and end apart: 30 -> 6, of which waited for: 14 -> 3; matrix products, arithmetic and copies ran while one was open for 1% -> 0% of each run, Pallas kernels for 0% -> 0%
where the time goes in v1:
time: 102 us
  blocking collectives  53.9 us (53%)
  Pallas kernels  29.7 us (29%)
  starting transfers between devices  10.3 us (10%)
  waiting for transfers between devices  3.7 us (4%)
  local copies, waits for them, and re-layouts  3.37 us (3%)
    all_to_all x3, blocking collectives, shards(): gram = lax.all_to_all(gram, 'rows', 0, 0)  53.9 us
    pallas_call x3, Pallas kernels, shards(): pl.pallas_call(functools.partial(krylov_kernel, step=step, first=step ==...  23 us
    ppermute x6, starting transfers between devices, exchange(): return (lax.ppermute(x, 'rows', within), lax.ppermute(x, 'rows', across))  10.3 us
    pallas_call x3, Pallas kernels, shards(): pl.pallas_call(functools.partial(update_kernel, step=step, first=step ==...  6.22 us
    ppermute x6, waiting for transfers between devices, exchange(): return (lax.ppermute(x, 'rows', within), lax.ppermute(x, 'rows', across))  3.7 us
    unnamed x10, local copies, waits for them, and re-layouts  3.37 us
  transfers between devices with their start and end apart: 6, of which 3 were waited for; matrix products, arithmetic and copies ran while one was open for 0% of the time, Pallas kernels for 0%

profile of v1, /device:TPU:0, one launch (start us, length us, event | category | flops | bytes accessed | tf_op | source)
XLA Modules:
  0.0 101.6 jit_solution(7384636155183265129)
XLA Ops:
  0.6 0.0 copy-start
  0.6 0.9 copy-done
  1.6 0.0 copy-start.1
  1.6 0.9 copy-done.1
  2.5 0.0 copy-start.2
  2.5 0.9 copy-done.2
  3.4 0.0 copy-start.4
  3.4 0.4 pack.1.mine_ref
  3.8 0.7 collective-permute-start.1
  4.5 4.4 %collective-permute-start = (f32[4,200,128]{2,1,0:T(8,128)S(1)}, f32[4,200,128]{2,1,0:T(8,128)S(1)}, u32[]{:S(2)}, u32[]{:S(2)}) collective-permute-start(f32[4,200,128]{2,1,0:T(8,128)S(1)} %pack.1.mine_ref), channel_id=1, source_target_pairs={{0,1},{1,0},{2,3},{3,2},{4,5},{5,4},{6,7},{7,6},{8,9},{9,8},{10,11... | collective-permute-start | bytes 1228808 | tf_op jit(solution)/shard_map/ppermute | solution.py:374
  8.9 0.0 collective-permute-done.1.odd_ref
  8.9 1.4 %collective-permute-done.even_ref = f32[4,200,128]{2,1,0:T(8,128)S(1)} collective-permute-done((f32[4,200,128]{2,1,0:T(8,128)S(1)}, f32[4,200,128]{2,1,0:T(8,128)S(1)}, u32[]{:S(2)}, u32[]{:S(2)}) %collective-permute-start) | collective-permute-done | bytes 409632 | tf_op jit(solution)/shard_map/ppermute | solution.py:374
  10.2 0.0 copy-start.3
  10.2 0.7 copy-done.3
  10.9 7.7 %krylov0.1 = (f32[2,9,4,16,128]{4,3,2,1,0:T(8,128)S(1)}, f32[4,4,192,128]{3,2,1,0:T(8,128)S(1)}, f32[32,4,128]{2,1,0:T(4,128)S(1)}) custom-call(s32[1]{0:T(128)} %bitcast.parity_ref, f32[3]{0:T(128)S(1)} %copy-done.3, f32[4,200,128]{2,1,0:T(8,128)S(1)} %pack.1.mine_ref, f32[4,200,128]{2,1,0:T(8,128)S(1)} %collective-permute-done.even_ref, ...), custom_call_target="tpu_custom_call" | custom-call | tf_op jit(solution)/shard_map/krylov0/pallas_call | solution.py:397
  18.6 21.7 %all_to_all.15.gram_ref = f32[32,4,128]{2,1,0:T(4,128)S(1)} all-to-all(f32[32,4,128]{2,1,0:T(4,128)S(1)} %get-tuple-element.13), channel_id=1, replica_groups=mesh['rows'=32] {'rows'}, dimensions={0} | all-to-all | bytes 131072 | tf_op jit(solution)/shard_map/all_to_all | solution.py:417
  40.4 0.0 copy-done.4
  40.4 2.1 %update0.1 = (f32[3,4,32,512]{3,2,1,0:T(8,128)}, f32[4,128,128]{2,1,0:T(8,128)S(1)}) custom-call(f32[3]{0:T(128)S(1)} %copy-done.4, f32[32,4,128]{2,1,0:T(4,128)S(1)} %all_to_all.15.gram_ref, f32[4,4,192,128]{3,2,1,0:T(8,128)S(1)} %get-tuple-element.14.z_ref, f32[4,200,128]{2,1,0:T(8,128)S(1)} %pack.1.mine_ref, ...), custom_call_target="tpu_custom_call" | custom-call | tf_op jit(solution)/shard_map/update0/pallas_call | solution.py:420
  42.4 0.7 collective-permute-start.3
  43.1 1.8 %collective-permute-start.2 = (f32[4,128,128]{2,1,0:T(8,128)S(1)}, f32[4,128,128]{2,1,0:T(8,128)S(1)}, u32[]{:S(2)}, u32[]{:S(2)}) collective-permute-start(f32[4,128,128]{2,1,0:T(8,128)S(1)} %get-tuple-element.16.mine_ref), channel_id=1, source_target_pairs={{0,1},{1,0},{2,3},{3,2},{4,5},{5,4},{6,7},{7,6},{8,9},{9,8},{10,11... | collective-permute-start | bytes 786440 | tf_op jit(solution)/shard_map/ppermute | solution.py:374
  44.9 0.0 collective-permute-done.3.odd_ref
  45.0 1.2 %collective-permute-done.2.even_ref = f32[4,128,128]{2,1,0:T(8,128)S(1)} collective-permute-done((f32[4,128,128]{2,1,0:T(8,128)S(1)}, f32[4,128,128]{2,1,0:T(8,128)S(1)}, u32[]{:S(2)}, u32[]{:S(2)}) %collective-permute-start.2) | collective-permute-done | bytes 262176 | tf_op jit(solution)/shard_map/ppermute | solution.py:374
  46.1 7.6 %krylov1.1 = (f32[4,4,192,128]{3,2,1,0:T(8,128)S(1)}, f32[32,4,128]{2,1,0:T(4,128)S(1)}) custom-call(s32[1]{0:T(128)} %bitcast.parity_ref, f32[3]{0:T(128)S(1)} %copy-done.4, f32[4,128,128]{2,1,0:T(8,128)S(1)} %get-tuple-element.16.mine_ref, f32[4,128,128]{2,1,0:T(8,128)S(1)} %collective-permute-done.2.even_ref, ...), custom_call_target="tpu_custom_call" | custom-call | tf_op jit(solution)/shard_map/krylov1/pallas_call | solution.py:397
  53.8 16.2 %all_to_all.16.gram_ref = f32[32,4,128]{2,1,0:T(4,128)S(1)} all-to-all(f32[32,4,128]{2,1,0:T(4,128)S(1)} %get-tuple-element.17), channel_id=1, replica_groups=mesh['rows'=32] {'rows'}, dimensions={0} | all-to-all | bytes 131072 | tf_op jit(solution)/shard_map/all_to_all | solution.py:417
  69.9 2.1 %update1.1 = (f32[3,4,32,512]{3,2,1,0:T(8,128)}, f32[4,128,128]{2,1,0:T(8,128)S(1)}) custom-call(f32[3]{0:T(128)S(1)} %copy-done.4, f32[32,4,128]{2,1,0:T(4,128)S(1)} %all_to_all.16.gram_ref, f32[4,4,192,128]{3,2,1,0:T(8,128)S(1)} %get-tuple-element.18.z_ref, f32[4,128,128]{2,1,0:T(8,128)S(1)} %get-tuple-element.16.mine_ref, ...), custom_call_target="tpu_custom_call", output_to_operand_aliasing={{0}: (5, {})} | custom-call | tf_op jit(solution)/shard_map/update1/pallas_call | solution.py:420
  72.0 0.8 collective-permute-start.5
  72.9 1.8 %collective-permute-start.4 = (f32[4,128,128]{2,1,0:T(8,128)S(1)}, f32[4,128,128]{2,1,0:T(8,128)S(1)}, u32[]{:S(2)}, u32[]{:S(2)}) collective-permute-start(f32[4,128,128]{2,1,0:T(8,128)S(1)} %get-tuple-element.20.mine_ref), channel_id=1, source_target_pairs={{0,1},{1,0},{2,3},{3,2},{4,5},{5,4},{6,7},{7,6},{8,9},{9,8},{10,11... | collective-permute-start | bytes 786440 | tf_op jit(solution)/shard_map/ppermute | solution.py:374
  74.7 0.0 collective-permute-done.5.odd_ref
  74.7 1.2 %collective-permute-done.4.even_ref = f32[4,128,128]{2,1,0:T(8,128)S(1)} collective-permute-done((f32[4,128,128]{2,1,0:T(8,128)S(1)}, f32[4,128,128]{2,1,0:T(8,128)S(1)}, u32[]{:S(2)}, u32[]{:S(2)}) %collective-permute-start.4) | collective-permute-done | bytes 262176 | tf_op jit(solution)/shard_map/ppermute | solution.py:374
  75.9 7.6 %krylov2.1 = (f32[4,4,192,128]{3,2,1,0:T(8,128)S(1)}, f32[32,4,128]{2,1,0:T(4,128)S(1)}) custom-call(s32[1]{0:T(128)} %bitcast.parity_ref, f32[3]{0:T(128)S(1)} %copy-done.4, f32[4,128,128]{2,1,0:T(8,128)S(1)} %get-tuple-element.20.mine_ref, f32[4,128,128]{2,1,0:T(8,128)S(1)} %collective-permute-done.4.even_ref, ...), custom_call_target="tpu_custom_call" | custom-call | tf_op jit(solution)/shard_map/krylov2/pallas_call | solution.py:397
  83.5 16.0 %all_to_all.17.gram_ref = f32[32,4,128]{2,1,0:T(4,128)S(1)} all-to-all(f32[32,4,128]{2,1,0:T(4,128)S(1)} %get-tuple-element.21), channel_id=1, replica_groups=mesh['rows'=32] {'rows'}, dimensions={0} | all-to-all | bytes 131072 | tf_op jit(solution)/shard_map/all_to_all | solution.py:417
  99.5 2.1 %update2.1 = (f32[3,4,32,512]{3,2,1,0:T(8,128)}, f32[4,32,512]{2,1,0:T(8,128)}) custom-call(f32[3]{0:T(128)S(1)} %copy-done.4, f32[32,4,128]{2,1,0:T(4,128)S(1)} %all_to_all.17.gram_ref, f32[4,4,192,128]{3,2,1,0:T(8,128)S(1)} %get-tuple-element.22.z_ref, f32[4,128,128]{2,1,0:T(8,128)S(1)} %get-tuple-element.20.mine_ref, ...), custom_call_target="tpu_custom_call", output_to_operand_aliasing={{0}: (5, {})} | custom-call | tf_op jit(solution)/shard_map/update2/pallas_call | solution.py:420
Async XLA Ops:
  0.6 1.0 copy-start
  1.6 0.9 copy-start.1
  2.5 0.9 copy-start.2
  3.4 37.0 %copy-start.4 = (f32[3]{0:T(128)S(1)}, f32[3]{0:T(128)}, u32[]{:S(2)}) copy-start(f32[3]{0:T(128)} %shift_ref.11) | copy-start | bytes 40
  3.8 5.1 %collective-permute-start.1 = (f32[4,200,128]{2,1,0:T(8,128)S(1)}, f32[4,200,128]{2,1,0:T(8,128)S(1)}, u32[]{:S(2)}, u32[]{:S(2)}) collective-permute-start(f32[4,200,128]{2,1,0:T(8,128)S(1)} %pack.1.mine_ref), channel_id=1, source_target_pairs={{1,2},{3,4},{5,6},{7,8},{9,10},{11,12},{13,14},{15,16},{17,18},{19... | collective-permute-start | bytes 1228808 | tf_op jit(solution)/shard_map/ppermute | solution.py:374
  4.5 5.7 %collective-permute-start = (f32[4,200,128]{2,1,0:T(8,128)S(1)}, f32[4,200,128]{2,1,0:T(8,128)S(1)}, u32[]{:S(2)}, u32[]{:S(2)}) collective-permute-start(f32[4,200,128]{2,1,0:T(8,128)S(1)} %pack.1.mine_ref), channel_id=1, source_target_pairs={{0,1},{1,0},{2,3},{3,2},{4,5},{5,4},{6,7},{7,6},{8,9},{9,8},{10,11... | collective-permute-start | bytes 1228808 | tf_op jit(solution)/shard_map/ppermute | solution.py:374
  10.2 0.7 copy-start.3
  42.4 2.5 %collective-permute-start.3 = (f32[4,128,128]{2,1,0:T(8,128)S(1)}, f32[4,128,128]{2,1,0:T(8,128)S(1)}, u32[]{:S(2)}, u32[]{:S(2)}) collective-permute-start(f32[4,128,128]{2,1,0:T(8,128)S(1)} %get-tuple-element.16.mine_ref), channel_id=1, source_target_pairs={{1,2},{3,4},{5,6},{7,8},{9,10},{11,12},{13,14},{15,16},{17,18},{19... | collective-permute-start | bytes 786440 | tf_op jit(solution)/shard_map/ppermute | solution.py:374
  43.1 3.0 %collective-permute-start.2 = (f32[4,128,128]{2,1,0:T(8,128)S(1)}, f32[4,128,128]{2,1,0:T(8,128)S(1)}, u32[]{:S(2)}, u32[]{:S(2)}) collective-permute-start(f32[4,128,128]{2,1,0:T(8,128)S(1)} %get-tuple-element.16.mine_ref), channel_id=1, source_target_pairs={{0,1},{1,0},{2,3},{3,2},{4,5},{5,4},{6,7},{7,6},{8,9},{9,8},{10,11... | collective-permute-start | bytes 786440 | tf_op jit(solution)/shard_map/ppermute | solution.py:374
  72.0 2.7 %collective-permute-start.5 = (f32[4,128,128]{2,1,0:T(8,128)S(1)}, f32[4,128,128]{2,1,0:T(8,128)S(1)}, u32[]{:S(2)}, u32[]{:S(2)}) collective-permute-start(f32[4,128,128]{2,1,0:T(8,128)S(1)} %get-tuple-element.20.mine_ref), channel_id=1, source_target_pairs={{1,2},{3,4},{5,6},{7,8},{9,10},{11,12},{13,14},{15,16},{17,18},{19... | collective-permute-start | bytes 786440 | tf_op jit(solution)/shard_map/ppermute | solution.py:374
  72.9 3.0 %collective-permute-start.4 = (f32[4,128,128]{2,1,0:T(8,128)S(1)}, f32[4,128,128]{2,1,0:T(8,128)S(1)}, u32[]{:S(2)}, u32[]{:S(2)}) collective-permute-start(f32[4,128,128]{2,1,0:T(8,128)S(1)} %get-tuple-element.20.mine_ref), channel_id=1, source_target_pairs={{0,1},{1,0},{2,3},{3,2},{4,5},{5,4},{6,7},{7,6},{8,9},{9,8},{10,11... | collective-permute-start | bytes 786440 | tf_op jit(solution)/shard_map/ppermute | solution.py:374

commit v2 on v1

v2 whole, which is shorter than its diff:
```python
import functools

import jax
import jax.numpy as jnp
from jax import lax
from jax.experimental import pallas as pl
from jax.experimental.pallas import tpu as pltpu
from jax.sharding import PartitionSpec as P

ITERS = 4
CELLS = 4
LANES = 128
PIVOT_TOL = 3e-7
OFFSETS = ((-1, -1), (-1, 0), (-1, 1), (0, -1), (0, 0), (0, 1), (1, -1), (1, 0), (1, 1))
OFF_ROW = (0, 1, 2, 6, 7, 8)
PAIRS = [(i, j) for i in range(ITERS + 1) for j in range(i, ITERS + 1)]

SUB = 8
DEPTH = LANES // SUB

E1, E2, G0, G1, G2, C0, C1, A3, L0, L1, L2, R0, R1, R2 = range(14)
PLANES = 14
TE, TINV, TH, TL, TR, TC3, TL0N, TR0N = range(8)
SINGLE = 8 * DEPTH
SA, SC, SB1, SF1, SB2, SF2, S4, SINV = range(8)
CHUNK_PLANES = SINGLE + 8


def roll(x, shift, axis=0):
    return pltpu.roll(x, shift % x.shape[axis], axis)


def params():
    return pltpu.CompilerParams(vmem_limit_bytes=40 * 1024 * 1024)


def to_chunks(natural, stage):
    for tile in range(CELLS):
        stage[tile * LANES : (tile + 1) * LANES, :] = natural[:, tile * LANES : (tile + 1) * LANES].T
    return [
        jnp.concatenate(
            [stage[pl.ds(depth * CELLS + cell, SUB, stride=CELLS * DEPTH), :] for depth in range(DEPTH)], axis=0
        ).T
        for cell in range(CELLS)
    ]


def from_chunks(planes, stage):
    for cell in range(CELLS):
        turned = planes[cell].T
        for depth in range(DEPTH):
            stage[pl.ds(depth * CELLS + cell, SUB, stride=CELLS * DEPTH), :] = turned[
                depth * SUB : (depth + 1) * SUB, :
            ]
    return [stage[tile * LANES : (tile + 1) * LANES, :].T for tile in range(CELLS)]


def split(matrix):
    return [matrix[depth * SUB : (depth + 1) * SUB, :] for depth in range(DEPTH)]


def next_chunk(registers):
    return registers[1:] + [roll(registers[0], -1)]


def previous_chunk(registers):
    return [roll(registers[-1], 1)] + registers[:-1]


def pack_kernel(shift_ref, stiff_ref, mass_ref, factor_ref, out_ref, shifts_out, stage, gather):
    rows, cols, width = factor_ref.shape
    for step in range(shifts_out.shape[0]):
        shifts_out[step] = jnp.full(shifts_out.shape[1:], shift_ref[step], jnp.float32)
    planes = to_chunks(factor_ref[...].reshape(rows * cols, width), stage)
    for cell in range(CELLS):
        out_ref[cell, 0 : rows * cols, :] = planes[cell]
    entries = len(OFFSETS)
    gather[...] = jnp.zeros(gather.shape, jnp.float32)
    for which, ref in enumerate((stiff_ref, mass_ref)):
        for entry in range(entries):
            at = (which * entries + entry) * rows
            gather[at : at + rows, :] = ref[entry]
    planes = to_chunks(gather[...], stage)
    count = 2 * entries * rows
    lane = lax.broadcasted_iota(jnp.int32, (count, LANES), 1)
    line = lax.broadcasted_iota(jnp.int32, (count, LANES), 0)
    column = (line // rows) % 3
    for cell in range(CELLS):
        plane = planes[cell][0:count, :]
        if cell == 0:
            plane = jnp.where((lane == 0) & (column == 0), 0.0, plane)
        if cell == CELLS - 1:
            plane = jnp.where((lane == LANES - 1) & (column == 2), 0.0, plane)
        out_ref[cell, rows * cols : rows * cols + count, :] = plane


def factor_chunks(group, below, center, above, c3, l0, r0, chunk):
    l0n, r0n = next_chunk(l0), next_chunk(r0)
    center = [center[v] + c3[v] * l0n[v] for v in range(DEPTH)]
    above = [c3[v] * r0n[v] for v in range(DEPTH)]

    def put(index, value):
        chunk[group, index] = value

    for v in range(DEPTH):
        put(TC3 * DEPTH + v, c3[v])
        put(TL0N * DEPTH + v, l0n[v])
        put(TR0N * DEPTH + v, r0n[v])
    last = DEPTH - 1
    inv, hi, left = [], [], []
    for v in range(last):
        if v == 0:
            inv.append(1.0 / center[0])
            left.append(-below[0])
        else:
            e = below[v] * inv[v - 1]
            put(TE * DEPTH + v, e)
            inv.append(1.0 / (center[v] - e * above[v - 1]))
            left.append(-e * left[v - 1])
        hi.append(above[v] * inv[v])
        put(TINV * DEPTH + v, inv[v])
        put(TH * DEPTH + v, hi[v])
    l = [None] * last
    r = [None] * last
    for v in reversed(range(last)):
        l[v] = left[v] * inv[v]
        if v == last - 1:
            r[v] = -hi[v]
        else:
            l[v] = l[v] - hi[v] * l[v + 1]
            r[v] = -hi[v] * r[v + 1]
        put(TL * DEPTH + v, l[v])
        put(TR * DEPTH + v, r[v])
    put(SINGLE + SA, below[last])
    put(SINGLE + SC, above[last])
    b = below[last] * l[last - 1]
    d = center[last] + below[last] * r[last - 1] + above[last] * roll(l[0], -1)
    f = above[last] * roll(r[0], -1)
    slot = SB1
    stride = 1
    while stride < SUB:
        inverse = 1.0 / d
        from_below = -b * roll(inverse, stride)
        from_above = -f * roll(inverse, -stride)
        d = d + from_below * roll(f, stride) + from_above * roll(b, -stride)
        b, f = from_below * roll(b, stride), from_above * roll(f, -stride)
        if 2 * stride == SUB:
            put(SINGLE + S4, from_below + from_above)
        else:
            put(SINGLE + slot, from_below)
            put(SINGLE + slot + 1, from_above)
            slot += 2
        stride *= 2
    put(SINGLE + SINV, 1.0 / d)


def solve_chunks(group, q, p0, chunk):
    def get(index):
        return chunk[group, index]

    p0n = next_chunk(p0)
    q = [q[v] - get(TC3 * DEPTH + v) * p0n[v] for v in range(DEPTH)]
    last = DEPTH - 1
    f = [q[0]]
    for v in range(1, last):
        f.append(q[v] - get(TE * DEPTH + v) * f[v - 1])
    p = [None] * last
    for v in reversed(range(last)):
        p[v] = f[v] * get(TINV * DEPTH + v)
        if v < last - 1:
            p[v] = p[v] - get(TH * DEPTH + v) * p[v + 1]
    s = q[last] - get(SINGLE + SA) * p[last - 1] - get(SINGLE + SC) * roll(p[0], -1)
    s = s + get(SINGLE + SB1) * roll(s, 1) + get(SINGLE + SF1) * roll(s, -1)
    s = s + get(SINGLE + SB2) * roll(s, 2) + get(SINGLE + SF2) * roll(s, -2)
    s = s + get(SINGLE + S4) * roll(s, 4)
    s = s * get(SINGLE + SINV)
    before = roll(s, 1)
    x = [p[v] + get(TL * DEPTH + v) * before + get(TR * DEPTH + v) * s for v in range(last)] + [s]
    xn = next_chunk(x)
    x0n = [p0n[v] + get(TL0N * DEPTH + v) * x[v] + get(TR0N * DEPTH + v) * xn[v] for v in range(DEPTH)]
    return x, previous_chunk(x), x0n


def build_factors(line, inner, chunk, rows, cols, ext):
    a = [line[3, cell, 0:ext, :] for cell in range(CELLS)]
    d = [line[4, cell, 0:ext, :] for cell in range(CELLS)]
    c = [line[5, cell, 0:ext, :] for cell in range(CELLS)]
    d = [jnp.where(x <= 0.0, 1.0, x) for x in d]
    g0 = 1.0 / d[0]
    e1 = a[1] * g0
    g1 = 1.0 / (d[1] - e1 * c[0])
    e2 = a[2] * g1
    g2 = 1.0 / (d[2] - e2 * c[1])
    f0 = -a[0]
    f1 = -e1 * f0
    f2 = -e2 * f1
    l2 = f2 * g2
    l1 = (f1 - c[1] * l2) * g1
    l0 = (f0 - c[0] * l1) * g0
    r2 = -c[2] * g2
    r1 = -c[1] * r2 * g1
    r0 = -c[0] * r1 * g0
    for index, value in (
        (E1, e1), (E2, e2), (G0, g0), (G1, g1), (G2, g2), (C0, c[0]), (C1, c[1]), (A3, a[3]),
        (L0, l0), (L1, l1), (L2, l2), (R0, r0), (R1, r1), (R2, r2),
    ):
        inner[index, 0:ext, :] = value
    planes = (a[3] * l2, d[3] + a[3] * r2, c[3], l0, r0)
    for group in range(ext // rows):
        turned = [
            split(
                jnp.concatenate(
                    [
                        jnp.broadcast_to(plane[row : row + 1, :], (cols, LANES))
                        for row in range(group * rows, (group + 1) * rows)
                    ],
                    axis=0,
                ).T
            )
            for plane in planes
        ]
        below, center, c3, l0t, r0t = turned
        factor_chunks(group, below, center, None, c3, l0t, r0t, chunk)


def stencil_rows(coef, entries, read, row):
    out = []
    for cell in range(CELLS):
        total = None
        for entry in entries:
            offset = OFFSETS[entry]
            term = coef(entry, cell) * read(1 + cell + offset[1], row + offset[0])
            total = term if total is None else total + term
        out.append(total)
    return out


def krylov_kernel(
    parity_ref, shift_ref, mine_ref, even_ref, odd_ref, *refs, step, first, rows, cols, peers
):
    if first:
        coefs_ref, z_out, gram_out, wx, zx, line, inner, chunk, px, qx, sums = refs
    else:
        coefs_ref, z_out, gram_out, wx, zx, line, inner, chunk, px, qx, sums = refs
    ext = 3 * rows
    entries = len(OFFSETS)
    block = rows * cols
    parity = parity_ref[0]
    at_even = jnp.where(parity == 0, 2 * rows, 0)
    at_odd = 2 * rows - at_even
    wx[0, :, pl.ds(rows * cols, block), :] = mine_ref[:, 0:block, :]
    wx[0, :, pl.ds(pl.multiple_of(at_even * cols, cols), block), :] = even_ref[:, 0:block, :]
    wx[0, :, pl.ds(pl.multiple_of(at_odd * cols, cols), block), :] = odd_ref[:, 0:block, :]
    if first:
        low_is_even = parity == 1
        for which in range(2):
            for entry in range(entries):
                at = block + (which * entries + entry) * rows
                for cell in range(CELLS):
                    even = even_ref[cell, at : at + rows, :]
                    odd = odd_ref[cell, at : at + rows, :]
                    coefs_ref[which, entry, cell, 0:rows, :] = jnp.where(low_is_even, even, odd)
                    coefs_ref[which, entry, cell, rows : 2 * rows, :] = mine_ref[cell, at : at + rows, :]
                    coefs_ref[which, entry, cell, 2 * rows : ext, :] = jnp.where(low_is_even, odd, even)
    shift = shift_ref[step, 0:1, :]
    for entry in range(entries):
        for cell in range(CELLS):
            line[entry, cell, 0:ext, :] = (
                coefs_ref[0, entry, cell, 0:ext, :] + shift * coefs_ref[1, entry, cell, 0:ext, :]
            )
    build_factors(line, inner, chunk, rows, cols, ext)

    def span(row, count=1):
        return slice(row * cols, (row + count) * cols)

    for k in range(ITERS):
        low, high = k, ext - k

        def coef(index, row):
            return inner[index, row : row + 1, :]

        for group in range(ext // rows):
            wanted = [row for row in range(group * rows, (group + 1) * rows) if low <= row < high]
            for row in wanted:
                v0, v1, v2, v3 = (wx[k, cell, span(row), :] for cell in range(CELLS))
                f1 = v1 - coef(E1, row) * v0
                f2 = v2 - coef(E2, row) * f1
                x2 = f2 * coef(G2, row)
                x1 = (f1 - coef(C1, row) * x2) * coef(G1, row)
                x0 = (v0 - coef(C0, row) * x1) * coef(G0, row)
                px[0, span(row), :] = x0
                px[1, span(row), :] = x1
                px[2, span(row), :] = x2
                qx[span(row), :] = v3 - coef(A3, row) * x2
            at = span(group * rows, rows)
            x, before, after = solve_chunks(group, split(qx[at, :].T), split(px[0, at, :].T), chunk)
            zx[CELLS, at, :] = jnp.concatenate(x, axis=0).T
            zx[0, at, :] = jnp.concatenate(before, axis=0).T
            zx[CELLS + 1, at, :] = jnp.concatenate(after, axis=0).T
            for row in wanted:
                x3 = zx[CELLS, span(row), :]
                x3b = zx[0, span(row), :]
                for cell in range(CELLS - 1):
                    zx[1 + cell, span(row), :] = (
                        px[cell, span(row), :] + coef(L0 + cell, row) * x3b + coef(R0 + cell, row) * x3
                    )
                if rows - 1 <= row <= 2 * rows:
                    for slot in range(CELLS + 2):
                        z_out[k, slot, span(row - rows + 1), :] = zx[slot, span(row), :]

        def read_z(slot, row):
            return zx[slot, span(row), :]

        for row in range(low + 1, high - 1):
            image = stencil_rows(lambda entry, cell: line[entry, cell, row : row + 1, :], OFF_ROW, read_z, row)
            for cell in range(CELLS):
                wx[k + 1, cell, span(row), :] = image[cell]

    for tile in range(cols // 8):
        total = [None] * len(PAIRS)
        for row in range(rows, 2 * rows):
            for cell in range(CELLS):
                at = row * cols + tile * 8
                w = [wx[k, cell, at : at + 8, :] for k in range(ITERS + 1)]
                for index, (i, j) in enumerate(PAIRS):
                    term = w[i] * w[j]
                    total[index] = term if total[index] is None else total[index] + term
        for index in range(len(PAIRS)):
            sums[index * cols + tile * 8 : index * cols + tile * 8 + 8, :] = total[index]
    sums[len(PAIRS) * cols :, :] = jnp.zeros((sums.shape[0] - len(PAIRS) * cols, LANES), jnp.float32)
    for part in range(sums.shape[0] // LANES):
        turned = sums[part * LANES : (part + 1) * LANES, :].T
        gram_out[:, part : part + 1, :] = jnp.broadcast_to(
            jnp.sum(turned, axis=0, keepdims=True)[None], (peers, 1, LANES)
        )


def weights_of(g):
    upper = [
        [(g[i, j] + g[i + 1, j + 1]) + (g[i, j + 1] + g[i + 1, j]) for j in range(ITERS)] for i in range(ITERS)
    ]
    diag = [upper[i][i] for i in range(ITERS)]
    right = [g[0, i] + g[0, i + 1] for i in range(ITERS)]
    inverse = [None] * ITERS
    for k in range(ITERS):
        good = upper[k][k] > PIVOT_TOL * diag[k]
        inverse[k] = jnp.where(good, 1.0 / jnp.where(good, upper[k][k], 1.0), 0.0)
        for i in range(k + 1, ITERS):
            scale = upper[k][i] * inverse[k]
            for j in range(i, ITERS):
                upper[i][j] = upper[i][j] - scale * upper[k][j]
            right[i] = right[i] - scale * right[k]
    y = [None] * ITERS
    for k in reversed(range(ITERS)):
        value = right[k]
        for j in range(k + 1, ITERS):
            value = value - upper[k][j] * y[j]
        y[k] = value * inverse[k]
    return y


def update_kernel(shift_ref, gram_ref, z_ref, mine_ref, coefs_ref, *refs, step, first, last, rows, cols):
    if not first:
        refs = refs[1:]
    low_out, next_out, ux, yx, own, stage = refs
    total = gram_ref[0]
    for peer in range(1, gram_ref.shape[0]):
        total = total + gram_ref[peer]
    g = {}
    per_part = LANES // cols
    for part in range(total.shape[0]):
        turned = jnp.broadcast_to(total[part : part + 1, :], (LANES, LANES)).T
        for index, (i, j) in enumerate(PAIRS[part * per_part : (part + 1) * per_part]):
            g[i, j] = g[j, i] = turned[index * cols : (index + 1) * cols, :]
    y = weights_of(g)
    for k in range(ITERS):
        yx[k] = y[k]

    def span(row, count=1):
        return slice(row * cols, (row + count) * cols)

    for row in range(rows + 2):
        for slot in range(CELLS + 2):
            value = yx[0] * z_ref[0, slot, span(row), :]
            for k in range(1, ITERS):
                value = value + yx[k] * z_ref[k, slot, span(row), :]
            ux[slot, span(row), :] = value

    def read_u(slot, row):
        return ux[slot, span(row), :]

    double = 2.0 * shift_ref[step, 0:1, :]
    for row in range(rows):
        image = stencil_rows(
            lambda entry, cell: coefs_ref[1, entry, cell, rows + row : rows + row + 1, :],
            range(len(OFFSETS)), read_u, row + 1,
        )
        for cell in range(CELLS):
            value = mine_ref[cell, span(row), :] - double * image[cell]
            if last:
                own[cell, span(row), :] = value
            else:
                next_out[cell, span(row), :] = value

    root = jnp.sqrt(double)
    tiles = from_chunks([root * ux[1 + cell, span(1, rows), :] for cell in range(CELLS)], stage)
    for tile in range(len(tiles)):
        low_out[0, :, :, tile * LANES : (tile + 1) * LANES] = tiles[tile].reshape(rows, cols, LANES)
    if last:
        tiles = from_chunks([own[cell] for cell in range(CELLS)], stage)
        for tile in range(len(tiles)):
            next_out[:, :, tile * LANES : (tile + 1) * LANES] = tiles[tile].reshape(rows, cols, LANES)


def vmem():
    return pl.BlockSpec(memory_space=pltpu.VMEM)


def smem():
    return pl.BlockSpec(memory_space=pltpu.SMEM)


def shards(stiffness, mass, shifts, factor):
    rows, cols, width = factor.shape
    steps = shifts.shape[0]
    entries = len(OFFSETS)
    peers = lax.axis_size("rows")
    parity = (lax.axis_index("rows") % 2).astype(jnp.int32).reshape(1)
    block = rows * cols
    ext = 3 * rows
    ext_pad = -(-ext // 8) * 8
    f32 = jnp.float32
    gram_rows = -(-len(PAIRS) * cols // LANES)
    assert block == LANES and width == CELLS * LANES

    within = [(i, i ^ 1) for i in range(peers) if i ^ 1 < peers]
    across = [(i, i + 1) for i in range(1, peers - 1, 2)]
    across = across + [(b, a) for a, b in across]

    def exchange(x):
        return lax.ppermute(x, "rows", within), lax.ppermute(x, "rows", across)

    whole = pl.BlockSpec
    mine, shift_rows = pl.pallas_call(
        pack_kernel,
        grid=(1,),
        in_specs=[
            smem(),
            whole(stiffness.shape, lambda i: (0, 0, 0)),
            whole(mass.shape, lambda i: (0, 0, 0)),
            whole(factor.shape, lambda i: (0, 0, 0)),
        ],
        out_specs=[vmem(), vmem()],
        out_shape=[
            jax.ShapeDtypeStruct((CELLS, block + 2 * entries * rows, LANES), f32),
            jax.ShapeDtypeStruct((steps, 8, LANES), f32),
        ],
        scratch_shapes=[pltpu.VMEM((width, LANES), f32), pltpu.VMEM((LANES, width), f32)],
        compiler_params=params(),
        name="pack",
    )(shifts, stiffness, mass, factor)

    coefs = None
    lowrank = None
    for step in range(steps):
        first = step == 0
        even, odd = exchange(mine)
        coef_shape = jax.ShapeDtypeStruct((2, entries, CELLS, ext_pad, LANES), f32)
        out_shape = [
            jax.ShapeDtypeStruct((ITERS, CELLS + 2, (rows + 2) * cols, LANES), f32),
            jax.ShapeDtypeStruct((peers, gram_rows, LANES), f32),
        ]
        if first:
            out_shape = [coef_shape] + out_shape
        outs = pl.pallas_call(
            functools.partial(krylov_kernel, step=step, first=first, rows=rows, cols=cols, peers=peers),
            in_specs=[smem()] + [vmem()] * (4 if first else 5),
            out_specs=[vmem() for shape in out_shape],
            out_shape=out_shape,
            scratch_shapes=[
                pltpu.VMEM((ITERS + 1, CELLS, ext * cols, LANES), f32),
                pltpu.VMEM((CELLS + 2, ext * cols, LANES), f32),
                pltpu.VMEM((entries, CELLS, ext_pad, LANES), f32),
                pltpu.VMEM((PLANES, ext_pad, LANES), f32),
                pltpu.VMEM((3, CHUNK_PLANES, SUB, LANES), f32),
                pltpu.VMEM((CELLS - 1, ext * cols, LANES), f32),
                pltpu.VMEM((ext * cols, LANES), f32),
                pltpu.VMEM((gram_rows * LANES, LANES), f32),
            ],
            compiler_params=params(),
            name=f"krylov{step}",
        )(*((parity, shift_rows, mine, even, odd) + (() if first else (coefs,))))
        if first:
            coefs = outs[0]
            outs = outs[1:]
        z, gram = outs
        gram = lax.all_to_all(gram, "rows", 0, 0)
        last = step + 1 == steps
        next_shape = (rows, cols, width) if last else (CELLS, block, LANES)
        lowrank, mine = pl.pallas_call(
            functools.partial(update_kernel, step=step, first=first, last=last, rows=rows, cols=cols),
            grid=(1,),
            in_specs=[vmem()] * 5 + ([] if first else [pl.BlockSpec(memory_space=pl.ANY)]),
            out_specs=[
                pl.BlockSpec((1, rows, cols, width), lambda i, step=step: (step, 0, 0, 0)),
                vmem(),
            ],
            out_shape=[
                jax.ShapeDtypeStruct((steps, rows, cols, width), f32),
                jax.ShapeDtypeStruct(next_shape, f32),
            ],
            scratch_shapes=[
                pltpu.VMEM((CELLS + 2, (rows + 2) * cols, LANES), f32),
                pltpu.VMEM((ITERS, cols, LANES), f32),
                pltpu.VMEM((CELLS, block, LANES), f32),
                pltpu.VMEM((width, LANES), f32),
            ],
            input_output_aliases={} if first else {5: 0},
            compiler_params=params(),
            name=f"update{step}",
        )(*((shift_rows, gram, z, mine, coefs) + (() if first else (lowrank,))))
    return lowrank, mine


def solution(mesh):
    in_specs = (P(None, "rows", None), P(None, "rows", None), P(), P("rows", None, None))
    out_specs = (P(None, "rows", None, None), P("rows", None, None))
    return jax.shard_map(shards, mesh=mesh, in_specs=in_specs, out_specs=out_specs, check_vma=False)
```

time: 102 us -> 88.3 us (0.87)
  Pallas kernels: 29.7 us -> 16 us
    pallas_call x7, Pallas kernels: 29.7 us -> 16 us  [the longest x3 10.2 us: shards(): pl.pallas_call(functools.partial(krylov_kernel, step=step, first=first, r...]
    unnamed x10 -> x8, local copies, waits for them, and re-layouts: 3.37 us -> 3.37 us
where the time goes in v2:
time: 88.3 us; the launch traced here: 87.9 us
  blocking collectives  53.9 us (61%)
  Pallas kernels  16 us (18%)
  starting transfers between devices  10.3 us (12%)
  waiting for transfers between devices  3.7 us (4%)
  local copies, waits for them, and re-layouts  3.37 us (4%)
    all_to_all x3, blocking collectives, shards(): gram = lax.all_to_all(gram, 'rows', 0, 0)  53.9 us
    ppermute x6, starting transfers between devices, exchange(): return (lax.ppermute(x, 'rows', within), lax.ppermute(x, 'rows', across))  10.3 us
    pallas_call x3, Pallas kernels, shards(): pl.pallas_call(functools.partial(krylov_kernel, step=step, first=first, r...  10.2 us
    pallas_call x3, Pallas kernels, shards(): pl.pallas_call(functools.partial(update_kernel, step=step, first=first, l...  4.68 us
    ppermute x6, waiting for transfers between devices, exchange(): return (lax.ppermute(x, 'rows', within), lax.ppermute(x, 'rows', across))  3.7 us
    unnamed x8, local copies, waits for them, and re-layouts  3.37 us
  transfers between devices with their start and end apart: 6, of which 3 were waited for; matrix products, arithmetic and copies ran while one was open for 0% of the time, Pallas kernels for 0%

profile of v2, /device:TPU:0, one launch (start us, length us, event | category | flops | bytes accessed | tf_op | source)
XLA Modules:
  0.0 87.9 jit_solution(3745170561722823024)
XLA Ops:
  0.6 0.0 copy-start
  0.6 0.9 %copy-done = f32[4,32,512]{2,1,0:T(8,128)S(1)} copy-done((f32[4,32,512]{2,1,0:T(8,128)S(1)}, f32[4,32,512]{2,1,0:T(8,128)}, u32[]{:S(2)}) %copy-start) | copy-done | bytes 262168
  1.6 0.0 copy-start.1
  1.6 0.9 %copy-done.1 = f32[9,4,512]{2,1,0:T(4,128)S(1)} copy-done((f32[9,4,512]{2,1,0:T(4,128)S(1)}, f32[9,4,512]{2,1,0:T(4,128)}, u32[]{:S(2)}) %copy-start.1) | copy-done | bytes 73752
  2.5 0.0 copy-start.2
  2.5 0.9 %copy-done.2 = f32[9,4,512]{2,1,0:T(4,128)S(1)} copy-done((f32[9,4,512]{2,1,0:T(4,128)S(1)}, f32[9,4,512]{2,1,0:T(4,128)}, u32[]{:S(2)}) %copy-start.2) | copy-done | bytes 73752
  3.4 0.0 copy-start.3
  3.4 0.7 copy-done.3
  4.0 1.1 %pack.1 = (f32[4,200,128]{2,1,0:T(8,128)S(1)}, f32[3,8,128]{2,1,0:T(8,128)S(1)}) custom-call(f32[3]{0:T(128)S(1)} %copy-done.3, f32[9,4,512]{2,1,0:T(4,128)S(1)} %copy-done.1, f32[9,4,512]{2,1,0:T(4,128)S(1)} %copy-done.2, f32[4,32,512]{2,1,0:T(8,128)S(1)} %copy-done), custom_call_target="tpu_custom_call" | custom-call | tf_op jit(solution)/shard_map/pack/pallas_call | solution.py:444
  5.1 0.7 collective-permute-start.1
  5.8 4.4 %collective-permute-start = (f32[4,200,128]{2,1,0:T(8,128)S(1)}, f32[4,200,128]{2,1,0:T(8,128)S(1)}, u32[]{:S(2)}, u32[]{:S(2)}) collective-permute-start(f32[4,200,128]{2,1,0:T(8,128)S(1)} %get-tuple-element.16.mine_ref), channel_id=1, source_target_pairs={{0,1},{1,0},{2,3},{3,2},{4,5},{5,4},{6,7},{7,6},{8,9},{9,8},{10,11... | collective-permute-start | bytes 1228808 | tf_op jit(solution)/shard_map/ppermute | solution.py:441
  10.2 0.0 collective-permute-done.1.odd_ref
  10.2 1.4 %collective-permute-done.even_ref = f32[4,200,128]{2,1,0:T(8,128)S(1)} collective-permute-done((f32[4,200,128]{2,1,0:T(8,128)S(1)}, f32[4,200,128]{2,1,0:T(8,128)S(1)}, u32[]{:S(2)}, u32[]{:S(2)}) %collective-permute-start) | collective-permute-done | bytes 409632 | tf_op jit(solution)/shard_map/ppermute | solution.py:441
  11.6 3.5 %krylov0.1 = (f32[2,9,4,16,128]{4,3,2,1,0:T(8,128)S(1)}, f32[4,6,192,128]{3,2,1,0:T(8,128)S(1)}, f32[32,4,128]{2,1,0:T(4,128)S(1)}) custom-call(s32[1]{0:T(128)} %bitcast.parity_ref, f32[3,8,128]{2,1,0:T(8,128)S(1)} %get-tuple-element.15.shift_ref, f32[4,200,128]{2,1,0:T(8,128)S(1)} %get-tuple-element.16.mine_ref, ...), custom_call_target="tpu_custom_call" | custom-call | tf_op jit(solution)/shard_map/krylov0/pallas_call | solution.py:475
  15.1 21.7 %all_to_all.15.gram_ref = f32[32,4,128]{2,1,0:T(4,128)S(1)} all-to-all(f32[32,4,128]{2,1,0:T(4,128)S(1)} %get-tuple-element.17), channel_id=1, replica_groups=mesh['rows'=32] {'rows'}, dimensions={0} | all-to-all | bytes 131072 | tf_op jit(solution)/shard_map/all_to_all | solution.py:497
  36.8 1.5 %update0.1 = (f32[3,4,32,512]{3,2,1,0:T(8,128)}, f32[4,128,128]{2,1,0:T(8,128)S(1)}) custom-call(f32[3,8,128]{2,1,0:T(8,128)S(1)} %get-tuple-element.15.shift_ref, f32[32,4,128]{2,1,0:T(4,128)S(1)} %all_to_all.15.gram_ref, f32[4,6,192,128]{3,2,1,0:T(8,128)S(1)} %get-tuple-element.18.z_ref, f32[4,200,128]{2,1,0:T(8,128)S(1)} %get-tuple-element.16.mine_ref, ...), custom_call_target="tpu_custom_call" | custom-call | tf_op jit(solution)/shard_map/update0/pallas_call | solution.py:500
  38.3 0.7 collective-permute-start.3
  39.0 1.8 %collective-permute-start.2 = (f32[4,128,128]{2,1,0:T(8,128)S(1)}, f32[4,128,128]{2,1,0:T(8,128)S(1)}, u32[]{:S(2)}, u32[]{:S(2)}) collective-permute-start(f32[4,128,128]{2,1,0:T(8,128)S(1)} %get-tuple-element.20.mine_ref), channel_id=1, source_target_pairs={{0,1},{1,0},{2,3},{3,2},{4,5},{5,4},{6,7},{7,6},{8,9},{9,8},{10,11... | collective-permute-start | bytes 786440 | tf_op jit(solution)/shard_map/ppermute | solution.py:441
  40.8 0.0 collective-permute-done.3.odd_ref
  40.8 1.2 %collective-permute-done.2.even_ref = f32[4,128,128]{2,1,0:T(8,128)S(1)} collective-permute-done((f32[4,128,128]{2,1,0:T(8,128)S(1)}, f32[4,128,128]{2,1,0:T(8,128)S(1)}, u32[]{:S(2)}, u32[]{:S(2)}) %collective-permute-start.2) | collective-permute-done | bytes 262176 | tf_op jit(solution)/shard_map/ppermute | solution.py:441
  42.0 3.4 %krylov1.1 = (f32[4,6,192,128]{3,2,1,0:T(8,128)S(1)}, f32[32,4,128]{2,1,0:T(4,128)S(1)}) custom-call(s32[1]{0:T(128)} %bitcast.parity_ref, f32[3,8,128]{2,1,0:T(8,128)S(1)} %get-tuple-element.15.shift_ref, f32[4,128,128]{2,1,0:T(8,128)S(1)} %get-tuple-element.20.mine_ref, f32[4,128,128]{2,1,0:T(8,128)S(1)} %collective-permute-done.2.even_ref, ...), custom_call_target="tpu_custom_call" | custom-call | tf_op jit(solution)/shard_map/krylov1/pallas_call | solution.py:475
  45.4 16.2 %all_to_all.16.gram_ref = f32[32,4,128]{2,1,0:T(4,128)S(1)} all-to-all(f32[32,4,128]{2,1,0:T(4,128)S(1)} %get-tuple-element.21), channel_id=1, replica_groups=mesh['rows'=32] {'rows'}, dimensions={0} | all-to-all | bytes 131072 | tf_op jit(solution)/shard_map/all_to_all | solution.py:497
  61.6 1.5 %update1.1 = (f32[3,4,32,512]{3,2,1,0:T(8,128)}, f32[4,128,128]{2,1,0:T(8,128)S(1)}) custom-call(f32[3,8,128]{2,1,0:T(8,128)S(1)} %get-tuple-element.15.shift_ref, f32[32,4,128]{2,1,0:T(4,128)S(1)} %all_to_all.16.gram_ref, f32[4,6,192,128]{3,2,1,0:T(8,128)S(1)} %get-tuple-element.22.z_ref, ...), custom_call_target="tpu_custom_call", output_to_operand_aliasing={{0}: (5, {})} | custom-call | tf_op jit(solution)/shard_map/update1/pallas_call | solution.py:500
  63.1 0.8 collective-permute-start.5
  63.9 1.8 %collective-permute-start.4 = (f32[4,128,128]{2,1,0:T(8,128)S(1)}, f32[4,128,128]{2,1,0:T(8,128)S(1)}, u32[]{:S(2)}, u32[]{:S(2)}) collective-permute-start(f32[4,128,128]{2,1,0:T(8,128)S(1)} %get-tuple-element.24.mine_ref), channel_id=1, source_target_pairs={{0,1},{1,0},{2,3},{3,2},{4,5},{5,4},{6,7},{7,6},{8,9},{9,8},{10,11... | collective-permute-start | bytes 786440 | tf_op jit(solution)/shard_map/ppermute | solution.py:441
  65.8 0.0 collective-permute-done.5.odd_ref
  65.8 1.2 %collective-permute-done.4.even_ref = f32[4,128,128]{2,1,0:T(8,128)S(1)} collective-permute-done((f32[4,128,128]{2,1,0:T(8,128)S(1)}, f32[4,128,128]{2,1,0:T(8,128)S(1)}, u32[]{:S(2)}, u32[]{:S(2)}) %collective-permute-start.4) | collective-permute-done | bytes 262176 | tf_op jit(solution)/shard_map/ppermute | solution.py:441
  66.9 3.4 %krylov2.1 = (f32[4,6,192,128]{3,2,1,0:T(8,128)S(1)}, f32[32,4,128]{2,1,0:T(4,128)S(1)}) custom-call(s32[1]{0:T(128)} %bitcast.parity_ref, f32[3,8,128]{2,1,0:T(8,128)S(1)} %get-tuple-element.15.shift_ref, f32[4,128,128]{2,1,0:T(8,128)S(1)} %get-tuple-element.24.mine_ref, f32[4,128,128]{2,1,0:T(8,128)S(1)} %collective-permute-done.4.even_ref, ...), custom_call_target="tpu_custom_call" | custom-call | tf_op jit(solution)/shard_map/krylov2/pallas_call | solution.py:475
  70.3 16.0 %all_to_all.17.gram_ref = f32[32,4,128]{2,1,0:T(4,128)S(1)} all-to-all(f32[32,4,128]{2,1,0:T(4,128)S(1)} %get-tuple-element.25), channel_id=1, replica_groups=mesh['rows'=32] {'rows'}, dimensions={0} | all-to-all | bytes 131072 | tf_op jit(solution)/shard_map/all_to_all | solution.py:497
  86.3 1.6 %update2.1 = (f32[3,4,32,512]{3,2,1,0:T(8,128)}, f32[4,32,512]{2,1,0:T(8,128)}) custom-call(f32[3,8,128]{2,1,0:T(8,128)S(1)} %get-tuple-element.15.shift_ref, f32[32,4,128]{2,1,0:T(4,128)S(1)} %all_to_all.17.gram_ref, f32[4,6,192,128]{3,2,1,0:T(8,128)S(1)} %get-tuple-element.26.z_ref, ...), custom_call_target="tpu_custom_call", output_to_operand_aliasing={{0}: (5, {})} | custom-call | tf_op jit(solution)/shard_map/update2/pallas_call | solution.py:500
Async XLA Ops:
  0.6 1.0 %copy-start = (f32[4,32,512]{2,1,0:T(8,128)S(1)}, f32[4,32,512]{2,1,0:T(8,128)}, u32[]{:S(2)}) copy-start(f32[4,32,512]{2,1,0:T(8,128)} %factor_ref.1) | copy-start | bytes 786436
  1.6 0.9 %copy-start.1 = (f32[9,4,512]{2,1,0:T(4,128)S(1)}, f32[9,4,512]{2,1,0:T(4,128)}, u32[]{:S(2)}) copy-start(f32[9,4,512]{2,1,0:T(4,128)} %stiff_ref.1) | copy-start | bytes 221188
  2.5 0.9 %copy-start.2 = (f32[9,4,512]{2,1,0:T(4,128)S(1)}, f32[9,4,512]{2,1,0:T(4,128)}, u32[]{:S(2)}) copy-start(f32[9,4,512]{2,1,0:T(4,128)} %mass_ref.1) | copy-start | bytes 221188
  3.4 0.7 copy-start.3
  5.1 5.1 %collective-permute-start.1 = (f32[4,200,128]{2,1,0:T(8,128)S(1)}, f32[4,200,128]{2,1,0:T(8,128)S(1)}, u32[]{:S(2)}, u32[]{:S(2)}) collective-permute-start(f32[4,200,128]{2,1,0:T(8,128)S(1)} %get-tuple-element.16.mine_ref), channel_id=1, source_target_pairs={{1,2},{3,4},{5,6},{7,8},{9,10},{11,12},{13,14},{15,16},{17,18},{19... | collective-permute-start | bytes 1228808 | tf_op jit(solution)/shard_map/ppermute | solution.py:441
  5.8 5.7 %collective-permute-start = (f32[4,200,128]{2,1,0:T(8,128)S(1)}, f32[4,200,128]{2,1,0:T(8,128)S(1)}, u32[]{:S(2)}, u32[]{:S(2)}) collective-permute-start(f32[4,200,128]{2,1,0:T(8,128)S(1)} %get-tuple-element.16.mine_ref), channel_id=1, source_target_pairs={{0,1},{1,0},{2,3},{3,2},{4,5},{5,4},{6,7},{7,6},{8,9},{9,8},{10,11... | collective-permute-start | bytes 1228808 | tf_op jit(solution)/shard_map/ppermute | solution.py:441
  38.3 2.5 %collective-permute-start.3 = (f32[4,128,128]{2,1,0:T(8,128)S(1)}, f32[4,128,128]{2,1,0:T(8,128)S(1)}, u32[]{:S(2)}, u32[]{:S(2)}) collective-permute-start(f32[4,128,128]{2,1,0:T(8,128)S(1)} %get-tuple-element.20.mine_ref), channel_id=1, source_target_pairs={{1,2},{3,4},{5,6},{7,8},{9,10},{11,12},{13,14},{15,16},{17,18},{19... | collective-permute-start | bytes 786440 | tf_op jit(solution)/shard_map/ppermute | solution.py:441
  39.0 3.0 %collective-permute-start.2 = (f32[4,128,128]{2,1,0:T(8,128)S(1)}, f32[4,128,128]{2,1,0:T(8,128)S(1)}, u32[]{:S(2)}, u32[]{:S(2)}) collective-permute-start(f32[4,128,128]{2,1,0:T(8,128)S(1)} %get-tuple-element.20.mine_ref), channel_id=1, source_target_pairs={{0,1},{1,0},{2,3},{3,2},{4,5},{5,4},{6,7},{7,6},{8,9},{9,8},{10,11... | collective-permute-start | bytes 786440 | tf_op jit(solution)/shard_map/ppermute | solution.py:441
  63.1 2.7 %collective-permute-start.5 = (f32[4,128,128]{2,1,0:T(8,128)S(1)}, f32[4,128,128]{2,1,0:T(8,128)S(1)}, u32[]{:S(2)}, u32[]{:S(2)}) collective-permute-start(f32[4,128,128]{2,1,0:T(8,128)S(1)} %get-tuple-element.24.mine_ref), channel_id=1, source_target_pairs={{1,2},{3,4},{5,6},{7,8},{9,10},{11,12},{13,14},{15,16},{17,18},{19... | collective-permute-start | bytes 786440 | tf_op jit(solution)/shard_map/ppermute | solution.py:441
  63.9 3.0 %collective-permute-start.4 = (f32[4,128,128]{2,1,0:T(8,128)S(1)}, f32[4,128,128]{2,1,0:T(8,128)S(1)}, u32[]{:S(2)}, u32[]{:S(2)}) collective-permute-start(f32[4,128,128]{2,1,0:T(8,128)S(1)} %get-tuple-element.24.mine_ref), channel_id=1, source_target_pairs={{0,1},{1,0},{2,3},{3,2},{4,5},{5,4},{6,7},{7,6},{8,9},{9,8},{10,11... | collective-permute-start | bytes 786440 | tf_op jit(solution)/shard_map/ppermute | solution.py:441

commit v3 on v2

--- a/solution.py
+++ b/solution.py
@@ -67,16 +67,30 @@
     return [roll(registers[-1], 1)] + registers[:-1]
 
 
-def pack_kernel(shift_ref, stiff_ref, mass_ref, factor_ref, out_ref, shifts_out, stage, gather):
+def pack_kernel(
+    shift_hbm, stiff_hbm, mass_hbm, factor_hbm, out_ref, shifts_out,
+    stage, gather, shift_ref, stiff_ref, mass_ref, factor_ref, shift_sem, stiff_sem, mass_sem, factor_sem,
+):
+    copies = [
+        pltpu.make_async_copy(*operands)
+        for operands in (
+            (factor_hbm, factor_ref, factor_sem),
+            (stiff_hbm, stiff_ref, stiff_sem),
+            (mass_hbm, mass_ref, mass_sem),
+            (shift_hbm, shift_ref, shift_sem),
+        )
+    ]
+    for copy in copies:
+        copy.start()
     rows, cols, width = factor_ref.shape
-    for step in range(shifts_out.shape[0]):
-        shifts_out[step] = jnp.full(shifts_out.shape[1:], shift_ref[step], jnp.float32)
+    entries = len(OFFSETS)
+    gather[...] = jnp.zeros(gather.shape, jnp.float32)
+    copies[0].wait()
     planes = to_chunks(factor_ref[...].reshape(rows * cols, width), stage)
     for cell in range(CELLS):
         out_ref[cell, 0 : rows * cols, :] = planes[cell]
-    entries = len(OFFSETS)
-    gather[...] = jnp.zeros(gather.shape, jnp.float32)
     for which, ref in enumerate((stiff_ref, mass_ref)):
+        copies[1 + which].wait()
         for entry in range(entries):
             at = (which * entries + entry) * rows
             gather[at : at + rows, :] = ref[entry]
@@ -92,6 +106,9 @@
         if cell == CELLS - 1:
             plane = jnp.where((lane == LANES - 1) & (column == 2), 0.0, plane)
         out_ref[cell, rows * cols : rows * cols + count, :] = plane
+    copies[3].wait()
+    for step in range(shifts_out.shape[0]):
+        shifts_out[step] = jnp.full(shifts_out.shape[1:], shift_ref[step], jnp.float32)
 
 
 def factor_chunks(group, below, center, above, c3, l0, r0, chunk):
@@ -181,6 +198,14 @@
     return x, previous_chunk(x), x0n
 
 
+def build_lines(coefs_ref, shift, line, ext):
+    for entry in range(len(OFFSETS)):
+        for cell in range(CELLS):
+            line[entry, cell, 0:ext, :] = (
+                coefs_ref[0, entry, cell, 0:ext, :] + shift * coefs_ref[1, entry, cell, 0:ext, :]
+            )
+
+
 def build_factors(line, inner, chunk, rows, cols, ext):
     a = [line[3, cell, 0:ext, :] for cell in range(CELLS)]
     d = [line[4, cell, 0:ext, :] for cell in range(CELLS)]
@@ -235,13 +260,69 @@
     return out
 
 
+def line_solve(group, wanted, read, inner, chunk, px, qx, zx, base, rows, cols):
+    def coef(index, row):
+        return inner[index, row : row + 1, :]
+
+    def span(row, count=1):
+        return slice((row - base) * cols, (row - base + count) * cols)
+
+    for row in wanted:
+        v0, v1, v2, v3 = (read(cell, row) for cell in range(CELLS))
+        f1 = v1 - coef(E1, row) * v0
+        f2 = v2 - coef(E2, row) * f1
+        x2 = f2 * coef(G2, row)
+        x1 = (f1 - coef(C1, row) * x2) * coef(G1, row)
+        x0 = (v0 - coef(C0, row) * x1) * coef(G0, row)
+        px[0, span(row), :] = x0
+        px[1, span(row), :] = x1
+        px[2, span(row), :] = x2
+        qx[span(row), :] = v3 - coef(A3, row) * x2
+    at = span(group * rows, rows)
+    x, before, after = solve_chunks(group, split(qx[at, :].T), split(px[0, at, :].T), chunk)
+    zx[CELLS, at, :] = jnp.concatenate(x, axis=0).T
+    zx[0, at, :] = jnp.concatenate(before, axis=0).T
+    zx[CELLS + 1, at, :] = jnp.concatenate(after, axis=0).T
+    for row in wanted:
+        x3 = zx[CELLS, span(row), :]
+        x3b = zx[0, span(row), :]
+        for cell in range(CELLS - 1):
+            zx[1 + cell, span(row), :] = (
+                px[cell, span(row), :] + coef(L0 + cell, row) * x3b + coef(R0 + cell, row) * x3
+            )
+
+
+def side_kernel(shift_ref, coefs_ref, mine_ref, u_ref, *refs, step, rows, cols):
+    low_out, line, inner, chunk, z_out, px, qx, stage = refs[-8:]
+    ext = 3 * rows
+    build_lines(coefs_ref, shift_ref[step + 1, 0:1, :], line, ext)
+    build_factors(line, inner, chunk, rows, cols, ext)
+
+    def read(cell, row):
+        return mine_ref[cell, (row - rows) * cols : (row - rows + 1) * cols, :]
+
+    line_solve(1, list(range(rows, 2 * rows)), read, inner, chunk, px, qx, z_out, rows, rows, cols)
+    root = jnp.sqrt(2.0 * shift_ref[step, 0:1, :])
+    write_natural(low_out, 0, [root * u_ref[cell] for cell in range(CELLS)], stage, rows, cols)
+
+
+def write_natural(out, lead, planes, stage, rows, cols):
+    tiles = from_chunks(planes, stage)
+    for tile in range(len(tiles)):
+        value = tiles[tile].reshape(rows, cols, LANES)
+        if lead is None:
+            out[:, :, tile * LANES : (tile + 1) * LANES] = value
+        else:
+            out[lead, :, :, tile * LANES : (tile + 1) * LANES] = value
+
+
 def krylov_kernel(
     parity_ref, shift_ref, mine_ref, even_ref, odd_ref, *refs, step, first, rows, cols, peers
 ):
     if first:
-        coefs_ref, z_out, gram_out, wx, zx, line, inner, chunk, px, qx, sums = refs
+        coefs_ref, z_out, gram_out, wx, zx, px, qx, sums, line, inner, chunk = refs
     else:
-        coefs_ref, z_out, gram_out, wx, zx, line, inner, chunk, px, qx, sums = refs
+        line, inner, chunk, z_mine, z_out, gram_out, wx, zx, px, qx, sums = refs
     ext = 3 * rows
     entries = len(OFFSETS)
     block = rows * cols
@@ -262,13 +343,8 @@
                     coefs_ref[which, entry, cell, 0:rows, :] = jnp.where(low_is_even, even, odd)
                     coefs_ref[which, entry, cell, rows : 2 * rows, :] = mine_ref[cell, at : at + rows, :]
                     coefs_ref[which, entry, cell, 2 * rows : ext, :] = jnp.where(low_is_even, odd, even)
-    shift = shift_ref[step, 0:1, :]
-    for entry in range(entries):
-        for cell in range(CELLS):
-            line[entry, cell, 0:ext, :] = (
-                coefs_ref[0, entry, cell, 0:ext, :] + shift * coefs_ref[1, entry, cell, 0:ext, :]
-            )
-    build_factors(line, inner, chunk, rows, cols, ext)
+        build_lines(coefs_ref, shift_ref[step, 0:1, :], line, ext)
+        build_factors(line, inner, chunk, rows, cols, ext)
 
     def span(row, count=1):
         return slice(row * cols, (row + count) * cols)
@@ -276,37 +352,17 @@
     for k in range(ITERS):
         low, high = k, ext - k
 
-        def coef(index, row):
-            return inner[index, row : row + 1, :]
+        def read_w(cell, row):
+            return wx[k, cell, span(row), :]
 
         for group in range(ext // rows):
+            if k == 0 and group == 1 and not first:
+                zx[:, span(rows, rows), :] = z_mine[...]
+                continue
             wanted = [row for row in range(group * rows, (group + 1) * rows) if low <= row < high]
-            for row in wanted:
-                v0, v1, v2, v3 = (wx[k, cell, span(row), :] for cell in range(CELLS))
-                f1 = v1 - coef(E1, row) * v0
-                f2 = v2 - coef(E2, row) * f1
-                x2 = f2 * coef(G2, row)
-                x1 = (f1 - coef(C1, row) * x2) * coef(G1, row)
-                x0 = (v0 - coef(C0, row) * x1) * coef(G0, row)
-                px[0, span(row), :] = x0
-                px[1, span(row), :] = x1
-                px[2, span(row), :] = x2
-                qx[span(row), :] = v3 - coef(A3, row) * x2
-            at = span(group * rows, rows)
-            x, before, after = solve_chunks(group, split(qx[at, :].T), split(px[0, at, :].T), chunk)
-            zx[CELLS, at, :] = jnp.concatenate(x, axis=0).T
-            zx[0, at, :] = jnp.concatenate(before, axis=0).T
-            zx[CELLS + 1, at, :] = jnp.concatenate(after, axis=0).T
-            for row in wanted:
-                x3 = zx[CELLS, span(row), :]
-                x3b = zx[0, span(row), :]
-                for cell in range(CELLS - 1):
-                    zx[1 + cell, span(row), :] = (
-                        px[cell, span(row), :] + coef(L0 + cell, row) * x3b + coef(R0 + cell, row) * x3
-                    )
-                if rows - 1 <= row <= 2 * rows:
-                    for slot in range(CELLS + 2):
-                        z_out[k, slot, span(row - rows + 1), :] = zx[slot, span(row), :]
+            line_solve(group, wanted, read_w, inner, chunk, px, qx, zx, 0, rows, cols)
+        for row in range(rows - 1, 2 * rows + 1):
+            z_out[k, :, span(row - rows + 1), :] = zx[:, span(row), :]
 
         def read_z(slot, row):
             return zx[slot, span(row), :]
@@ -359,13 +415,12 @@
     return y
 
 
-def update_kernel(shift_ref, gram_ref, z_ref, mine_ref, coefs_ref, *refs, step, first, last, rows, cols):
-    if not first:
-        refs = refs[1:]
-    low_out, next_out, ux, yx, own, stage = refs
-    total = gram_ref[0]
-    for peer in range(1, gram_ref.shape[0]):
-        total = total + gram_ref[peer]
+def update_kernel(shift_ref, gram_ref, z_ref, mine_ref, coefs_ref, *refs, step, last, rows, cols):
+    low_out, next_out, ux, yx, own, stage = refs[-6:]
+    parts = [gram_ref[peer] for peer in range(gram_ref.shape[0])]
+    while len(parts) > 1:
+        parts = [a + b for a, b in zip(parts[0::2], parts[1::2])] + parts[len(parts) // 2 * 2 :]
+    total = parts[0]
     g = {}
     per_part = LANES // cols
     for part in range(total.shape[0]):
@@ -385,6 +440,8 @@
             for k in range(1, ITERS):
                 value = value + yx[k] * z_ref[k, slot, span(row), :]
             ux[slot, span(row), :] = value
+            if not last and 0 < row <= rows and 0 < slot <= CELLS:
+                low_out[slot - 1, span(row - 1), :] = value
 
     def read_u(slot, row):
         return ux[slot, span(row), :]
@@ -401,19 +458,19 @@
                 own[cell, span(row), :] = value
             else:
                 next_out[cell, span(row), :] = value
-
-    root = jnp.sqrt(double)
-    tiles = from_chunks([root * ux[1 + cell, span(1, rows), :] for cell in range(CELLS)], stage)
-    for tile in range(len(tiles)):
-        low_out[0, :, :, tile * LANES : (tile + 1) * LANES] = tiles[tile].reshape(rows, cols, LANES)
     if last:
-        tiles = from_chunks([own[cell] for cell in range(CELLS)], stage)
-        for tile in range(len(tiles)):
-            next_out[:, :, tile * LANES : (tile + 1) * LANES] = tiles[tile].reshape(rows, cols, LANES)
+        root = jnp.sqrt(double)
+        planes = [root * ux[1 + cell, span(1, rows), :] for cell in range(CELLS)]
+        write_natural(low_out, 0, planes, stage, rows, cols)
+        write_natural(next_out, None, [own[cell] for cell in range(CELLS)], stage, rows, cols)
 
 
 def vmem():
     return pl.BlockSpec(memory_space=pltpu.VMEM)
+
+
+def low_block(steps, rows, cols, width, step):
+    return pl.BlockSpec((1, rows, cols, width), lambda i: (step, 0, 0, 0))
 
 
 def smem():
@@ -440,86 +497,99 @@
     def exchange(x):
         return lax.ppermute(x, "rows", within), lax.ppermute(x, "rows", across)
 
-    whole = pl.BlockSpec
+    arrays = (shifts, stiffness, mass, factor)
     mine, shift_rows = pl.pallas_call(
         pack_kernel,
-        grid=(1,),
-        in_specs=[
-            smem(),
-            whole(stiffness.shape, lambda i: (0, 0, 0)),
-            whole(mass.shape, lambda i: (0, 0, 0)),
-            whole(factor.shape, lambda i: (0, 0, 0)),
-        ],
+        in_specs=[pl.BlockSpec(memory_space=pltpu.HBM)] * 4,
         out_specs=[vmem(), vmem()],
         out_shape=[
             jax.ShapeDtypeStruct((CELLS, block + 2 * entries * rows, LANES), f32),
             jax.ShapeDtypeStruct((steps, 8, LANES), f32),
         ],
-        scratch_shapes=[pltpu.VMEM((width, LANES), f32), pltpu.VMEM((LANES, width), f32)],
+        scratch_shapes=[pltpu.VMEM((width, LANES), f32), pltpu.VMEM((LANES, width), f32)]
+        + [pltpu.SMEM(shifts.shape, f32)]
+        + [pltpu.VMEM(array.shape, f32) for array in arrays[1:]]
+        + [pltpu.SemaphoreType.DMA] * 4,
         compiler_params=params(),
         name="pack",
-    )(shifts, stiffness, mass, factor)
-
+    )(*arrays)
+
+    z_shape = (ITERS, CELLS + 2, (rows + 2) * cols, LANES)
+    coef_shape = (2, entries, CELLS, ext_pad, LANES)
+    factor_shapes = (
+        (entries, CELLS, ext_pad, LANES),
+        (PLANES, ext_pad, LANES),
+        (3, CHUNK_PLANES, SUB, LANES),
+    )
+    work = [(CELLS - 1, ext * cols, LANES), (ext * cols, LANES)]
+    low_spec = pl.BlockSpec(memory_space=pl.ANY)
     coefs = None
     lowrank = None
+    factors = ()
     for step in range(steps):
         first = step == 0
+        last = step + 1 == steps
         even, odd = exchange(mine)
-        coef_shape = jax.ShapeDtypeStruct((2, entries, CELLS, ext_pad, LANES), f32)
-        out_shape = [
-            jax.ShapeDtypeStruct((ITERS, CELLS + 2, (rows + 2) * cols, LANES), f32),
-            jax.ShapeDtypeStruct((peers, gram_rows, LANES), f32),
-        ]
+        if not first:
+            outs = pl.pallas_call(
+                functools.partial(side_kernel, step=step - 1, rows=rows, cols=cols),
+                grid=(1,),
+                in_specs=[vmem()] * 4 + ([] if lowrank is None else [low_spec]),
+                out_specs=[low_block(steps, rows, cols, width, step - 1)] + [vmem()] * 4,
+                out_shape=[
+                    jax.ShapeDtypeStruct(shape, f32)
+                    for shape in ((steps, rows, cols, width),) + factor_shapes + ((CELLS + 2, block, LANES),)
+                ],
+                scratch_shapes=[
+                    pltpu.VMEM((CELLS - 1, block, LANES), f32),
+                    pltpu.VMEM((block, LANES), f32),
+                    pltpu.VMEM((width, LANES), f32),
+                ],
+                input_output_aliases={} if lowrank is None else {4: 0},
+                compiler_params=params(),
+                name=f"side{step}",
+            )(*((shift_rows, coefs, mine, u_mine) + (() if lowrank is None else (lowrank,))))
+            lowrank = outs[0]
+            factors = tuple(outs[1:])
+        shapes = [z_shape, (peers, gram_rows, LANES)]
         if first:
-            out_shape = [coef_shape] + out_shape
+            shapes = [coef_shape] + shapes
+        scratch = [(ITERS + 1, CELLS, ext * cols, LANES), (CELLS + 2, ext * cols, LANES)] + work
+        scratch = scratch + [(gram_rows * LANES, LANES)] + (list(factor_shapes) if first else [])
         outs = pl.pallas_call(
             functools.partial(krylov_kernel, step=step, first=first, rows=rows, cols=cols, peers=peers),
-            in_specs=[smem()] + [vmem()] * (4 if first else 5),
-            out_specs=[vmem() for shape in out_shape],
-            out_shape=out_shape,
-            scratch_shapes=[
-                pltpu.VMEM((ITERS + 1, CELLS, ext * cols, LANES), f32),
-                pltpu.VMEM((CELLS + 2, ext * cols, LANES), f32),
-                pltpu.VMEM((entries, CELLS, ext_pad, LANES), f32),
-                pltpu.VMEM((PLANES, ext_pad, LANES), f32),
-                pltpu.VMEM((3, CHUNK_PLANES, SUB, LANES), f32),
-                pltpu.VMEM((CELLS - 1, ext * cols, LANES), f32),
-                pltpu.VMEM((ext * cols, LANES), f32),
-                pltpu.VMEM((gram_rows * LANES, LANES), f32),
-            ],
+            in_specs=[smem()] + [vmem()] * (4 + len(factors)),
+            out_specs=[vmem() for shape in shapes],
+            out_shape=[jax.ShapeDtypeStruct(shape, f32) for shape in shapes],
+            scratch_shapes=[pltpu.VMEM(shape, f32) for shape in scratch],
             compiler_params=params(),
             name=f"krylov{step}",
-        )(*((parity, shift_rows, mine, even, odd) + (() if first else (coefs,))))
+        )(parity, shift_rows, mine, even, odd, *factors)
         if first:
             coefs = outs[0]
             outs = outs[1:]
         z, gram = outs
         gram = lax.all_to_all(gram, "rows", 0, 0)
-        last = step + 1 == steps
-        next_shape = (rows, cols, width) if last else (CELLS, block, LANES)
-        lowrank, mine = pl.pallas_call(
-            functools.partial(update_kernel, step=step, first=first, last=last, rows=rows, cols=cols),
+        chunked = (CELLS, block, LANES)
+        shapes = [(steps, rows, cols, width), (rows, cols, width)] if last else [chunked, chunked]
+        alias = last and lowrank is not None
+        u_mine, mine = pl.pallas_call(
+            functools.partial(update_kernel, step=step, last=last, rows=rows, cols=cols),
             grid=(1,),
-            in_specs=[vmem()] * 5 + ([] if first else [pl.BlockSpec(memory_space=pl.ANY)]),
-            out_specs=[
-                pl.BlockSpec((1, rows, cols, width), lambda i, step=step: (step, 0, 0, 0)),
-                vmem(),
-            ],
-            out_shape=[
-                jax.ShapeDtypeStruct((steps, rows, cols, width), f32),
-                jax.ShapeDtypeStruct(next_shape, f32),
-            ],
+            in_specs=[vmem()] * 5 + ([low_spec] if alias else []),
+            out_specs=[low_block(steps, rows, cols, width, step) if last else vmem(), vmem()],
+            out_shape=[jax.ShapeDtypeStruct(shape, f32) for shape in shapes],
             scratch_shapes=[
                 pltpu.VMEM((CELLS + 2, (rows + 2) * cols, LANES), f32),
                 pltpu.VMEM((ITERS, cols, LANES), f32),
-                pltpu.VMEM((CELLS, block, LANES), f32),
+                pltpu.VMEM(chunked, f32),
                 pltpu.VMEM((width, LANES), f32),
             ],
-            input_output_aliases={} if first else {5: 0},
+            input_output_aliases={5: 0} if alias else {},
             compiler_params=params(),
             name=f"update{step}",
-        )(*((shift_rows, gram, z, mine, coefs) + (() if first else (lowrank,))))
-    return lowrank, mine
+        )(*((shift_rows, gram, z, mine, coefs) + ((lowrank,) if alias else ())))
+    return u_mine, mine
 
 
 def solution(mesh):

time: 88.3 us -> 84.4 us (0.956)
  waiting for transfers between devices: 3.7 us -> 1.38 us
    ppermute x6, waiting for transfers between devices: 3.7 us -> 1.38 us  [exchange(): return (lax.ppermute(x, 'rows', within), lax.ppermute(x, 'rows', across))]
    pallas_call x3, Pallas kernels: 10.2 us -> 8.29 us  [shards(): pl.pallas_call(functools.partial(krylov_kernel, step=step, first=first, r...]
    pallas_call x4 -> x6, Pallas kernels: 5.81 us -> 6.93 us  [the longest x2 3.12 us: shards(): pl.pallas_call(functools.partial(side_kernel, step=step - 1, rows=rows, c...]
  transfers between devices with their start and end apart: 6 -> 6, of which waited for: 3 -> 1; matrix products, arithmetic and copies ran while one was open for 0% -> 0% of each run, Pallas kernels for 0% -> 4%
where the time goes in v3:
time: 84.4 us; the launch traced here: 84.1 us
  blocking collectives  53.1 us (63%)
  Pallas kernels  15.2 us (18%)
  starting transfers between devices  10.3 us (12%)
  local copies, waits for them, and re-layouts  3.37 us (4%)
  waiting for transfers between devices  1.38 us (2%)
    all_to_all x3, blocking collectives, shards(): gram = lax.all_to_all(gram, 'rows', 0, 0)  53.1 us
    ppermute x6, starting transfers between devices, exchange(): return (lax.ppermute(x, 'rows', within), lax.ppermute(x, 'rows', across))  10.3 us
    pallas_call x3, Pallas kernels, shards(): pl.pallas_call(functools.partial(krylov_kernel, step=step, first=first, r...  8.29 us
    unnamed x8, local copies, waits for them, and re-layouts  3.37 us
    pallas_call x2, Pallas kernels, shards(): pl.pallas_call(functools.partial(side_kernel, step=step - 1, rows=rows, c...  3.12 us
    pallas_call x3, Pallas kernels, shards(): pl.pallas_call(functools.partial(update_kernel, step=step, last=last, row...  2.89 us
  transfers between devices with their start and end apart: 6, of which 1 were waited for; matrix products, arithmetic and copies ran while one was open for 0% of the time, Pallas kernels for 4%

profile of v3, /device:TPU:0, one launch (start us, length us, event | category | flops | bytes accessed | tf_op | source)
XLA Modules:
  0.0 84.1 jit_solution(5074024051315112840)
XLA Ops:
  0.6 0.0 copy-start
  0.6 0.9 %copy-done = f32[4,32,512]{2,1,0:T(8,128)S(1)} copy-done((f32[4,32,512]{2,1,0:T(8,128)S(1)}, f32[4,32,512]{2,1,0:T(8,128)}, u32[]{:S(2)}) %copy-start) | copy-done | bytes 262168
  1.6 0.0 copy-start.1
  1.6 0.9 %copy-done.1 = f32[9,4,512]{2,1,0:T(4,128)S(1)} copy-done((f32[9,4,512]{2,1,0:T(4,128)S(1)}, f32[9,4,512]{2,1,0:T(4,128)}, u32[]{:S(2)}) %copy-start.1) | copy-done | bytes 73752
  2.5 0.0 copy-start.2
  2.5 0.9 %copy-done.2 = f32[9,4,512]{2,1,0:T(4,128)S(1)} copy-done((f32[9,4,512]{2,1,0:T(4,128)S(1)}, f32[9,4,512]{2,1,0:T(4,128)}, u32[]{:S(2)}) %copy-start.2) | copy-done | bytes 73752
  3.4 0.0 copy-start.3
  3.4 0.7 copy-done.3
  4.0 0.9 %pack.1 = (f32[4,200,128]{2,1,0:T(8,128)S(1)}, f32[3,8,128]{2,1,0:T(8,128)S(1)}) custom-call(f32[3]{0:T(128)S(1)} %copy-done.3, f32[9,4,512]{2,1,0:T(4,128)S(1)} %copy-done.1, f32[9,4,512]{2,1,0:T(4,128)S(1)} %copy-done.2, f32[4,32,512]{2,1,0:T(8,128)S(1)} %copy-done), custom_call_target="tpu_custom_call" | custom-call | tf_op jit(solution)/shard_map/pack/pallas_call | solution.py:501
  4.9 0.7 collective-permute-start.1
  5.6 4.4 %collective-permute-start = (f32[4,200,128]{2,1,0:T(8,128)S(1)}, f32[4,200,128]{2,1,0:T(8,128)S(1)}, u32[]{:S(2)}, u32[]{:S(2)}) collective-permute-start(f32[4,200,128]{2,1,0:T(8,128)S(1)} %get-tuple-element.26.mine_ref), channel_id=1, source_target_pairs={{0,1},{1,0},{2,3},{3,2},{4,5},{5,4},{6,7},{7,6},{8,9},{9,8},{10,11... | collective-permute-start | bytes 1228808 | tf_op jit(solution)/shard_map/ppermute | solution.py:498
  10.0 0.0 collective-permute-done.1.odd_ref
  10.0 1.4 %collective-permute-done.even_ref = f32[4,200,128]{2,1,0:T(8,128)S(1)} collective-permute-done((f32[4,200,128]{2,1,0:T(8,128)S(1)}, f32[4,200,128]{2,1,0:T(8,128)S(1)}, u32[]{:S(2)}, u32[]{:S(2)}) %collective-permute-start) | collective-permute-done | bytes 409632 | tf_op jit(solution)/shard_map/ppermute | solution.py:498
  11.4 3.5 %krylov0.1 = (f32[2,9,4,16,128]{4,3,2,1,0:T(8,128)S(1)}, f32[4,6,192,128]{3,2,1,0:T(8,128)S(1)}, f32[32,4,128]{2,1,0:T(4,128)S(1)}) custom-call(s32[1]{0:T(128)} %bitcast.parity_ref, f32[3,8,128]{2,1,0:T(8,128)S(1)} %get-tuple-element.25.shift_ref, f32[4,200,128]{2,1,0:T(8,128)S(1)} %get-tuple-element.26.mine_ref, ...), custom_call_target="tpu_custom_call" | custom-call | tf_op jit(solution)/shard_map/krylov0/pallas_call | solution.py:559
  14.9 21.7 %all_to_all.15.gram_ref = f32[32,4,128]{2,1,0:T(4,128)S(1)} all-to-all(f32[32,4,128]{2,1,0:T(4,128)S(1)} %get-tuple-element.27), channel_id=1, replica_groups=mesh['rows'=32] {'rows'}, dimensions={0} | all-to-all | bytes 131072 | tf_op jit(solution)/shard_map/all_to_all | solution.py:572
  36.6 0.6 update0.1
  37.2 0.7 collective-permute-start.3
  37.9 1.8 %collective-permute-start.2 = (f32[4,128,128]{2,1,0:T(8,128)S(1)}, f32[4,128,128]{2,1,0:T(8,128)S(1)}, u32[]{:S(2)}, u32[]{:S(2)}) collective-permute-start(f32[4,128,128]{2,1,0:T(8,128)S(1)} %get-tuple-element.30.mine_ref), channel_id=1, source_target_pairs={{0,1},{1,0},{2,3},{3,2},{4,5},{5,4},{6,7},{7,6},{8,9},{9,8},{10,11... | collective-permute-start | bytes 786440 | tf_op jit(solution)/shard_map/ppermute | solution.py:498
  39.8 1.6 %side1.1 = (f32[3,4,32,512]{3,2,1,0:T(8,128)}, f32[9,4,16,128]{3,2,1,0:T(8,128)S(1)}, f32[14,16,128]{2,1,0:T(8,128)S(1)}, f32[3,136,8,128]{3,2,1,0:T(8,128)S(1)}, f32[6,128,128]{2,1,0:T(8,128)S(1)}) custom-call(f32[3,8,128]{2,1,0:T(8,128)S(1)} %get-tuple-element.25.shift_ref, f32[2,9,4,16,128]{4,3,2,1,0:T(8,128)S(1)} %get-tuple-element.29.coefs_ref, ...), custom_call_target="tpu_custom_call" | custom-call | tf_op jit(solution)/shard_map/side1/pallas_call | solution.py:534
  41.3 0.0 collective-permute-done.3.odd_ref
  41.3 0.0 collective-permute-done.2.even_ref
  41.3 2.4 %krylov1.1 = (f32[4,6,192,128]{3,2,1,0:T(8,128)S(1)}, f32[32,4,128]{2,1,0:T(4,128)S(1)}) custom-call(s32[1]{0:T(128)} %bitcast.parity_ref, f32[3,8,128]{2,1,0:T(8,128)S(1)} %get-tuple-element.25.shift_ref, f32[4,128,128]{2,1,0:T(8,128)S(1)} %get-tuple-element.30.mine_ref, f32[4,128,128]{2,1,0:T(8,128)S(1)} %collective-permute-done.2.even_ref, ...), custom_call_target="tpu_custom_call" | custom-call | tf_op jit(solution)/shard_map/krylov1/pallas_call | solution.py:559
  43.7 15.8 %all_to_all.16.gram_ref = f32[32,4,128]{2,1,0:T(4,128)S(1)} all-to-all(f32[32,4,128]{2,1,0:T(4,128)S(1)} %get-tuple-element.36), channel_id=1, replica_groups=mesh['rows'=32] {'rows'}, dimensions={0} | all-to-all | bytes 131072 | tf_op jit(solution)/shard_map/all_to_all | solution.py:572
  59.5 0.6 update1.1
  60.1 0.9 %collective-permute-start.5 = (f32[4,128,128]{2,1,0:T(8,128)S(1)}, f32[4,128,128]{2,1,0:T(8,128)S(1)}, u32[]{:S(2)}, u32[]{:S(2)}) collective-permute-start(f32[4,128,128]{2,1,0:T(8,128)S(1)} %get-tuple-element.38.mine_ref), channel_id=1, source_target_pairs={{1,2},{3,4},{5,6},{7,8},{9,10},{11,12},{13,14},{15,16},{17,18},{19... | collective-permute-start | bytes 786440 | tf_op jit(solution)/shard_map/ppermute | solution.py:498
  61.0 1.8 %collective-permute-start.4 = (f32[4,128,128]{2,1,0:T(8,128)S(1)}, f32[4,128,128]{2,1,0:T(8,128)S(1)}, u32[]{:S(2)}, u32[]{:S(2)}) collective-permute-start(f32[4,128,128]{2,1,0:T(8,128)S(1)} %get-tuple-element.38.mine_ref), channel_id=1, source_target_pairs={{0,1},{1,0},{2,3},{3,2},{4,5},{5,4},{6,7},{7,6},{8,9},{9,8},{10,11... | collective-permute-start | bytes 786440 | tf_op jit(solution)/shard_map/ppermute | solution.py:498
  62.8 1.6 %side2.1 = (f32[3,4,32,512]{3,2,1,0:T(8,128)}, f32[9,4,16,128]{3,2,1,0:T(8,128)S(1)}, f32[14,16,128]{2,1,0:T(8,128)S(1)}, f32[3,136,8,128]{3,2,1,0:T(8,128)S(1)}, f32[6,128,128]{2,1,0:T(8,128)S(1)}) custom-call(f32[3,8,128]{2,1,0:T(8,128)S(1)} %get-tuple-element.25.shift_ref, ...), custom_call_target="tpu_custom_call", output_to_operand_aliasing={{0}: (4, {})} | custom-call | tf_op jit(solution)/shard_map/side2/pallas_call | solution.py:534
  64.4 0.0 collective-permute-done.5.odd_ref
  64.4 0.0 collective-permute-done.4.even_ref
  64.4 2.4 %krylov2.1 = (f32[4,6,192,128]{3,2,1,0:T(8,128)S(1)}, f32[32,4,128]{2,1,0:T(4,128)S(1)}) custom-call(s32[1]{0:T(128)} %bitcast.parity_ref, f32[3,8,128]{2,1,0:T(8,128)S(1)} %get-tuple-element.25.shift_ref, f32[4,128,128]{2,1,0:T(8,128)S(1)} %get-tuple-element.38.mine_ref, f32[4,128,128]{2,1,0:T(8,128)S(1)} %collective-permute-done.4.even_ref, ...), custom_call_target="tpu_custom_call" | custom-call | tf_op jit(solution)/shard_map/krylov2/pallas_call | solution.py:559
  66.8 15.6 %all_to_all.17.gram_ref = f32[32,4,128]{2,1,0:T(4,128)S(1)} all-to-all(f32[32,4,128]{2,1,0:T(4,128)S(1)} %get-tuple-element.45), channel_id=1, replica_groups=mesh['rows'=32] {'rows'}, dimensions={0} | all-to-all | bytes 131072 | tf_op jit(solution)/shard_map/all_to_all | solution.py:572
  82.4 1.6 %update2.1 = (f32[3,4,32,512]{3,2,1,0:T(8,128)}, f32[4,32,512]{2,1,0:T(8,128)}) custom-call(f32[3,8,128]{2,1,0:T(8,128)S(1)} %get-tuple-element.25.shift_ref, f32[32,4,128]{2,1,0:T(4,128)S(1)} %all_to_all.17.gram_ref, f32[4,6,192,128]{3,2,1,0:T(8,128)S(1)} %get-tuple-element.46.z_ref, ...), custom_call_target="tpu_custom_call", output_to_operand_aliasing={{0}: (5, {})} | custom-call | tf_op jit(solution)/shard_map/update2/pallas_call | solution.py:576
Async XLA Ops:
  0.6 1.0 %copy-start = (f32[4,32,512]{2,1,0:T(8,128)S(1)}, f32[4,32,512]{2,1,0:T(8,128)}, u32[]{:S(2)}) copy-start(f32[4,32,512]{2,1,0:T(8,128)} %factor_hbm.1) | copy-start | bytes 786436
  1.6 0.9 %copy-start.1 = (f32[9,4,512]{2,1,0:T(4,128)S(1)}, f32[9,4,512]{2,1,0:T(4,128)}, u32[]{:S(2)}) copy-start(f32[9,4,512]{2,1,0:T(4,128)} %stiff_hbm.1) | copy-start | bytes 221188
  2.5 0.9 %copy-start.2 = (f32[9,4,512]{2,1,0:T(4,128)S(1)}, f32[9,4,512]{2,1,0:T(4,128)}, u32[]{:S(2)}) copy-start(f32[9,4,512]{2,1,0:T(4,128)} %mass_hbm.1) | copy-start | bytes 221188
  3.4 0.7 copy-start.3
  4.9 5.1 %collective-permute-start.1 = (f32[4,200,128]{2,1,0:T(8,128)S(1)}, f32[4,200,128]{2,1,0:T(8,128)S(1)}, u32[]{:S(2)}, u32[]{:S(2)}) collective-permute-start(f32[4,200,128]{2,1,0:T(8,128)S(1)} %get-tuple-element.26.mine_ref), channel_id=1, source_target_pairs={{1,2},{3,4},{5,6},{7,8},{9,10},{11,12},{13,14},{15,16},{17,18},{19... | collective-permute-start | bytes 1228808 | tf_op jit(solution)/shard_map/ppermute | solution.py:498
  5.6 5.7 %collective-permute-start = (f32[4,200,128]{2,1,0:T(8,128)S(1)}, f32[4,200,128]{2,1,0:T(8,128)S(1)}, u32[]{:S(2)}, u32[]{:S(2)}) collective-permute-start(f32[4,200,128]{2,1,0:T(8,128)S(1)} %get-tuple-element.26.mine_ref), channel_id=1, source_target_pairs={{0,1},{1,0},{2,3},{3,2},{4,5},{5,4},{6,7},{7,6},{8,9},{9,8},{10,11... | collective-permute-start | bytes 1228808 | tf_op jit(solution)/shard_map/ppermute | solution.py:498
  37.2 4.1 %collective-permute-start.3 = (f32[4,128,128]{2,1,0:T(8,128)S(1)}, f32[4,128,128]{2,1,0:T(8,128)S(1)}, u32[]{:S(2)}, u32[]{:S(2)}) collective-permute-start(f32[4,128,128]{2,1,0:T(8,128)S(1)} %get-tuple-element.30.mine_ref), channel_id=1, source_target_pairs={{1,2},{3,4},{5,6},{7,8},{9,10},{11,12},{13,14},{15,16},{17,18},{19... | collective-permute-start | bytes 786440 | tf_op jit(solution)/shard_map/ppermute | solution.py:498
  37.9 3.4 %collective-permute-start.2 = (f32[4,128,128]{2,1,0:T(8,128)S(1)}, f32[4,128,128]{2,1,0:T(8,128)S(1)}, u32[]{:S(2)}, u32[]{:S(2)}) collective-permute-start(f32[4,128,128]{2,1,0:T(8,128)S(1)} %get-tuple-element.30.mine_ref), channel_id=1, source_target_pairs={{0,1},{1,0},{2,3},{3,2},{4,5},{5,4},{6,7},{7,6},{8,9},{9,8},{10,11... | collective-permute-start | bytes 786440 | tf_op jit(solution)/shard_map/ppermute | solution.py:498
  60.1 4.3 %collective-permute-start.5 = (f32[4,128,128]{2,1,0:T(8,128)S(1)}, f32[4,128,128]{2,1,0:T(8,128)S(1)}, u32[]{:S(2)}, u32[]{:S(2)}) collective-permute-start(f32[4,128,128]{2,1,0:T(8,128)S(1)} %get-tuple-element.38.mine_ref), channel_id=1, source_target_pairs={{1,2},{3,4},{5,6},{7,8},{9,10},{11,12},{13,14},{15,16},{17,18},{19... | collective-permute-start | bytes 786440 | tf_op jit(solution)/shard_map/ppermute | solution.py:498
  61.0 3.4 %collective-permute-start.4 = (f32[4,128,128]{2,1,0:T(8,128)S(1)}, f32[4,128,128]{2,1,0:T(8,128)S(1)}, u32[]{:S(2)}, u32[]{:S(2)}) collective-permute-start(f32[4,128,128]{2,1,0:T(8,128)S(1)} %get-tuple-element.38.mine_ref), channel_id=1, source_target_pairs={{0,1},{1,0},{2,3},{3,2},{4,5},{5,4},{6,7},{7,6},{8,9},{9,8},{10,11... | collective-permute-start | bytes 786440 | tf_op jit(solution)/shard_map/ppermute | solution.py:498

commit v4 on v3

--- a/solution.py
+++ b/solution.py
@@ -6,6 +6,7 @@
 from jax.experimental import pallas as pl
 from jax.experimental.pallas import tpu as pltpu
 from jax.sharding import PartitionSpec as P
+
 
 ITERS = 4
 CELLS = 4
@@ -68,7 +69,7 @@
 
 
 def pack_kernel(
-    shift_hbm, stiff_hbm, mass_hbm, factor_hbm, out_ref, shifts_out,
+    shift_hbm, stiff_hbm, mass_hbm, factor_hbm, coefs_out, field_out, shifts_out,
     stage, gather, shift_ref, stiff_ref, mass_ref, factor_ref, shift_sem, stiff_sem, mass_sem, factor_sem,
 ):
     copies = [
@@ -85,10 +86,6 @@
     rows, cols, width = factor_ref.shape
     entries = len(OFFSETS)
     gather[...] = jnp.zeros(gather.shape, jnp.float32)
-    copies[0].wait()
-    planes = to_chunks(factor_ref[...].reshape(rows * cols, width), stage)
-    for cell in range(CELLS):
-        out_ref[cell, 0 : rows * cols, :] = planes[cell]
     for which, ref in enumerate((stiff_ref, mass_ref)):
         copies[1 + which].wait()
         for entry in range(entries):
@@ -105,7 +102,11 @@
             plane = jnp.where((lane == 0) & (column == 0), 0.0, plane)
         if cell == CELLS - 1:
             plane = jnp.where((lane == LANES - 1) & (column == 2), 0.0, plane)
-        out_ref[cell, rows * cols : rows * cols + count, :] = plane
+        coefs_out[cell] = plane
+    copies[0].wait()
+    planes = to_chunks(factor_ref[...].reshape(rows * cols, width), stage)
+    for cell in range(CELLS):
+        field_out[cell] = planes[cell]
     copies[3].wait()
     for step in range(shifts_out.shape[0]):
         shifts_out[step] = jnp.full(shifts_out.shape[1:], shift_ref[step], jnp.float32)
@@ -292,18 +293,34 @@
             )
 
 
-def side_kernel(shift_ref, coefs_ref, mine_ref, u_ref, *refs, step, rows, cols):
-    low_out, line, inner, chunk, z_out, px, qx, stage = refs[-8:]
+def side_kernel(parity_ref, shift_ref, *refs, step, rows, cols):
     ext = 3 * rows
-    build_lines(coefs_ref, shift_ref[step + 1, 0:1, :], line, ext)
+    entries = len(OFFSETS)
+    if step == 0:
+        own_ref, even_ref, odd_ref, mine_ref, coefs_ref, line, inner, chunk, z_out, px, qx = refs
+        low_is_even = parity_ref[0] == 1
+        for which in range(2):
+            for entry in range(entries):
+                at = (which * entries + entry) * rows
+                for cell in range(CELLS):
+                    even = even_ref[cell, at : at + rows, :]
+                    odd = odd_ref[cell, at : at + rows, :]
+                    coefs_ref[which, entry, cell, 0:rows, :] = jnp.where(low_is_even, even, odd)
+                    coefs_ref[which, entry, cell, rows : 2 * rows, :] = own_ref[cell, at : at + rows, :]
+                    coefs_ref[which, entry, cell, 2 * rows : ext, :] = jnp.where(low_is_even, odd, even)
+    else:
+        coefs_ref, mine_ref, u_ref = refs[:3]
+        low_out, line, inner, chunk, z_out, px, qx, stage = refs[-8:]
+    build_lines(coefs_ref, shift_ref[step, 0:1, :], line, ext)
     build_factors(line, inner, chunk, rows, cols, ext)
 
     def read(cell, row):
         return mine_ref[cell, (row - rows) * cols : (row - rows + 1) * cols, :]
 
     line_solve(1, list(range(rows, 2 * rows)), read, inner, chunk, px, qx, z_out, rows, rows, cols)
-    root = jnp.sqrt(2.0 * shift_ref[step, 0:1, :])
-    write_natural(low_out, 0, [root * u_ref[cell] for cell in range(CELLS)], stage, rows, cols)
+    if step > 0:
+        root = jnp.sqrt(2.0 * shift_ref[step - 1, 0:1, :])
+        write_natural(low_out, 0, [root * u_ref[cell] for cell in range(CELLS)], stage, rows, cols)
 
 
 def write_natural(out, lead, planes, stage, rows, cols):
@@ -317,34 +334,17 @@
 
 
 def krylov_kernel(
-    parity_ref, shift_ref, mine_ref, even_ref, odd_ref, *refs, step, first, rows, cols, peers
+    parity_ref, mine_ref, even_ref, odd_ref, line, inner, chunk, z_mine,
+    z_out, gram_out, wx, zx, px, qx, sums, *, rows, cols, peers,
 ):
-    if first:
-        coefs_ref, z_out, gram_out, wx, zx, px, qx, sums, line, inner, chunk = refs
-    else:
-        line, inner, chunk, z_mine, z_out, gram_out, wx, zx, px, qx, sums = refs
     ext = 3 * rows
-    entries = len(OFFSETS)
     block = rows * cols
     parity = parity_ref[0]
     at_even = jnp.where(parity == 0, 2 * rows, 0)
     at_odd = 2 * rows - at_even
-    wx[0, :, pl.ds(rows * cols, block), :] = mine_ref[:, 0:block, :]
-    wx[0, :, pl.ds(pl.multiple_of(at_even * cols, cols), block), :] = even_ref[:, 0:block, :]
-    wx[0, :, pl.ds(pl.multiple_of(at_odd * cols, cols), block), :] = odd_ref[:, 0:block, :]
-    if first:
-        low_is_even = parity == 1
-        for which in range(2):
-            for entry in range(entries):
-                at = block + (which * entries + entry) * rows
-                for cell in range(CELLS):
-                    even = even_ref[cell, at : at + rows, :]
-                    odd = odd_ref[cell, at : at + rows, :]
-                    coefs_ref[which, entry, cell, 0:rows, :] = jnp.where(low_is_even, even, odd)
-                    coefs_ref[which, entry, cell, rows : 2 * rows, :] = mine_ref[cell, at : at + rows, :]
-                    coefs_ref[which, entry, cell, 2 * rows : ext, :] = jnp.where(low_is_even, odd, even)
-        build_lines(coefs_ref, shift_ref[step, 0:1, :], line, ext)
-        build_factors(line, inner, chunk, rows, cols, ext)
+    wx[0, :, pl.ds(rows * cols, block), :] = mine_ref[...]
+    wx[0, :, pl.ds(pl.multiple_of(at_even * cols, cols), block), :] = even_ref[...]
+    wx[0, :, pl.ds(pl.multiple_of(at_odd * cols, cols), block), :] = odd_ref[...]
 
     def span(row, count=1):
         return slice(row * cols, (row + count) * cols)
@@ -356,7 +356,7 @@
             return wx[k, cell, span(row), :]
 
         for group in range(ext // rows):
-            if k == 0 and group == 1 and not first:
+            if k == 0 and group == 1:
                 zx[:, span(rows, rows), :] = z_mine[...]
                 continue
             wanted = [row for row in range(group * rows, (group + 1) * rows) if low <= row < high]
@@ -469,7 +469,7 @@
     return pl.BlockSpec(memory_space=pltpu.VMEM)
 
 
-def low_block(steps, rows, cols, width, step):
+def low_block(rows, cols, width, step):
     return pl.BlockSpec((1, rows, cols, width), lambda i: (step, 0, 0, 0))
 
 
@@ -497,18 +497,21 @@
     def exchange(x):
         return lax.ppermute(x, "rows", within), lax.ppermute(x, "rows", across)
 
-    arrays = (shifts, stiffness, mass, factor)
-    mine, shift_rows = pl.pallas_call(
+    arrays = [
+        pltpu.with_memory_space_constraint(array, pltpu.HBM) for array in (shifts, stiffness, mass, factor)
+    ]
+    chunked = (CELLS, block, LANES)
+    stencils, mine, shift_rows = pl.pallas_call(
         pack_kernel,
         in_specs=[pl.BlockSpec(memory_space=pltpu.HBM)] * 4,
-        out_specs=[vmem(), vmem()],
+        out_specs=[vmem()] * 3,
         out_shape=[
-            jax.ShapeDtypeStruct((CELLS, block + 2 * entries * rows, LANES), f32),
-            jax.ShapeDtypeStruct((steps, 8, LANES), f32),
+            jax.ShapeDtypeStruct(shape, f32)
+            for shape in ((CELLS, 2 * entries * rows, LANES), chunked, (steps, 8, LANES))
         ],
         scratch_shapes=[pltpu.VMEM((width, LANES), f32), pltpu.VMEM((LANES, width), f32)]
         + [pltpu.SMEM(shifts.shape, f32)]
-        + [pltpu.VMEM(array.shape, f32) for array in arrays[1:]]
+        + [pltpu.VMEM(array.shape, f32) for array in (stiffness, mass, factor)]
         + [pltpu.SemaphoreType.DMA] * 4,
         compiler_params=params(),
         name="pack",
@@ -520,64 +523,63 @@
         (entries, CELLS, ext_pad, LANES),
         (PLANES, ext_pad, LANES),
         (3, CHUNK_PLANES, SUB, LANES),
+        (CELLS + 2, block, LANES),
     )
-    work = [(CELLS - 1, ext * cols, LANES), (ext * cols, LANES)]
+    low_shape = (steps, rows, cols, width)
     low_spec = pl.BlockSpec(memory_space=pl.ANY)
     coefs = None
     lowrank = None
-    factors = ()
     for step in range(steps):
         first = step == 0
         last = step + 1 == steps
+        if first:
+            beside = (stencils, *exchange(stencils), mine)
+            lead_shape, lead_spec = coef_shape, vmem()
+            scratch = []
+        else:
+            beside = (coefs, mine, u_mine) + (() if lowrank is None else (lowrank,))
+            lead_shape, lead_spec = low_shape, low_block(rows, cols, width, step - 1)
+            scratch = [pltpu.VMEM((width, LANES), f32)]
         even, odd = exchange(mine)
-        if not first:
-            outs = pl.pallas_call(
-                functools.partial(side_kernel, step=step - 1, rows=rows, cols=cols),
-                grid=(1,),
-                in_specs=[vmem()] * 4 + ([] if lowrank is None else [low_spec]),
-                out_specs=[low_block(steps, rows, cols, width, step - 1)] + [vmem()] * 4,
-                out_shape=[
-                    jax.ShapeDtypeStruct(shape, f32)
-                    for shape in ((steps, rows, cols, width),) + factor_shapes + ((CELLS + 2, block, LANES),)
-                ],
-                scratch_shapes=[
-                    pltpu.VMEM((CELLS - 1, block, LANES), f32),
-                    pltpu.VMEM((block, LANES), f32),
-                    pltpu.VMEM((width, LANES), f32),
-                ],
-                input_output_aliases={} if lowrank is None else {4: 0},
-                compiler_params=params(),
-                name=f"side{step}",
-            )(*((shift_rows, coefs, mine, u_mine) + (() if lowrank is None else (lowrank,))))
-            lowrank = outs[0]
-            factors = tuple(outs[1:])
+        lead, *factors = pl.pallas_call(
+            functools.partial(side_kernel, step=step, rows=rows, cols=cols),
+            grid=(1,),
+            in_specs=[smem()] + [vmem()] * (5 if first else 4) + [low_spec] * (len(beside) - (4 if first else 3)),
+            out_specs=[lead_spec] + [vmem()] * 4,
+            out_shape=[jax.ShapeDtypeStruct(shape, f32) for shape in (lead_shape,) + factor_shapes],
+            scratch_shapes=[pltpu.VMEM((CELLS - 1, block, LANES), f32), pltpu.VMEM((block, LANES), f32)] + scratch,
+            input_output_aliases={} if first or lowrank is None else {5: 0},
+            compiler_params=params(),
+        )(parity, shift_rows, *beside)
+        if first:
+            coefs = lead
+        else:
+            lowrank = lead
         shapes = [z_shape, (peers, gram_rows, LANES)]
-        if first:
-            shapes = [coef_shape] + shapes
-        scratch = [(ITERS + 1, CELLS, ext * cols, LANES), (CELLS + 2, ext * cols, LANES)] + work
-        scratch = scratch + [(gram_rows * LANES, LANES)] + (list(factor_shapes) if first else [])
-        outs = pl.pallas_call(
-            functools.partial(krylov_kernel, step=step, first=first, rows=rows, cols=cols, peers=peers),
-            in_specs=[smem()] + [vmem()] * (4 + len(factors)),
+        scratch = [
+            (ITERS + 1, CELLS, ext * cols, LANES),
+            (CELLS + 2, ext * cols, LANES),
+            (CELLS - 1, ext * cols, LANES),
+            (ext * cols, LANES),
+            (gram_rows * LANES, LANES),
+        ]
+        z, gram = pl.pallas_call(
+            functools.partial(krylov_kernel, rows=rows, cols=cols, peers=peers),
+            in_specs=[smem()] + [vmem()] * 7,
             out_specs=[vmem() for shape in shapes],
             out_shape=[jax.ShapeDtypeStruct(shape, f32) for shape in shapes],
             scratch_shapes=[pltpu.VMEM(shape, f32) for shape in scratch],
             compiler_params=params(),
-            name=f"krylov{step}",
-        )(parity, shift_rows, mine, even, odd, *factors)
-        if first:
-            coefs = outs[0]
-            outs = outs[1:]
-        z, gram = outs
+            name="krylov",
+        )(parity, mine, even, odd, *factors)
         gram = lax.all_to_all(gram, "rows", 0, 0)
-        chunked = (CELLS, block, LANES)
-        shapes = [(steps, rows, cols, width), (rows, cols, width)] if last else [chunked, chunked]
+        shapes = [low_shape, (rows, cols, width)] if last else [chunked, chunked]
         alias = last and lowrank is not None
         u_mine, mine = pl.pallas_call(
             functools.partial(update_kernel, step=step, last=last, rows=rows, cols=cols),
             grid=(1,),
             in_specs=[vmem()] * 5 + ([low_spec] if alias else []),
-            out_specs=[low_block(steps, rows, cols, width, step) if last else vmem(), vmem()],
+            out_specs=[low_block(rows, cols, width, step) if last else vmem(), vmem()],
             out_shape=[jax.ShapeDtypeStruct(shape, f32) for shape in shapes],
             scratch_shapes=[
                 pltpu.VMEM((CELLS + 2, (rows + 2) * cols, LANES), f32),
@@ -587,7 +589,6 @@
             ],
             input_output_aliases={5: 0} if alias else {},
             compiler_params=params(),
-            name=f"update{step}",
         )(*((shift_rows, gram, z, mine, coefs) + ((lowrank,) if alias else ())))
     return u_mine, mine
 

time: 84.4 us -> 81.7 us (0.968)
  starting transfers between devices: 10.3 us -> 13.8 us
  local copies, waits for them, and re-layouts: 3.37 us -> 0 us
  blocking collectives: 53.1 us -> 49.9 us
    ppermute x6 -> x8, starting transfers between devices: 10.3 us -> 13.8 us  [exchange(): return (lax.ppermute(x, 'rows', within), lax.ppermute(x, 'rows', across))]
    unnamed x8 -> x0, local copies, waits for them, and re-layouts: 3.37 us -> none
    all_to_all x3, blocking collectives: 53.1 us -> 49.9 us  [shards(): gram = lax.all_to_all(gram, 'rows', 0, 0)]
    pallas_call x5 -> x6, Pallas kernels: 11.4 us -> 11.3 us  [the longest x3 7.53 us: shards(): pl.pallas_call(functools.partial(krylov_kernel, rows=rows, cols=cols, pee...]
  transfers between devices with their start and end apart: 6 -> 8, of which waited for: 1 -> 1; matrix products, arithmetic and copies ran while one was open for 0% -> 0% of each run, Pallas kernels for 4% -> 5%
where the time goes in v4:
time: 81.7 us; the launch traced here: 81.4 us
  blocking collectives  49.9 us (61%)
  Pallas kernels  16 us (20%)
  starting transfers between devices  13.8 us (17%)
  waiting for transfers between devices  1.02 us (1%)
    all_to_all x3, blocking collectives, shards(): gram = lax.all_to_all(gram, 'rows', 0, 0)  49.9 us
    ppermute x8, starting transfers between devices, exchange(): return (lax.ppermute(x, 'rows', within), lax.ppermute(x, 'rows', across))  13.8 us
    pallas_call x3, Pallas kernels, shards(): pl.pallas_call(functools.partial(krylov_kernel, rows=rows, cols=cols, pee...  7.53 us
    pallas_call x3, Pallas kernels, shards(): pl.pallas_call(functools.partial(side_kernel, step=step, rows=rows, cols=...  3.77 us
    pallas_call x3, Pallas kernels, shards(): pl.pallas_call(functools.partial(update_kernel, step=step, last=last, row...  2.98 us
    pallas_call x1, Pallas kernels, shards(): pl.pallas_call(pack_kernel, in_specs=[pl.BlockSpec(memory_space=pltpu.HBM...  1.69 us
  transfers between devices with their start and end apart: 8, of which 1 were waited for; matrix products, arithmetic and copies ran while one was open for 0% of the time, Pallas kernels for 5%

profile of v4, /device:TPU:0, one launch (start us, length us, event | category | flops | bytes accessed | tf_op | source)
XLA Modules:
  0.0 81.4 jit_solution(1141026580435973257)
XLA Ops:
  0.6 1.7 %pack.1 = (f32[4,72,128]{2,1,0:T(8,128)S(1)}, f32[4,128,128]{2,1,0:T(8,128)S(1)}, f32[3,8,128]{2,1,0:T(8,128)S(1)}) custom-call(f32[3]{0:T(128)} %shift_hbm.1, f32[9,4,512]{2,1,0:T(4,128)} %stiff_hbm.1, f32[9,4,512]{2,1,0:T(4,128)} %mass_hbm.1, f32[4,32,512]{2,1,0:T(8,128)} %factor_hbm.1), custom_call_target="tpu_custom_call" | custom-call | tf_op jit(solution)/shard_map/pack/pallas_call | solution.py:504
  2.3 0.7 collective-permute-start.1
  3.0 4.4 %collective-permute-start = (f32[4,128,128]{2,1,0:T(8,128)S(1)}, f32[4,128,128]{2,1,0:T(8,128)S(1)}, u32[]{:S(2)}, u32[]{:S(2)}) collective-permute-start(f32[4,128,128]{2,1,0:T(8,128)S(1)} %get-tuple-element.31.refs_3_.mine_ref), channel_id=1, source_target_pairs={{0,1},{1,0},{2,3},{3,2},{4,5},{5,4},{6,7},{7,6},{8,9},{9,8},{10,11... | collective-permute-start | bytes 786440 | tf_op jit(solution)/shard_map/ppermute | solution.py:498
  7.4 0.7 collective-permute-start.3
  8.1 2.9 %collective-permute-start.2 = (f32[4,72,128]{2,1,0:T(8,128)S(1)}, f32[4,72,128]{2,1,0:T(8,128)S(1)}, u32[]{:S(2)}, u32[]{:S(2)}) collective-permute-start(f32[4,72,128]{2,1,0:T(8,128)S(1)} %get-tuple-element.32.refs_0_), channel_id=1, source_target_pairs={{0,1},{1,0},{2,3},{3,2},{4,5},{5,4},{6,7},{7,6},{8,9},{9,8},{10,11... | collective-permute-start | bytes 442376 | tf_op jit(solution)/shard_map/ppermute | solution.py:498
  11.0 0.0 collective-permute-done.3.refs_2_
  11.0 1.0 %collective-permute-done.2.refs_1_ = f32[4,72,128]{2,1,0:T(8,128)S(1)} collective-permute-done((f32[4,72,128]{2,1,0:T(8,128)S(1)}, f32[4,72,128]{2,1,0:T(8,128)S(1)}, u32[]{:S(2)}, u32[]{:S(2)}) %collective-permute-start.2) | collective-permute-done | bytes 147488 | tf_op jit(solution)/shard_map/ppermute | solution.py:498
  12.0 0.6 shard_map.59
  12.6 0.0 collective-permute-done.1.odd_ref
  12.6 0.0 collective-permute-done.even_ref
  12.6 2.5 %krylov.3 = (f32[4,6,192,128]{3,2,1,0:T(8,128)S(1)}, f32[32,4,128]{2,1,0:T(4,128)S(1)}) custom-call(s32[1]{0:T(128)} %bitcast.parity_ref, f32[4,128,128]{2,1,0:T(8,128)S(1)} %get-tuple-element.31.refs_3_.mine_ref, f32[4,128,128]{2,1,0:T(8,128)S(1)} %collective-permute-done.even_ref, f32[4,128,128]{2,1,0:T(8,128)S(1)} %collective-permute-done.1.odd_ref, ...), custom_call_target="tpu_custom_call" | custom-call | tf_op jit(solution)/shard_map/krylov/pallas_call | solution.py:566
  15.1 18.5 %all_to_all.15.gram_ref = f32[32,4,128]{2,1,0:T(4,128)S(1)} all-to-all(f32[32,4,128]{2,1,0:T(4,128)S(1)} %get-tuple-element.37), channel_id=1, replica_groups=mesh['rows'=32] {'rows'}, dimensions={0} | all-to-all | bytes 131072 | tf_op jit(solution)/shard_map/all_to_all | solution.py:575
  33.7 0.7 shard_map.60
  34.3 0.7 collective-permute-start.5
  35.0 1.8 %collective-permute-start.4 = (f32[4,128,128]{2,1,0:T(8,128)S(1)}, f32[4,128,128]{2,1,0:T(8,128)S(1)}, u32[]{:S(2)}, u32[]{:S(2)}) collective-permute-start(f32[4,128,128]{2,1,0:T(8,128)S(1)} %get-tuple-element.40.refs_1_.mine_ref), channel_id=1, source_target_pairs={{0,1},{1,0},{2,3},{3,2},{4,5},{5,4},{6,7},{7,6},{8,9},{9,8},{10,11... | collective-permute-start | bytes 786440 | tf_op jit(solution)/shard_map/ppermute | solution.py:498
  36.8 1.6 %shard_map.61 = (f32[3,4,32,512]{3,2,1,0:T(8,128)}, f32[9,4,16,128]{3,2,1,0:T(8,128)S(1)}, f32[14,16,128]{2,1,0:T(8,128)S(1)}, f32[3,136,8,128]{3,2,1,0:T(8,128)S(1)}, f32[6,128,128]{2,1,0:T(8,128)S(1)}) custom-call(s32[1]{0:T(128)} %bitcast.parity_ref, f32[3,8,128]{2,1,0:T(8,128)S(1)} %get-tuple-element.30.shift_ref, ...), custom_call_target="tpu_custom_call" | custom-call | tf_op jit(solution)/shard_map/pallas_call | solution.py:544
  38.4 0.0 collective-permute-done.5.odd_ref
  38.4 0.0 collective-permute-done.4.even_ref
  38.4 2.6 %krylov.4 = (f32[4,6,192,128]{3,2,1,0:T(8,128)S(1)}, f32[32,4,128]{2,1,0:T(4,128)S(1)}) custom-call(s32[1]{0:T(128)} %bitcast.parity_ref, f32[4,128,128]{2,1,0:T(8,128)S(1)} %get-tuple-element.40.refs_1_.mine_ref, f32[4,128,128]{2,1,0:T(8,128)S(1)} %collective-permute-done.4.even_ref, f32[4,128,128]{2,1,0:T(8,128)S(1)} %collective-permute-done.5.odd_ref, ...), custom_call_target="tpu_custom_call" | custom-call | tf_op jit(solution)/shard_map/krylov/pallas_call | solution.py:566
  41.0 15.8 %all_to_all.16.gram_ref = f32[32,4,128]{2,1,0:T(4,128)S(1)} all-to-all(f32[32,4,128]{2,1,0:T(4,128)S(1)} %get-tuple-element.46), channel_id=1, replica_groups=mesh['rows'=32] {'rows'}, dimensions={0} | all-to-all | bytes 131072 | tf_op jit(solution)/shard_map/all_to_all | solution.py:575
  56.8 0.7 shard_map.62
  57.4 0.9 %collective-permute-start.7 = (f32[4,128,128]{2,1,0:T(8,128)S(1)}, f32[4,128,128]{2,1,0:T(8,128)S(1)}, u32[]{:S(2)}, u32[]{:S(2)}) collective-permute-start(f32[4,128,128]{2,1,0:T(8,128)S(1)} %get-tuple-element.48.refs_1_.mine_ref), channel_id=1, source_target_pairs={{1,2},{3,4},{5,6},{7,8},{9,10},{11,12},{13,14},{15,16},{17,18},{19... | collective-permute-start | bytes 786440 | tf_op jit(solution)/shard_map/ppermute | solution.py:498
  58.3 1.8 %collective-permute-start.6 = (f32[4,128,128]{2,1,0:T(8,128)S(1)}, f32[4,128,128]{2,1,0:T(8,128)S(1)}, u32[]{:S(2)}, u32[]{:S(2)}) collective-permute-start(f32[4,128,128]{2,1,0:T(8,128)S(1)} %get-tuple-element.48.refs_1_.mine_ref), channel_id=1, source_target_pairs={{0,1},{1,0},{2,3},{3,2},{4,5},{5,4},{6,7},{7,6},{8,9},{9,8},{10,11... | collective-permute-start | bytes 786440 | tf_op jit(solution)/shard_map/ppermute | solution.py:498
  60.1 1.6 %shard_map.63 = (f32[3,4,32,512]{3,2,1,0:T(8,128)}, f32[9,4,16,128]{3,2,1,0:T(8,128)S(1)}, f32[14,16,128]{2,1,0:T(8,128)S(1)}, f32[3,136,8,128]{3,2,1,0:T(8,128)S(1)}, f32[6,128,128]{2,1,0:T(8,128)S(1)}) custom-call(s32[1]{0:T(128)} %bitcast.parity_ref, f32[3,8,128]{2,1,0:T(8,128)S(1)} %get-tuple-element.30.shift_ref, ...), custom_call_target="tpu_custom_call", output_to_operand_aliasing={{0}: (5, {})} | custom-call | tf_op jit(solution)/shard_map/pallas_call | solution.py:544
  61.7 0.0 collective-permute-done.7.odd_ref
  61.7 0.0 collective-permute-done.6.even_ref
  61.7 2.5 %krylov.5 = (f32[4,6,192,128]{3,2,1,0:T(8,128)S(1)}, f32[32,4,128]{2,1,0:T(4,128)S(1)}) custom-call(s32[1]{0:T(128)} %bitcast.parity_ref, f32[4,128,128]{2,1,0:T(8,128)S(1)} %get-tuple-element.48.refs_1_.mine_ref, f32[4,128,128]{2,1,0:T(8,128)S(1)} %collective-permute-done.6.even_ref, f32[4,128,128]{2,1,0:T(8,128)S(1)} %collective-permute-done.7.odd_ref, ...), custom_call_target="tpu_custom_call" | custom-call | tf_op jit(solution)/shard_map/krylov/pallas_call | solution.py:566
  64.2 15.6 %all_to_all.17.gram_ref = f32[32,4,128]{2,1,0:T(4,128)S(1)} all-to-all(f32[32,4,128]{2,1,0:T(4,128)S(1)} %get-tuple-element.55), channel_id=1, replica_groups=mesh['rows'=32] {'rows'}, dimensions={0} | all-to-all | bytes 131072 | tf_op jit(solution)/shard_map/all_to_all | solution.py:575
  79.8 1.7 %shard_map.64 = (f32[3,4,32,512]{3,2,1,0:T(8,128)}, f32[4,32,512]{2,1,0:T(8,128)}) custom-call(f32[3,8,128]{2,1,0:T(8,128)S(1)} %get-tuple-element.30.shift_ref, f32[32,4,128]{2,1,0:T(4,128)S(1)} %all_to_all.17.gram_ref, f32[4,6,192,128]{3,2,1,0:T(8,128)S(1)} %get-tuple-element.56.z_ref, ...), custom_call_target="tpu_custom_call", output_to_operand_aliasing={{0}: (5, {})} | custom-call | tf_op jit(solution)/shard_map/pallas_call | solution.py:578
Async XLA Ops:
  2.3 10.3 %collective-permute-start.1 = (f32[4,128,128]{2,1,0:T(8,128)S(1)}, f32[4,128,128]{2,1,0:T(8,128)S(1)}, u32[]{:S(2)}, u32[]{:S(2)}) collective-permute-start(f32[4,128,128]{2,1,0:T(8,128)S(1)} %get-tuple-element.31.refs_3_.mine_ref), channel_id=1, source_target_pairs={{1,2},{3,4},{5,6},{7,8},{9,10},{11,12},{13,14},{15,16},{17,18},{19... | collective-permute-start | bytes 786440 | tf_op jit(solution)/shard_map/ppermute | solution.py:498
  3.0 9.6 %collective-permute-start = (f32[4,128,128]{2,1,0:T(8,128)S(1)}, f32[4,128,128]{2,1,0:T(8,128)S(1)}, u32[]{:S(2)}, u32[]{:S(2)}) collective-permute-start(f32[4,128,128]{2,1,0:T(8,128)S(1)} %get-tuple-element.31.refs_3_.mine_ref), channel_id=1, source_target_pairs={{0,1},{1,0},{2,3},{3,2},{4,5},{5,4},{6,7},{7,6},{8,9},{9,8},{10,11... | collective-permute-start | bytes 786440 | tf_op jit(solution)/shard_map/ppermute | solution.py:498
  7.4 3.6 %collective-permute-start.3 = (f32[4,72,128]{2,1,0:T(8,128)S(1)}, f32[4,72,128]{2,1,0:T(8,128)S(1)}, u32[]{:S(2)}, u32[]{:S(2)}) collective-permute-start(f32[4,72,128]{2,1,0:T(8,128)S(1)} %get-tuple-element.32.refs_0_), channel_id=1, source_target_pairs={{1,2},{3,4},{5,6},{7,8},{9,10},{11,12},{13,14},{15,16},{17,18},{19... | collective-permute-start | bytes 442376 | tf_op jit(solution)/shard_map/ppermute | solution.py:498
  8.1 3.9 %collective-permute-start.2 = (f32[4,72,128]{2,1,0:T(8,128)S(1)}, f32[4,72,128]{2,1,0:T(8,128)S(1)}, u32[]{:S(2)}, u32[]{:S(2)}) collective-permute-start(f32[4,72,128]{2,1,0:T(8,128)S(1)} %get-tuple-element.32.refs_0_), channel_id=1, source_target_pairs={{0,1},{1,0},{2,3},{3,2},{4,5},{5,4},{6,7},{7,6},{8,9},{9,8},{10,11... | collective-permute-start | bytes 442376 | tf_op jit(solution)/shard_map/ppermute | solution.py:498
  34.3 4.1 %collective-permute-start.5 = (f32[4,128,128]{2,1,0:T(8,128)S(1)}, f32[4,128,128]{2,1,0:T(8,128)S(1)}, u32[]{:S(2)}, u32[]{:S(2)}) collective-permute-start(f32[4,128,128]{2,1,0:T(8,128)S(1)} %get-tuple-element.40.refs_1_.mine_ref), channel_id=1, source_target_pairs={{1,2},{3,4},{5,6},{7,8},{9,10},{11,12},{13,14},{15,16},{17,18},{19... | collective-permute-start | bytes 786440 | tf_op jit(solution)/shard_map/ppermute | solution.py:498
  35.0 3.4 %collective-permute-start.4 = (f32[4,128,128]{2,1,0:T(8,128)S(1)}, f32[4,128,128]{2,1,0:T(8,128)S(1)}, u32[]{:S(2)}, u32[]{:S(2)}) collective-permute-start(f32[4,128,128]{2,1,0:T(8,128)S(1)} %get-tuple-element.40.refs_1_.mine_ref), channel_id=1, source_target_pairs={{0,1},{1,0},{2,3},{3,2},{4,5},{5,4},{6,7},{7,6},{8,9},{9,8},{10,11... | collective-permute-start | bytes 786440 | tf_op jit(solution)/shard_map/ppermute | solution.py:498
  57.4 4.3 %collective-permute-start.7 = (f32[4,128,128]{2,1,0:T(8,128)S(1)}, f32[4,128,128]{2,1,0:T(8,128)S(1)}, u32[]{:S(2)}, u32[]{:S(2)}) collective-permute-start(f32[4,128,128]{2,1,0:T(8,128)S(1)} %get-tuple-element.48.refs_1_.mine_ref), channel_id=1, source_target_pairs={{1,2},{3,4},{5,6},{7,8},{9,10},{11,12},{13,14},{15,16},{17,18},{19... | collective-permute-start | bytes 786440 | tf_op jit(solution)/shard_map/ppermute | solution.py:498
  58.3 3.4 %collective-permute-start.6 = (f32[4,128,128]{2,1,0:T(8,128)S(1)}, f32[4,128,128]{2,1,0:T(8,128)S(1)}, u32[]{:S(2)}, u32[]{:S(2)}) collective-permute-start(f32[4,128,128]{2,1,0:T(8,128)S(1)} %get-tuple-element.48.refs_1_.mine_ref), channel_id=1, source_target_pairs={{0,1},{1,0},{2,3},{3,2},{4,5},{5,4},{6,7},{7,6},{8,9},{9,8},{10,11... | collective-permute-start | bytes 786440 | tf_op jit(solution)/shard_map/ppermute | solution.py:498

commit v5 on v4

--- a/solution.py
+++ b/solution.py
@@ -6,7 +6,6 @@
 from jax.experimental import pallas as pl
 from jax.experimental.pallas import tpu as pltpu
 from jax.sharding import PartitionSpec as P
-
 
 ITERS = 4
 CELLS = 4
@@ -469,7 +468,7 @@
     return pl.BlockSpec(memory_space=pltpu.VMEM)
 
 
-def low_block(rows, cols, width, step):
+def low_block(steps, rows, cols, width, step):
     return pl.BlockSpec((1, rows, cols, width), lambda i: (step, 0, 0, 0))
 
 
@@ -538,7 +537,7 @@
             scratch = []
         else:
             beside = (coefs, mine, u_mine) + (() if lowrank is None else (lowrank,))
-            lead_shape, lead_spec = low_shape, low_block(rows, cols, width, step - 1)
+            lead_shape, lead_spec = low_shape, low_block(steps, rows, cols, width, step - 1)
             scratch = [pltpu.VMEM((width, LANES), f32)]
         even, odd = exchange(mine)
         lead, *factors = pl.pallas_call(
@@ -550,6 +549,7 @@
             scratch_shapes=[pltpu.VMEM((CELLS - 1, block, LANES), f32), pltpu.VMEM((block, LANES), f32)] + scratch,
             input_output_aliases={} if first or lowrank is None else {5: 0},
             compiler_params=params(),
+            name=f"side{step}",
         )(parity, shift_rows, *beside)
         if first:
             coefs = lead
@@ -579,7 +579,7 @@
             functools.partial(update_kernel, step=step, last=last, rows=rows, cols=cols),
             grid=(1,),
             in_specs=[vmem()] * 5 + ([low_spec] if alias else []),
-            out_specs=[low_block(rows, cols, width, step) if last else vmem(), vmem()],
+            out_specs=[low_block(steps, rows, cols, width, step) if last else vmem(), vmem()],
             out_shape=[jax.ShapeDtypeStruct(shape, f32) for shape in shapes],
             scratch_shapes=[
                 pltpu.VMEM((CELLS + 2, (rows + 2) * cols, LANES), f32),
@@ -589,6 +589,7 @@
             ],
             input_output_aliases={5: 0} if alias else {},
             compiler_params=params(),
+            name=f"update{step}",
         )(*((shift_rows, gram, z, mine, coefs) + ((lowrank,) if alias else ())))
     return u_mine, mine
 

time: 81.7 us -> 81.7 us (level)
  no operation moved by 1% of the time
where the time goes in v5:
time: 81.7 us; the launch traced here: 81.4 us
  blocking collectives  49.9 us (61%)
  Pallas kernels  16 us (20%)
  starting transfers between devices  13.8 us (17%)
  waiting for transfers between devices  1.02 us (1%)
    all_to_all x3, blocking collectives, shards(): gram = lax.all_to_all(gram, 'rows', 0, 0)  49.9 us
    ppermute x8, starting transfers between devices, exchange(): return (lax.ppermute(x, 'rows', within), lax.ppermute(x, 'rows', across))  13.8 us
    pallas_call x3, Pallas kernels, shards(): pl.pallas_call(functools.partial(krylov_kernel, rows=rows, cols=cols, pee...  7.53 us
    pallas_call x3, Pallas kernels, shards(): pl.pallas_call(functools.partial(side_kernel, step=step, rows=rows, cols=...  3.77 us
    pallas_call x3, Pallas kernels, shards(): pl.pallas_call(functools.partial(update_kernel, step=step, last=last, row...  2.98 us
    pallas_call x1, Pallas kernels, shards(): pl.pallas_call(pack_kernel, in_specs=[pl.BlockSpec(memory_space=pltpu.HBM...  1.69 us
  transfers between devices with their start and end apart: 8, of which 1 were waited for; matrix products, arithmetic and copies ran while one was open for 0% of the time, Pallas kernels for 5%

profile of v5, /device:TPU:0, one launch (start us, length us, event | category | flops | bytes accessed | tf_op | source)
XLA Modules:
  0.0 81.4 jit_solution(1141026580435973257)
XLA Ops:
  0.6 1.7 %pack.1 = (f32[4,72,128]{2,1,0:T(8,128)S(1)}, f32[4,128,128]{2,1,0:T(8,128)S(1)}, f32[3,8,128]{2,1,0:T(8,128)S(1)}) custom-call(f32[3]{0:T(128)} %shift_hbm.1, f32[9,4,512]{2,1,0:T(4,128)} %stiff_hbm.1, f32[9,4,512]{2,1,0:T(4,128)} %mass_hbm.1, f32[4,32,512]{2,1,0:T(8,128)} %factor_hbm.1), custom_call_target="tpu_custom_call" | custom-call | tf_op jit(solution)/shard_map/pack/pallas_call | solution.py:503
  2.3 0.7 collective-permute-start.1
  3.0 4.4 %collective-permute-start = (f32[4,128,128]{2,1,0:T(8,128)S(1)}, f32[4,128,128]{2,1,0:T(8,128)S(1)}, u32[]{:S(2)}, u32[]{:S(2)}) collective-permute-start(f32[4,128,128]{2,1,0:T(8,128)S(1)} %get-tuple-element.31.refs_3_.mine_ref), channel_id=1, source_target_pairs={{0,1},{1,0},{2,3},{3,2},{4,5},{5,4},{6,7},{7,6},{8,9},{9,8},{10,11... | collective-permute-start | bytes 786440 | tf_op jit(solution)/shard_map/ppermute | solution.py:497
  7.4 0.7 collective-permute-start.3
  8.1 2.9 %collective-permute-start.2 = (f32[4,72,128]{2,1,0:T(8,128)S(1)}, f32[4,72,128]{2,1,0:T(8,128)S(1)}, u32[]{:S(2)}, u32[]{:S(2)}) collective-permute-start(f32[4,72,128]{2,1,0:T(8,128)S(1)} %get-tuple-element.32.refs_0_), channel_id=1, source_target_pairs={{0,1},{1,0},{2,3},{3,2},{4,5},{5,4},{6,7},{7,6},{8,9},{9,8},{10,11... | collective-permute-start | bytes 442376 | tf_op jit(solution)/shard_map/ppermute | solution.py:497
  11.0 0.0 collective-permute-done.3.refs_2_
  11.0 1.0 %collective-permute-done.2.refs_1_ = f32[4,72,128]{2,1,0:T(8,128)S(1)} collective-permute-done((f32[4,72,128]{2,1,0:T(8,128)S(1)}, f32[4,72,128]{2,1,0:T(8,128)S(1)}, u32[]{:S(2)}, u32[]{:S(2)}) %collective-permute-start.2) | collective-permute-done | bytes 147488 | tf_op jit(solution)/shard_map/ppermute | solution.py:497
  12.0 0.6 side0.1
  12.6 0.0 collective-permute-done.1.odd_ref
  12.6 0.0 collective-permute-done.even_ref
  12.6 2.5 %krylov.3 = (f32[4,6,192,128]{3,2,1,0:T(8,128)S(1)}, f32[32,4,128]{2,1,0:T(4,128)S(1)}) custom-call(s32[1]{0:T(128)} %bitcast.parity_ref, f32[4,128,128]{2,1,0:T(8,128)S(1)} %get-tuple-element.31.refs_3_.mine_ref, f32[4,128,128]{2,1,0:T(8,128)S(1)} %collective-permute-done.even_ref, f32[4,128,128]{2,1,0:T(8,128)S(1)} %collective-permute-done.1.odd_ref, ...), custom_call_target="tpu_custom_call" | custom-call | tf_op jit(solution)/shard_map/krylov/pallas_call | solution.py:566
  15.1 18.5 %all_to_all.15.gram_ref = f32[32,4,128]{2,1,0:T(4,128)S(1)} all-to-all(f32[32,4,128]{2,1,0:T(4,128)S(1)} %get-tuple-element.37), channel_id=1, replica_groups=mesh['rows'=32] {'rows'}, dimensions={0} | all-to-all | bytes 131072 | tf_op jit(solution)/shard_map/all_to_all | solution.py:575
  33.7 0.7 update0.1
  34.3 0.7 collective-permute-start.5
  35.0 1.8 %collective-permute-start.4 = (f32[4,128,128]{2,1,0:T(8,128)S(1)}, f32[4,128,128]{2,1,0:T(8,128)S(1)}, u32[]{:S(2)}, u32[]{:S(2)}) collective-permute-start(f32[4,128,128]{2,1,0:T(8,128)S(1)} %get-tuple-element.40.refs_1_.mine_ref), channel_id=1, source_target_pairs={{0,1},{1,0},{2,3},{3,2},{4,5},{5,4},{6,7},{7,6},{8,9},{9,8},{10,11... | collective-permute-start | bytes 786440 | tf_op jit(solution)/shard_map/ppermute | solution.py:497
  36.8 1.6 %side1.1 = (f32[3,4,32,512]{3,2,1,0:T(8,128)}, f32[9,4,16,128]{3,2,1,0:T(8,128)S(1)}, f32[14,16,128]{2,1,0:T(8,128)S(1)}, f32[3,136,8,128]{3,2,1,0:T(8,128)S(1)}, f32[6,128,128]{2,1,0:T(8,128)S(1)}) custom-call(s32[1]{0:T(128)} %bitcast.parity_ref, f32[3,8,128]{2,1,0:T(8,128)S(1)} %get-tuple-element.30.shift_ref, ...), custom_call_target="tpu_custom_call" | custom-call | tf_op jit(solution)/shard_map/side1/pallas_call | solution.py:543
  38.4 0.0 collective-permute-done.5.odd_ref
  38.4 0.0 collective-permute-done.4.even_ref
  38.4 2.6 %krylov.4 = (f32[4,6,192,128]{3,2,1,0:T(8,128)S(1)}, f32[32,4,128]{2,1,0:T(4,128)S(1)}) custom-call(s32[1]{0:T(128)} %bitcast.parity_ref, f32[4,128,128]{2,1,0:T(8,128)S(1)} %get-tuple-element.40.refs_1_.mine_ref, f32[4,128,128]{2,1,0:T(8,128)S(1)} %collective-permute-done.4.even_ref, f32[4,128,128]{2,1,0:T(8,128)S(1)} %collective-permute-done.5.odd_ref, ...), custom_call_target="tpu_custom_call" | custom-call | tf_op jit(solution)/shard_map/krylov/pallas_call | solution.py:566
  41.0 15.8 %all_to_all.16.gram_ref = f32[32,4,128]{2,1,0:T(4,128)S(1)} all-to-all(f32[32,4,128]{2,1,0:T(4,128)S(1)} %get-tuple-element.46), channel_id=1, replica_groups=mesh['rows'=32] {'rows'}, dimensions={0} | all-to-all | bytes 131072 | tf_op jit(solution)/shard_map/all_to_all | solution.py:575
  56.8 0.7 update1.1
  57.4 0.9 %collective-permute-start.7 = (f32[4,128,128]{2,1,0:T(8,128)S(1)}, f32[4,128,128]{2,1,0:T(8,128)S(1)}, u32[]{:S(2)}, u32[]{:S(2)}) collective-permute-start(f32[4,128,128]{2,1,0:T(8,128)S(1)} %get-tuple-element.48.refs_1_.mine_ref), channel_id=1, source_target_pairs={{1,2},{3,4},{5,6},{7,8},{9,10},{11,12},{13,14},{15,16},{17,18},{19... | collective-permute-start | bytes 786440 | tf_op jit(solution)/shard_map/ppermute | solution.py:497
  58.3 1.8 %collective-permute-start.6 = (f32[4,128,128]{2,1,0:T(8,128)S(1)}, f32[4,128,128]{2,1,0:T(8,128)S(1)}, u32[]{:S(2)}, u32[]{:S(2)}) collective-permute-start(f32[4,128,128]{2,1,0:T(8,128)S(1)} %get-tuple-element.48.refs_1_.mine_ref), channel_id=1, source_target_pairs={{0,1},{1,0},{2,3},{3,2},{4,5},{5,4},{6,7},{7,6},{8,9},{9,8},{10,11... | collective-permute-start | bytes 786440 | tf_op jit(solution)/shard_map/ppermute | solution.py:497
  60.1 1.6 %side2.1 = (f32[3,4,32,512]{3,2,1,0:T(8,128)}, f32[9,4,16,128]{3,2,1,0:T(8,128)S(1)}, f32[14,16,128]{2,1,0:T(8,128)S(1)}, f32[3,136,8,128]{3,2,1,0:T(8,128)S(1)}, f32[6,128,128]{2,1,0:T(8,128)S(1)}) custom-call(s32[1]{0:T(128)} %bitcast.parity_ref, f32[3,8,128]{2,1,0:T(8,128)S(1)} %get-tuple-element.30.shift_ref, ...), custom_call_target="tpu_custom_call", output_to_operand_aliasing={{0}: (5, {})} | custom-call | tf_op jit(solution)/shard_map/side2/pallas_call | solution.py:543
  61.7 0.0 collective-permute-done.7.odd_ref
  61.7 0.0 collective-permute-done.6.even_ref
  61.7 2.5 %krylov.5 = (f32[4,6,192,128]{3,2,1,0:T(8,128)S(1)}, f32[32,4,128]{2,1,0:T(4,128)S(1)}) custom-call(s32[1]{0:T(128)} %bitcast.parity_ref, f32[4,128,128]{2,1,0:T(8,128)S(1)} %get-tuple-element.48.refs_1_.mine_ref, f32[4,128,128]{2,1,0:T(8,128)S(1)} %collective-permute-done.6.even_ref, f32[4,128,128]{2,1,0:T(8,128)S(1)} %collective-permute-done.7.odd_ref, ...), custom_call_target="tpu_custom_call" | custom-call | tf_op jit(solution)/shard_map/krylov/pallas_call | solution.py:566
  64.2 15.6 %all_to_all.17.gram_ref = f32[32,4,128]{2,1,0:T(4,128)S(1)} all-to-all(f32[32,4,128]{2,1,0:T(4,128)S(1)} %get-tuple-element.55), channel_id=1, replica_groups=mesh['rows'=32] {'rows'}, dimensions={0} | all-to-all | bytes 131072 | tf_op jit(solution)/shard_map/all_to_all | solution.py:575
  79.8 1.7 %update2.1 = (f32[3,4,32,512]{3,2,1,0:T(8,128)}, f32[4,32,512]{2,1,0:T(8,128)}) custom-call(f32[3,8,128]{2,1,0:T(8,128)S(1)} %get-tuple-element.30.shift_ref, f32[32,4,128]{2,1,0:T(4,128)S(1)} %all_to_all.17.gram_ref, f32[4,6,192,128]{3,2,1,0:T(8,128)S(1)} %get-tuple-element.56.z_ref, ...), custom_call_target="tpu_custom_call", output_to_operand_aliasing={{0}: (5, {})} | custom-call | tf_op jit(solution)/shard_map/update2/pallas_call | solution.py:578
Async XLA Ops:
  2.3 10.3 %collective-permute-start.1 = (f32[4,128,128]{2,1,0:T(8,128)S(1)}, f32[4,128,128]{2,1,0:T(8,128)S(1)}, u32[]{:S(2)}, u32[]{:S(2)}) collective-permute-start(f32[4,128,128]{2,1,0:T(8,128)S(1)} %get-tuple-element.31.refs_3_.mine_ref), channel_id=1, source_target_pairs={{1,2},{3,4},{5,6},{7,8},{9,10},{11,12},{13,14},{15,16},{17,18},{19... | collective-permute-start | bytes 786440 | tf_op jit(solution)/shard_map/ppermute | solution.py:497
  3.0 9.6 %collective-permute-start = (f32[4,128,128]{2,1,0:T(8,128)S(1)}, f32[4,128,128]{2,1,0:T(8,128)S(1)}, u32[]{:S(2)}, u32[]{:S(2)}) collective-permute-start(f32[4,128,128]{2,1,0:T(8,128)S(1)} %get-tuple-element.31.refs_3_.mine_ref), channel_id=1, source_target_pairs={{0,1},{1,0},{2,3},{3,2},{4,5},{5,4},{6,7},{7,6},{8,9},{9,8},{10,11... | collective-permute-start | bytes 786440 | tf_op jit(solution)/shard_map/ppermute | solution.py:497
  7.4 3.6 %collective-permute-start.3 = (f32[4,72,128]{2,1,0:T(8,128)S(1)}, f32[4,72,128]{2,1,0:T(8,128)S(1)}, u32[]{:S(2)}, u32[]{:S(2)}) collective-permute-start(f32[4,72,128]{2,1,0:T(8,128)S(1)} %get-tuple-element.32.refs_0_), channel_id=1, source_target_pairs={{1,2},{3,4},{5,6},{7,8},{9,10},{11,12},{13,14},{15,16},{17,18},{19... | collective-permute-start | bytes 442376 | tf_op jit(solution)/shard_map/ppermute | solution.py:497
  8.1 3.9 %collective-permute-start.2 = (f32[4,72,128]{2,1,0:T(8,128)S(1)}, f32[4,72,128]{2,1,0:T(8,128)S(1)}, u32[]{:S(2)}, u32[]{:S(2)}) collective-permute-start(f32[4,72,128]{2,1,0:T(8,128)S(1)} %get-tuple-element.32.refs_0_), channel_id=1, source_target_pairs={{0,1},{1,0},{2,3},{3,2},{4,5},{5,4},{6,7},{7,6},{8,9},{9,8},{10,11... | collective-permute-start | bytes 442376 | tf_op jit(solution)/shard_map/ppermute | solution.py:497
  34.3 4.1 %collective-permute-start.5 = (f32[4,128,128]{2,1,0:T(8,128)S(1)}, f32[4,128,128]{2,1,0:T(8,128)S(1)}, u32[]{:S(2)}, u32[]{:S(2)}) collective-permute-start(f32[4,128,128]{2,1,0:T(8,128)S(1)} %get-tuple-element.40.refs_1_.mine_ref), channel_id=1, source_target_pairs={{1,2},{3,4},{5,6},{7,8},{9,10},{11,12},{13,14},{15,16},{17,18},{19... | collective-permute-start | bytes 786440 | tf_op jit(solution)/shard_map/ppermute | solution.py:497
  35.0 3.4 %collective-permute-start.4 = (f32[4,128,128]{2,1,0:T(8,128)S(1)}, f32[4,128,128]{2,1,0:T(8,128)S(1)}, u32[]{:S(2)}, u32[]{:S(2)}) collective-permute-start(f32[4,128,128]{2,1,0:T(8,128)S(1)} %get-tuple-element.40.refs_1_.mine_ref), channel_id=1, source_target_pairs={{0,1},{1,0},{2,3},{3,2},{4,5},{5,4},{6,7},{7,6},{8,9},{9,8},{10,11... | collective-permute-start | bytes 786440 | tf_op jit(solution)/shard_map/ppermute | solution.py:497
  57.4 4.3 %collective-permute-start.7 = (f32[4,128,128]{2,1,0:T(8,128)S(1)}, f32[4,128,128]{2,1,0:T(8,128)S(1)}, u32[]{:S(2)}, u32[]{:S(2)}) collective-permute-start(f32[4,128,128]{2,1,0:T(8,128)S(1)} %get-tuple-element.48.refs_1_.mine_ref), channel_id=1, source_target_pairs={{1,2},{3,4},{5,6},{7,8},{9,10},{11,12},{13,14},{15,16},{17,18},{19... | collective-permute-start | bytes 786440 | tf_op jit(solution)/shard_map/ppermute | solution.py:497
  58.3 3.4 %collective-permute-start.6 = (f32[4,128,128]{2,1,0:T(8,128)S(1)}, f32[4,128,128]{2,1,0:T(8,128)S(1)}, u32[]{:S(2)}, u32[]{:S(2)}) collective-permute-start(f32[4,128,128]{2,1,0:T(8,128)S(1)} %get-tuple-element.48.refs_1_.mine_ref), channel_id=1, source_target_pairs={{0,1},{1,0},{2,3},{3,2},{4,5},{5,4},{6,7},{7,6},{8,9},{9,8},{10,11... | collective-permute-start | bytes 786440 | tf_op jit(solution)/shard_map/ppermute | solution.py:497

commit v6 on v4

--- a/solution.py
+++ b/solution.py
@@ -69,7 +69,7 @@
 
 
 def pack_kernel(
-    shift_hbm, stiff_hbm, mass_hbm, factor_hbm, coefs_out, field_out, shifts_out,
+    shift_hbm, stiff_hbm, mass_hbm, factor_hbm, field_out, mass_out, shifts_out,
     stage, gather, shift_ref, stiff_ref, mass_ref, factor_ref, shift_sem, stiff_sem, mass_sem, factor_sem,
 ):
     copies = [
@@ -91,25 +91,31 @@
         for entry in range(entries):
             at = (which * entries + entry) * rows
             gather[at : at + rows, :] = ref[entry]
+    copies[3].wait()
+    for step in range(shifts_out.shape[0]):
+        shifts_out[step] = jnp.full(shifts_out.shape[1:], shift_ref[step], jnp.float32)
     planes = to_chunks(gather[...], stage)
-    count = 2 * entries * rows
+    count = entries * rows
     lane = lax.broadcasted_iota(jnp.int32, (count, LANES), 1)
-    line = lax.broadcasted_iota(jnp.int32, (count, LANES), 0)
-    column = (line // rows) % 3
+    column = (lax.broadcasted_iota(jnp.int32, (count, LANES), 0) // rows) % 3
     for cell in range(CELLS):
-        plane = planes[cell][0:count, :]
+        stiff = planes[cell][0:count, :]
+        mass = planes[cell][count : 2 * count, :]
+        plane = stiff + shift_ref[0] * mass
+        outside = None
         if cell == 0:
-            plane = jnp.where((lane == 0) & (column == 0), 0.0, plane)
+            outside = (lane == 0) & (column == 0)
         if cell == CELLS - 1:
-            plane = jnp.where((lane == LANES - 1) & (column == 2), 0.0, plane)
-        coefs_out[cell] = plane
+            outside = (lane == LANES - 1) & (column == 2)
+        if outside is not None:
+            plane = jnp.where(outside, 0.0, plane)
+            mass = jnp.where(outside, 0.0, mass)
+        field_out[cell, rows * cols : rows * cols + count, :] = plane
+        mass_out[cell] = mass
     copies[0].wait()
     planes = to_chunks(factor_ref[...].reshape(rows * cols, width), stage)
     for cell in range(CELLS):
-        field_out[cell] = planes[cell]
-    copies[3].wait()
-    for step in range(shifts_out.shape[0]):
-        shifts_out[step] = jnp.full(shifts_out.shape[1:], shift_ref[step], jnp.float32)
+        field_out[cell, 0 : rows * cols, :] = planes[cell]
 
 
 def factor_chunks(group, below, center, above, c3, l0, r0, chunk):
@@ -199,15 +205,18 @@
     return x, previous_chunk(x), x0n
 
 
-def build_lines(coefs_ref, shift, line, ext):
+def join_rows(out, own_ref, even_ref, odd_ref, low_is_even, rows, base):
     for entry in range(len(OFFSETS)):
+        at = slice(base + entry * rows, base + (entry + 1) * rows)
         for cell in range(CELLS):
-            line[entry, cell, 0:ext, :] = (
-                coefs_ref[0, entry, cell, 0:ext, :] + shift * coefs_ref[1, entry, cell, 0:ext, :]
-            )
-
-
-def build_factors(line, inner, chunk, rows, cols, ext):
+            even = even_ref[cell, at, :]
+            odd = odd_ref[cell, at, :]
+            out[entry, cell, 0:rows, :] = jnp.where(low_is_even, even, odd)
+            out[entry, cell, rows : 2 * rows, :] = own_ref[cell, at, :]
+            out[entry, cell, 2 * rows : 3 * rows, :] = jnp.where(low_is_even, odd, even)
+
+
+def build_factors(line, inner, chunk, rows, cols, ext, groups=(0, 1, 2)):
     a = [line[3, cell, 0:ext, :] for cell in range(CELLS)]
     d = [line[4, cell, 0:ext, :] for cell in range(CELLS)]
     c = [line[5, cell, 0:ext, :] for cell in range(CELLS)]
@@ -232,7 +241,7 @@
     ):
         inner[index, 0:ext, :] = value
     planes = (a[3] * l2, d[3] + a[3] * r2, c[3], l0, r0)
-    for group in range(ext // rows):
+    for group in groups:
         turned = [
             split(
                 jnp.concatenate(
@@ -293,32 +302,46 @@
             )
 
 
-def side_kernel(parity_ref, shift_ref, *refs, step, rows, cols):
-    ext = 3 * rows
-    entries = len(OFFSETS)
-    if step == 0:
-        own_ref, even_ref, odd_ref, mine_ref, coefs_ref, line, inner, chunk, z_out, px, qx = refs
-        low_is_even = parity_ref[0] == 1
-        for which in range(2):
-            for entry in range(entries):
-                at = (which * entries + entry) * rows
-                for cell in range(CELLS):
-                    even = even_ref[cell, at : at + rows, :]
-                    odd = odd_ref[cell, at : at + rows, :]
-                    coefs_ref[which, entry, cell, 0:rows, :] = jnp.where(low_is_even, even, odd)
-                    coefs_ref[which, entry, cell, rows : 2 * rows, :] = own_ref[cell, at : at + rows, :]
-                    coefs_ref[which, entry, cell, 2 * rows : ext, :] = jnp.where(low_is_even, odd, even)
-    else:
-        coefs_ref, mine_ref, u_ref = refs[:3]
-        low_out, line, inner, chunk, z_out, px, qx, stage = refs[-8:]
-    build_lines(coefs_ref, shift_ref[step, 0:1, :], line, ext)
-    build_factors(line, inner, chunk, rows, cols, ext)
-
+def own_kernel(mine_ref, z_out, line, inner, chunk, px, qx, *, rows, cols):
+    line[...] = jnp.zeros(line.shape, jnp.float32)
+    for entry in (3, 4, 5):
+        at = rows * cols + entry * rows
+        for cell in range(CELLS):
+            line[entry, cell, rows : 2 * rows, :] = mine_ref[cell, at : at + rows, :]
+    build_factors(line, inner, chunk, rows, cols, 3 * rows, (1,))
+    solve_own(mine_ref, inner, chunk, px, qx, z_out, rows, cols)
+
+
+def solve_own(mine_ref, inner, chunk, px, qx, z_out, rows, cols):
     def read(cell, row):
         return mine_ref[cell, (row - rows) * cols : (row - rows + 1) * cols, :]
 
     line_solve(1, list(range(rows, 2 * rows)), read, inner, chunk, px, qx, z_out, rows, rows, cols)
+
+
+def side_kernel(parity_ref, shift_ref, mine_ref, *refs, step, rows, cols):
+    ext = 3 * rows
+    low_is_even = parity_ref[0] == 1
+    if step == 0:
+        even_ref, odd_ref, line, inner, chunk = refs
+        join_rows(line, mine_ref, even_ref, odd_ref, low_is_even, rows, rows * cols)
+    else:
+        if step == 1:
+            base_ref, u_ref, mass_ref, even_ref, odd_ref = refs[:5]
+            low_out, line, inner, chunk, z_out, mass_all, px, qx, stage = refs[-9:]
+            join_rows(mass_all, mass_ref, even_ref, odd_ref, low_is_even, rows, 0)
+        else:
+            base_ref, u_ref, mass_all = refs[:3]
+            low_out, line, inner, chunk, z_out, px, qx, stage = refs[-8:]
+        shift = shift_ref[step, 0:1, :] - shift_ref[0, 0:1, :]
+        for entry in range(len(OFFSETS)):
+            for cell in range(CELLS):
+                line[entry, cell, 0:ext, :] = (
+                    base_ref[entry, cell, 0:ext, :] + shift * mass_all[entry, cell, 0:ext, :]
+                )
+    build_factors(line, inner, chunk, rows, cols, ext)
     if step > 0:
+        solve_own(mine_ref, inner, chunk, px, qx, z_out, rows, cols)
         root = jnp.sqrt(2.0 * shift_ref[step - 1, 0:1, :])
         write_natural(low_out, 0, [root * u_ref[cell] for cell in range(CELLS)], stage, rows, cols)
 
@@ -342,9 +365,9 @@
     parity = parity_ref[0]
     at_even = jnp.where(parity == 0, 2 * rows, 0)
     at_odd = 2 * rows - at_even
-    wx[0, :, pl.ds(rows * cols, block), :] = mine_ref[...]
-    wx[0, :, pl.ds(pl.multiple_of(at_even * cols, cols), block), :] = even_ref[...]
-    wx[0, :, pl.ds(pl.multiple_of(at_odd * cols, cols), block), :] = odd_ref[...]
+    wx[0, :, pl.ds(rows * cols, block), :] = mine_ref[:, 0:block, :]
+    wx[0, :, pl.ds(pl.multiple_of(at_even * cols, cols), block), :] = even_ref[:, 0:block, :]
+    wx[0, :, pl.ds(pl.multiple_of(at_odd * cols, cols), block), :] = odd_ref[:, 0:block, :]
 
     def span(row, count=1):
         return slice(row * cols, (row + count) * cols)
@@ -415,7 +438,7 @@
     return y
 
 
-def update_kernel(shift_ref, gram_ref, z_ref, mine_ref, coefs_ref, *refs, step, last, rows, cols):
+def update_kernel(shift_ref, gram_ref, z_ref, mine_ref, mass_ref, *refs, step, last, rows, cols):
     low_out, next_out, ux, yx, own, stage = refs[-6:]
     parts = [gram_ref[peer] for peer in range(gram_ref.shape[0])]
     while len(parts) > 1:
@@ -449,7 +472,7 @@
     double = 2.0 * shift_ref[step, 0:1, :]
     for row in range(rows):
         image = stencil_rows(
-            lambda entry, cell: coefs_ref[1, entry, cell, rows + row : rows + row + 1, :],
+            lambda entry, cell: mass_ref[cell, entry * rows + row : entry * rows + row + 1, :],
             range(len(OFFSETS)), read_u, row + 1,
         )
         for cell in range(CELLS):
@@ -501,13 +524,17 @@
         pltpu.with_memory_space_constraint(array, pltpu.HBM) for array in (shifts, stiffness, mass, factor)
     ]
     chunked = (CELLS, block, LANES)
-    stencils, mine, shift_rows = pl.pallas_call(
+    mine, mass_own, shift_rows = pl.pallas_call(
         pack_kernel,
         in_specs=[pl.BlockSpec(memory_space=pltpu.HBM)] * 4,
         out_specs=[vmem()] * 3,
         out_shape=[
             jax.ShapeDtypeStruct(shape, f32)
-            for shape in ((CELLS, 2 * entries * rows, LANES), chunked, (steps, 8, LANES))
+            for shape in (
+                (CELLS, block + entries * rows, LANES),
+                (CELLS, entries * rows, LANES),
+                (steps, 8, LANES),
+            )
         ],
         scratch_shapes=[pltpu.VMEM((width, LANES), f32), pltpu.VMEM((LANES, width), f32)]
         + [pltpu.SMEM(shifts.shape, f32)]
@@ -518,43 +545,63 @@
     )(*arrays)
 
     z_shape = (ITERS, CELLS + 2, (rows + 2) * cols, LANES)
-    coef_shape = (2, entries, CELLS, ext_pad, LANES)
+    line_shape = (entries, CELLS, ext_pad, LANES)
     factor_shapes = (
-        (entries, CELLS, ext_pad, LANES),
+        line_shape,
         (PLANES, ext_pad, LANES),
         (3, CHUNK_PLANES, SUB, LANES),
         (CELLS + 2, block, LANES),
     )
+    solver_shapes = ((CELLS - 1, block, LANES), (block, LANES))
     low_shape = (steps, rows, cols, width)
     low_spec = pl.BlockSpec(memory_space=pl.ANY)
-    coefs = None
     lowrank = None
     for step in range(steps):
         first = step == 0
         last = step + 1 == steps
+        even, odd = exchange(mine)
         if first:
-            beside = (stencils, *exchange(stencils), mine)
-            lead_shape, lead_spec = coef_shape, vmem()
-            scratch = []
+            mass_ghosts = exchange(mass_own)
+            z_own = pl.pallas_call(
+                functools.partial(own_kernel, rows=rows, cols=cols),
+                in_specs=[vmem()],
+                out_specs=vmem(),
+                out_shape=jax.ShapeDtypeStruct(factor_shapes[3], f32),
+                scratch_shapes=[pltpu.VMEM(shape, f32) for shape in factor_shapes[:3] + solver_shapes],
+                compiler_params=params(),
+                name="own0",
+            )(mine)
+            beside = (even, odd)
         else:
-            beside = (coefs, mine, u_mine) + (() if lowrank is None else (lowrank,))
-            lead_shape, lead_spec = low_shape, low_block(rows, cols, width, step - 1)
-            scratch = [pltpu.VMEM((width, LANES), f32)]
-        even, odd = exchange(mine)
-        lead, *factors = pl.pallas_call(
+            beside = (base, u_mine) + ((mass_own, *mass_ghosts) if step == 1 else (mass_all,))
+        fixed = len(beside)
+        shapes = factor_shapes[:3] if first else factor_shapes
+        specs = [vmem()] * len(shapes)
+        scratch = [] if first else [pltpu.VMEM(shape, f32) for shape in solver_shapes]
+        if not first:
+            if lowrank is not None:
+                beside = beside + (lowrank,)
+            shapes = (low_shape,) + shapes + ((line_shape,) if step == 1 else ())
+            specs = [low_block(rows, cols, width, step - 1)] + [vmem()] * (len(shapes) - 1)
+            scratch = scratch + [pltpu.VMEM((width, LANES), f32)]
+        outs = pl.pallas_call(
             functools.partial(side_kernel, step=step, rows=rows, cols=cols),
             grid=(1,),
-            in_specs=[smem()] + [vmem()] * (5 if first else 4) + [low_spec] * (len(beside) - (4 if first else 3)),
-            out_specs=[lead_spec] + [vmem()] * 4,
-            out_shape=[jax.ShapeDtypeStruct(shape, f32) for shape in (lead_shape,) + factor_shapes],
-            scratch_shapes=[pltpu.VMEM((CELLS - 1, block, LANES), f32), pltpu.VMEM((block, LANES), f32)] + scratch,
-            input_output_aliases={} if first or lowrank is None else {5: 0},
+            in_specs=[smem()] + [vmem()] * (2 + fixed) + [low_spec] * (len(beside) - fixed),
+            out_specs=specs,
+            out_shape=[jax.ShapeDtypeStruct(shape, f32) for shape in shapes],
+            scratch_shapes=scratch,
+            input_output_aliases={3 + fixed: 0} if len(beside) > fixed else {},
             compiler_params=params(),
-        )(parity, shift_rows, *beside)
+        )(parity, shift_rows, mine, *beside)
+        if not first:
+            lowrank, *outs = outs
+        if step == 1:
+            *outs, mass_all = outs
+        factors = tuple(outs)
         if first:
-            coefs = lead
-        else:
-            lowrank = lead
+            base = factors[0]
+            factors = factors + (z_own,)
         shapes = [z_shape, (peers, gram_rows, LANES)]
         scratch = [
             (ITERS + 1, CELLS, ext * cols, LANES),
@@ -589,7 +636,7 @@
             ],
             input_output_aliases={5: 0} if alias else {},
             compiler_params=params(),
-        )(*((shift_rows, gram, z, mine, coefs) + ((lowrank,) if alias else ())))
+        )(*((shift_rows, gram, z, mine, mass_own) + ((lowrank,) if alias else ())))
     return u_mine, mine
 
 

time: 81.7 us -> 83.6 us (1.023)
  transfers between devices with their start and end apart: 8 -> 8, of which waited for: 1 -> 2; matrix products, arithmetic and copies ran while one was open for 0% -> 0% of each run, Pallas kernels for 5% -> 4%
where the time goes in v6:
time: 83.6 us; the launch traced here: 83.3 us
  blocking collectives  50.5 us (60%)
  Pallas kernels  16.5 us (20%)
  starting transfers between devices  14 us (17%)
  waiting for transfers between devices  1.67 us (2%)
    all_to_all x3, blocking collectives, shards(): gram = lax.all_to_all(gram, 'rows', 0, 0)  50.5 us
    ppermute x8, starting transfers between devices, exchange(): return (lax.ppermute(x, 'rows', within), lax.ppermute(x, 'rows', across))  14 us
    pallas_call x3, Pallas kernels, shards(): pl.pallas_call(functools.partial(krylov_kernel, rows=rows, cols=cols, pee...  7.59 us
    pallas_call x3, Pallas kernels, shards(): pl.pallas_call(functools.partial(side_kernel, step=step, rows=rows, cols=...  3.72 us
    pallas_call x3, Pallas kernels, shards(): pl.pallas_call(functools.partial(update_kernel, step=step, last=last, row...  2.96 us
    pallas_call x1, Pallas kernels, shards(): pl.pallas_call(pack_kernel, in_specs=[pl.BlockSpec(memory_space=pltpu.HBM...  1.7 us
    ppermute x8, waiting for transfers between devices, exchange(): return (lax.ppermute(x, 'rows', within), lax.ppermute(x, 'rows', across))  1.67 us
  transfers between devices with their start and end apart: 8, of which 2 were waited for; matrix products, arithmetic and copies ran while one was open for 0% of the time, Pallas kernels for 4%

profile of v6, /device:TPU:0, one launch (start us, length us, event | category | flops | bytes accessed | tf_op | source)
XLA Modules:
  0.0 83.3 jit_solution(6669066878405162651)
XLA Ops:
  0.6 1.7 %pack.1 = (f32[4,164,128]{2,1,0:T(8,128)S(1)}, f32[4,36,128]{2,1,0:T(8,128)S(1)}, f32[3,8,128]{2,1,0:T(8,128)S(1)}) custom-call(f32[3]{0:T(128)} %shift_hbm.1, f32[9,4,512]{2,1,0:T(4,128)} %stiff_hbm.1, f32[9,4,512]{2,1,0:T(4,128)} %mass_hbm.1, f32[4,32,512]{2,1,0:T(8,128)} %factor_hbm.1), custom_call_target="tpu_custom_call" | custom-call | tf_op jit(solution)/shard_map/pack/pallas_call | solution.py:527
  2.3 0.7 collective-permute-start.1
  3.0 4.4 %collective-permute-start = (f32[4,164,128]{2,1,0:T(8,128)S(1)}, f32[4,164,128]{2,1,0:T(8,128)S(1)}, u32[]{:S(2)}, u32[]{:S(2)}) collective-permute-start(f32[4,164,128]{2,1,0:T(8,128)S(1)} %get-tuple-element.30.mine_ref), channel_id=1, source_target_pairs={{0,1},{1,0},{2,3},{3,2},{4,5},{5,4},{6,7},{7,6},{8,9},{9,8},{10,11... | collective-permute-start | bytes 1007624 | tf_op jit(solution)/shard_map/ppermute | solution.py:521
  7.4 0.5 own0.1.z_mine
  7.9 0.0 collective-permute-done.1.refs_1_.odd_ref
  7.9 0.7 collective-permute-done.refs_0_.even_ref
  8.7 0.6 shard_map.59
  9.2 2.6 %krylov.3 = (f32[4,6,192,128]{3,2,1,0:T(8,128)S(1)}, f32[32,4,128]{2,1,0:T(4,128)S(1)}) custom-call(s32[1]{0:T(128)} %bitcast.parity_ref, f32[4,164,128]{2,1,0:T(8,128)S(1)} %get-tuple-element.30.mine_ref, f32[4,164,128]{2,1,0:T(8,128)S(1)} %collective-permute-done.refs_0_.even_ref, f32[4,164,128]{2,1,0:T(8,128)S(1)} %collective-permute-done.1.refs_1_.odd_ref, ...), custom_call_target="tpu_custom_call" | custom-call | tf_op jit(solution)/shard_map/krylov/pallas_call | solution.py:613
  11.8 20.4 %all_to_all.15.gram_ref = f32[32,4,128]{2,1,0:T(4,128)S(1)} all-to-all(f32[32,4,128]{2,1,0:T(4,128)S(1)} %get-tuple-element.34), channel_id=1, replica_groups=mesh['rows'=32] {'rows'}, dimensions={0} | all-to-all | bytes 131072 | tf_op jit(solution)/shard_map/all_to_all | solution.py:622
  32.3 0.6 shard_map.60
  32.9 0.7 collective-permute-start.3
  33.6 1.8 %collective-permute-start.2 = (f32[4,128,128]{2,1,0:T(8,128)S(1)}, f32[4,128,128]{2,1,0:T(8,128)S(1)}, u32[]{:S(2)}, u32[]{:S(2)}) collective-permute-start(f32[4,128,128]{2,1,0:T(8,128)S(1)} %get-tuple-element.37.mine_ref), channel_id=1, source_target_pairs={{0,1},{1,0},{2,3},{3,2},{4,5},{5,4},{6,7},{7,6},{8,9},{9,8},{10,11... | collective-permute-start | bytes 786440 | tf_op jit(solution)/shard_map/ppermute | solution.py:521
  35.4 0.7 collective-permute-start.5
  36.1 3.0 %collective-permute-start.4 = (f32[4,36,128]{2,1,0:T(8,128)S(1)}, f32[4,36,128]{2,1,0:T(8,128)S(1)}, u32[]{:S(2)}, u32[]{:S(2)}) collective-permute-start(f32[4,36,128]{2,1,0:T(8,128)S(1)} %get-tuple-element.36.mass_ref.refs_2_), channel_id=1, source_target_pairs={{0,1},{1,0},{2,3},{3,2},{4,5},{5,4},{6,7},{7,6},{8,9},{9,8},{10,11... | collective-permute-start | bytes 221192 | tf_op jit(solution)/shard_map/ppermute | solution.py:521
  39.1 0.0 collective-permute-done.5.refs_4_
  39.1 0.9 %collective-permute-done.4.refs_3_ = f32[4,36,128]{2,1,0:T(8,128)S(1)} collective-permute-done((f32[4,36,128]{2,1,0:T(8,128)S(1)}, f32[4,36,128]{2,1,0:T(8,128)S(1)}, u32[]{:S(2)}, u32[]{:S(2)}) %collective-permute-start.4) | collective-permute-done | bytes 73760 | tf_op jit(solution)/shard_map/ppermute | solution.py:521
  40.1 1.6 %shard_map.61 = (f32[3,4,32,512]{3,2,1,0:T(8,128)}, f32[9,4,16,128]{3,2,1,0:T(8,128)S(1)}, f32[14,16,128]{2,1,0:T(8,128)S(1)}, f32[3,136,8,128]{3,2,1,0:T(8,128)...) custom-call(s32[1]{0:T(128)} %bitcast.parity_ref, f32[3,8,128]{2,1,0:T(8,128)S(1)} %get-tuple-element.29.shift_ref, ...), custom_call_target="tpu_custom_call" | custom-call | tf_op jit(solution)/shard_map/pallas_call | solution.py:587
  41.7 0.0 collective-permute-done.3.odd_ref
  41.7 0.0 collective-permute-done.2.even_ref
  41.7 2.4 %krylov.4 = (f32[4,6,192,128]{3,2,1,0:T(8,128)S(1)}, f32[32,4,128]{2,1,0:T(4,128)S(1)}) custom-call(s32[1]{0:T(128)} %bitcast.parity_ref, f32[4,128,128]{2,1,0:T(8,128)S(1)} %get-tuple-element.37.mine_ref, f32[4,128,128]{2,1,0:T(8,128)S(1)} %collective-permute-done.2.even_ref, f32[4,128,128]{2,1,0:T(8,128)S(1)} %collective-permute-done.3.odd_ref, ...), custom_call_target="tpu_custom_call" | custom-call | tf_op jit(solution)/shard_map/krylov/pallas_call | solution.py:613
  44.1 14.5 %all_to_all.16.gram_ref = f32[32,4,128]{2,1,0:T(4,128)S(1)} all-to-all(f32[32,4,128]{2,1,0:T(4,128)S(1)} %get-tuple-element.43), channel_id=1, replica_groups=mesh['rows'=32] {'rows'}, dimensions={0} | all-to-all | bytes 131072 | tf_op jit(solution)/shard_map/all_to_all | solution.py:622
  58.6 0.7 shard_map.62
  59.2 0.9 %collective-permute-start.7 = (f32[4,128,128]{2,1,0:T(8,128)S(1)}, f32[4,128,128]{2,1,0:T(8,128)S(1)}, u32[]{:S(2)}, u32[]{:S(2)}) collective-permute-start(f32[4,128,128]{2,1,0:T(8,128)S(1)} %get-tuple-element.45.mine_ref), channel_id=1, source_target_pairs={{1,2},{3,4},{5,6},{7,8},{9,10},{11,12},{13,14},{15,16},{17,18},{19... | collective-permute-start | bytes 786440 | tf_op jit(solution)/shard_map/ppermute | solution.py:521
  60.1 1.8 %collective-permute-start.6 = (f32[4,128,128]{2,1,0:T(8,128)S(1)}, f32[4,128,128]{2,1,0:T(8,128)S(1)}, u32[]{:S(2)}, u32[]{:S(2)}) collective-permute-start(f32[4,128,128]{2,1,0:T(8,128)S(1)} %get-tuple-element.45.mine_ref), channel_id=1, source_target_pairs={{0,1},{1,0},{2,3},{3,2},{4,5},{5,4},{6,7},{7,6},{8,9},{9,8},{10,11... | collective-permute-start | bytes 786440 | tf_op jit(solution)/shard_map/ppermute | solution.py:521
  61.9 1.6 %shard_map.63 = (f32[3,4,32,512]{3,2,1,0:T(8,128)}, f32[9,4,16,128]{3,2,1,0:T(8,128)S(1)}, f32[14,16,128]{2,1,0:T(8,128)S(1)}, f32[3,136,8,128]{3,2,1,0:T(8,128)S(1)}, f32[6,128,128]{2,1,0:T(8,128)S(1)}) custom-call(s32[1]{0:T(128)} %bitcast.parity_ref, f32[3,8,128]{2,1,0:T(8,128)S(1)} %get-tuple-element.29.shift_ref, ...), custom_call_target="tpu_custom_call", output_to_operand_aliasing={{0}: (6, {})} | custom-call | tf_op jit(solution)/shard_map/pallas_call | solution.py:587
  63.5 0.0 collective-permute-done.7.odd_ref
  63.5 0.0 collective-permute-done.6.even_ref
  63.5 2.6 %krylov.5 = (f32[4,6,192,128]{3,2,1,0:T(8,128)S(1)}, f32[32,4,128]{2,1,0:T(4,128)S(1)}) custom-call(s32[1]{0:T(128)} %bitcast.parity_ref, f32[4,128,128]{2,1,0:T(8,128)S(1)} %get-tuple-element.45.mine_ref, f32[4,128,128]{2,1,0:T(8,128)S(1)} %collective-permute-done.6.even_ref, f32[4,128,128]{2,1,0:T(8,128)S(1)} %collective-permute-done.7.odd_ref, ...), custom_call_target="tpu_custom_call" | custom-call | tf_op jit(solution)/shard_map/krylov/pallas_call | solution.py:613
  66.1 15.6 %all_to_all.17.gram_ref = f32[32,4,128]{2,1,0:T(4,128)S(1)} all-to-all(f32[32,4,128]{2,1,0:T(4,128)S(1)} %get-tuple-element.53), channel_id=1, replica_groups=mesh['rows'=32] {'rows'}, dimensions={0} | all-to-all | bytes 131072 | tf_op jit(solution)/shard_map/all_to_all | solution.py:622
  81.7 1.7 %shard_map.64 = (f32[3,4,32,512]{3,2,1,0:T(8,128)}, f32[4,32,512]{2,1,0:T(8,128)}) custom-call(f32[3,8,128]{2,1,0:T(8,128)S(1)} %get-tuple-element.29.shift_ref, f32[32,4,128]{2,1,0:T(4,128)S(1)} %all_to_all.17.gram_ref, f32[4,6,192,128]{3,2,1,0:T(8,128)S(1)} %get-tuple-element.54.z_ref, ...), custom_call_target="tpu_custom_call", output_to_operand_aliasing={{0}: (5, {})} | custom-call | tf_op jit(solution)/shard_map/pallas_call | solution.py:625
Async XLA Ops:
  2.3 5.6 %collective-permute-start.1 = (f32[4,164,128]{2,1,0:T(8,128)S(1)}, f32[4,164,128]{2,1,0:T(8,128)S(1)}, u32[]{:S(2)}, u32[]{:S(2)}) collective-permute-start(f32[4,164,128]{2,1,0:T(8,128)S(1)} %get-tuple-element.30.mine_ref), channel_id=1, source_target_pairs={{1,2},{3,4},{5,6},{7,8},{9,10},{11,12},{13,14},{15,16},{17,18},{19... | collective-permute-start | bytes 1007624 | tf_op jit(solution)/shard_map/ppermute | solution.py:521
  3.0 5.7 %collective-permute-start = (f32[4,164,128]{2,1,0:T(8,128)S(1)}, f32[4,164,128]{2,1,0:T(8,128)S(1)}, u32[]{:S(2)}, u32[]{:S(2)}) collective-permute-start(f32[4,164,128]{2,1,0:T(8,128)S(1)} %get-tuple-element.30.mine_ref), channel_id=1, source_target_pairs={{0,1},{1,0},{2,3},{3,2},{4,5},{5,4},{6,7},{7,6},{8,9},{9,8},{10,11... | collective-permute-start | bytes 1007624 | tf_op jit(solution)/shard_map/ppermute | solution.py:521
  32.9 8.8 %collective-permute-start.3 = (f32[4,128,128]{2,1,0:T(8,128)S(1)}, f32[4,128,128]{2,1,0:T(8,128)S(1)}, u32[]{:S(2)}, u32[]{:S(2)}) collective-permute-start(f32[4,128,128]{2,1,0:T(8,128)S(1)} %get-tuple-element.37.mine_ref), channel_id=1, source_target_pairs={{1,2},{3,4},{5,6},{7,8},{9,10},{11,12},{13,14},{15,16},{17,18},{19... | collective-permute-start | bytes 786440 | tf_op jit(solution)/shard_map/ppermute | solution.py:521
  33.6 8.1 %collective-permute-start.2 = (f32[4,128,128]{2,1,0:T(8,128)S(1)}, f32[4,128,128]{2,1,0:T(8,128)S(1)}, u32[]{:S(2)}, u32[]{:S(2)}) collective-permute-start(f32[4,128,128]{2,1,0:T(8,128)S(1)} %get-tuple-element.37.mine_ref), channel_id=1, source_target_pairs={{0,1},{1,0},{2,3},{3,2},{4,5},{5,4},{6,7},{7,6},{8,9},{9,8},{10,11... | collective-permute-start | bytes 786440 | tf_op jit(solution)/shard_map/ppermute | solution.py:521
  35.4 3.7 %collective-permute-start.5 = (f32[4,36,128]{2,1,0:T(8,128)S(1)}, f32[4,36,128]{2,1,0:T(8,128)S(1)}, u32[]{:S(2)}, u32[]{:S(2)}) collective-permute-start(f32[4,36,128]{2,1,0:T(8,128)S(1)} %get-tuple-element.36.mass_ref.refs_2_), channel_id=1, source_target_pairs={{1,2},{3,4},{5,6},{7,8},{9,10},{11,12},{13,14},{15,16},{17,18},{19... | collective-permute-start | bytes 221192 | tf_op jit(solution)/shard_map/ppermute | solution.py:521
  36.1 4.0 %collective-permute-start.4 = (f32[4,36,128]{2,1,0:T(8,128)S(1)}, f32[4,36,128]{2,1,0:T(8,128)S(1)}, u32[]{:S(2)}, u32[]{:S(2)}) collective-permute-start(f32[4,36,128]{2,1,0:T(8,128)S(1)} %get-tuple-element.36.mass_ref.refs_2_), channel_id=1, source_target_pairs={{0,1},{1,0},{2,3},{3,2},{4,5},{5,4},{6,7},{7,6},{8,9},{9,8},{10,11... | collective-permute-start | bytes 221192 | tf_op jit(solution)/shard_map/ppermute | solution.py:521
  59.2 4.3 %collective-permute-start.7 = (f32[4,128,128]{2,1,0:T(8,128)S(1)}, f32[4,128,128]{2,1,0:T(8,128)S(1)}, u32[]{:S(2)}, u32[]{:S(2)}) collective-permute-start(f32[4,128,128]{2,1,0:T(8,128)S(1)} %get-tuple-element.45.mine_ref), channel_id=1, source_target_pairs={{1,2},{3,4},{5,6},{7,8},{9,10},{11,12},{13,14},{15,16},{17,18},{19... | collective-permute-start | bytes 786440 | tf_op jit(solution)/shard_map/ppermute | solution.py:521
  60.1 3.4 %collective-permute-start.6 = (f32[4,128,128]{2,1,0:T(8,128)S(1)}, f32[4,128,128]{2,1,0:T(8,128)S(1)}, u32[]{:S(2)}, u32[]{:S(2)}) collective-permute-start(f32[4,128,128]{2,1,0:T(8,128)S(1)} %get-tuple-element.45.mine_ref), channel_id=1, source_target_pairs={{0,1},{1,0},{2,3},{3,2},{4,5},{5,4},{6,7},{7,6},{8,9},{9,8},{10,11... | collective-permute-start | bytes 786440 | tf_op jit(solution)/shard_map/ppermute | solution.py:521

commit v7 on v6

--- a/solution.py
+++ b/solution.py
@@ -358,14 +358,13 @@
 
 def krylov_kernel(
     parity_ref, mine_ref, even_ref, odd_ref, line, inner, chunk, z_mine,
-    z_out, gram_out, wx, zx, px, qx, sums, *, rows, cols, peers,
+    z_out, gram_out, wx, px, qx, sums, *, rows, cols, peers,
 ):
     ext = 3 * rows
     block = rows * cols
     parity = parity_ref[0]
     at_even = jnp.where(parity == 0, 2 * rows, 0)
     at_odd = 2 * rows - at_even
-    wx[0, :, pl.ds(rows * cols, block), :] = mine_ref[:, 0:block, :]
     wx[0, :, pl.ds(pl.multiple_of(at_even * cols, cols), block), :] = even_ref[:, 0:block, :]
     wx[0, :, pl.ds(pl.multiple_of(at_odd * cols, cols), block), :] = odd_ref[:, 0:block, :]
 
@@ -374,6 +373,7 @@
 
     for k in range(ITERS):
         low, high = k, ext - k
+        zx = z_out.at[k]
 
         def read_w(cell, row):
             return wx[k, cell, span(row), :]
@@ -384,8 +384,6 @@
                 continue
             wanted = [row for row in range(group * rows, (group + 1) * rows) if low <= row < high]
             line_solve(group, wanted, read_w, inner, chunk, px, qx, zx, 0, rows, cols)
-        for row in range(rows - 1, 2 * rows + 1):
-            z_out[k, :, span(row - rows + 1), :] = zx[:, span(row), :]
 
         def read_z(slot, row):
             return zx[slot, span(row), :]
@@ -400,7 +398,8 @@
         for row in range(rows, 2 * rows):
             for cell in range(CELLS):
                 at = row * cols + tile * 8
-                w = [wx[k, cell, at : at + 8, :] for k in range(ITERS + 1)]
+                w = [mine_ref[cell, at - block : at - block + 8, :]]
+                w = w + [wx[k, cell, at : at + 8, :] for k in range(1, ITERS + 1)]
                 for index, (i, j) in enumerate(PAIRS):
                     term = w[i] * w[j]
                     total[index] = term if total[index] is None else total[index] + term
@@ -459,9 +458,9 @@
 
     for row in range(rows + 2):
         for slot in range(CELLS + 2):
-            value = yx[0] * z_ref[0, slot, span(row), :]
+            value = yx[0] * z_ref[0, slot, span(row + rows - 1), :]
             for k in range(1, ITERS):
-                value = value + yx[k] * z_ref[k, slot, span(row), :]
+                value = value + yx[k] * z_ref[k, slot, span(row + rows - 1), :]
             ux[slot, span(row), :] = value
             if not last and 0 < row <= rows and 0 < slot <= CELLS:
                 low_out[slot - 1, span(row - 1), :] = value
@@ -544,7 +543,7 @@
         name="pack",
     )(*arrays)
 
-    z_shape = (ITERS, CELLS + 2, (rows + 2) * cols, LANES)
+    z_shape = (ITERS, CELLS + 2, ext * cols, LANES)
     line_shape = (entries, CELLS, ext_pad, LANES)
     factor_shapes = (
         line_shape,
@@ -605,7 +604,6 @@
         shapes = [z_shape, (peers, gram_rows, LANES)]
         scratch = [
             (ITERS + 1, CELLS, ext * cols, LANES),
-            (CELLS + 2, ext * cols, LANES),
             (CELLS - 1, ext * cols, LANES),
             (ext * cols, LANES),
             (gram_rows * LANES, LANES),

time: 83.6 us -> 83.3 us (level)
  no operation moved by 1% of the time
where the time goes in v7:
time: 83.3 us; the launch traced here: 83.1 us
  blocking collectives  50.5 us (61%)
  Pallas kernels  16.2 us (19%)
  starting transfers between devices  14 us (17%)
  waiting for transfers between devices  1.67 us (2%)
    all_to_all x3, blocking collectives, shards(): gram = lax.all_to_all(gram, 'rows', 0, 0)  50.5 us
    ppermute x8, starting transfers between devices, exchange(): return (lax.ppermute(x, 'rows', within), lax.ppermute(x, 'rows', across))  14 us
    pallas_call x3, Pallas kernels, shards(): pl.pallas_call(functools.partial(krylov_kernel, rows=rows, cols=cols, pee...  7.36 us
    pallas_call x3, Pallas kernels, shards(): pl.pallas_call(functools.partial(side_kernel, step=step, rows=rows, cols=...  3.7 us
    pallas_call x3, Pallas kernels, shards(): pl.pallas_call(functools.partial(update_kernel, step=step, last=last, row...  2.94 us
    pallas_call x1, Pallas kernels, shards(): pl.pallas_call(pack_kernel, in_specs=[pl.BlockSpec(memory_space=pltpu.HBM...  1.7 us
    ppermute x8, waiting for transfers between devices, exchange(): return (lax.ppermute(x, 'rows', within), lax.ppermute(x, 'rows', across))  1.67 us
  transfers between devices with their start and end apart: 8, of which 2 were waited for; matrix products, arithmetic and copies ran while one was open for 0% of the time, Pallas kernels for 4%

profile of v7, /device:TPU:0, one launch (start us, length us, event | category | flops | bytes accessed | tf_op | source)
XLA Modules:
  0.0 83.1 jit_solution(11587594898461894823)
XLA Ops:
  0.6 1.7 %pack.1 = (f32[4,164,128]{2,1,0:T(8,128)S(1)}, f32[4,36,128]{2,1,0:T(8,128)S(1)}, f32[3,8,128]{2,1,0:T(8,128)S(1)}) custom-call(f32[3]{0:T(128)} %shift_hbm.1, f32[9,4,512]{2,1,0:T(4,128)} %stiff_hbm.1, f32[9,4,512]{2,1,0:T(4,128)} %mass_hbm.1, f32[4,32,512]{2,1,0:T(8,128)} %factor_hbm.1), custom_call_target="tpu_custom_call" | custom-call | tf_op jit(solution)/shard_map/pack/pallas_call | solution.py:526
  2.3 0.7 collective-permute-start.1
  3.0 4.4 %collective-permute-start = (f32[4,164,128]{2,1,0:T(8,128)S(1)}, f32[4,164,128]{2,1,0:T(8,128)S(1)}, u32[]{:S(2)}, u32[]{:S(2)}) collective-permute-start(f32[4,164,128]{2,1,0:T(8,128)S(1)} %get-tuple-element.30.mine_ref), channel_id=1, source_target_pairs={{0,1},{1,0},{2,3},{3,2},{4,5},{5,4},{6,7},{7,6},{8,9},{9,8},{10,11... | collective-permute-start | bytes 1007624 | tf_op jit(solution)/shard_map/ppermute | solution.py:520
  7.4 0.5 own0.1.z_mine
  7.9 0.0 collective-permute-done.1.refs_1_.odd_ref
  7.9 0.7 collective-permute-done.refs_0_.even_ref
  8.7 0.6 shard_map.59
  9.2 2.4 %krylov.3 = (f32[4,6,384,128]{3,2,1,0:T(8,128)S(1)}, f32[32,4,128]{2,1,0:T(4,128)S(1)}) custom-call(s32[1]{0:T(128)} %bitcast.parity_ref, f32[4,164,128]{2,1,0:T(8,128)S(1)} %get-tuple-element.30.mine_ref, f32[4,164,128]{2,1,0:T(8,128)S(1)} %collective-permute-done.refs_0_.even_ref, f32[4,164,128]{2,1,0:T(8,128)S(1)} %collective-permute-done.1.refs_1_.odd_ref, ...), custom_call_target="tpu_custom_call" | custom-call | tf_op jit(solution)/shard_map/krylov/pallas_call | solution.py:611
  11.7 20.4 %all_to_all.15.gram_ref = f32[32,4,128]{2,1,0:T(4,128)S(1)} all-to-all(f32[32,4,128]{2,1,0:T(4,128)S(1)} %get-tuple-element.34), channel_id=1, replica_groups=mesh['rows'=32] {'rows'}, dimensions={0} | all-to-all | bytes 131072 | tf_op jit(solution)/shard_map/all_to_all | solution.py:620
  32.1 0.6 shard_map.60
  32.7 0.7 collective-permute-start.3
  33.4 1.8 %collective-permute-start.2 = (f32[4,128,128]{2,1,0:T(8,128)S(1)}, f32[4,128,128]{2,1,0:T(8,128)S(1)}, u32[]{:S(2)}, u32[]{:S(2)}) collective-permute-start(f32[4,128,128]{2,1,0:T(8,128)S(1)} %get-tuple-element.37.mine_ref), channel_id=1, source_target_pairs={{0,1},{1,0},{2,3},{3,2},{4,5},{5,4},{6,7},{7,6},{8,9},{9,8},{10,11... | collective-permute-start | bytes 786440 | tf_op jit(solution)/shard_map/ppermute | solution.py:520
  35.3 0.7 collective-permute-start.5
  35.9 3.0 %collective-permute-start.4 = (f32[4,36,128]{2,1,0:T(8,128)S(1)}, f32[4,36,128]{2,1,0:T(8,128)S(1)}, u32[]{:S(2)}, u32[]{:S(2)}) collective-permute-start(f32[4,36,128]{2,1,0:T(8,128)S(1)} %get-tuple-element.36.mass_ref.refs_2_), channel_id=1, source_target_pairs={{0,1},{1,0},{2,3},{3,2},{4,5},{5,4},{6,7},{7,6},{8,9},{9,8},{10,11... | collective-permute-start | bytes 221192 | tf_op jit(solution)/shard_map/ppermute | solution.py:520
  39.0 0.0 collective-permute-done.5.refs_4_
  39.0 0.9 %collective-permute-done.4.refs_3_ = f32[4,36,128]{2,1,0:T(8,128)S(1)} collective-permute-done((f32[4,36,128]{2,1,0:T(8,128)S(1)}, f32[4,36,128]{2,1,0:T(8,128)S(1)}, u32[]{:S(2)}, u32[]{:S(2)}) %collective-permute-start.4) | collective-permute-done | bytes 73760 | tf_op jit(solution)/shard_map/ppermute | solution.py:520
  39.9 1.6 %shard_map.61 = (f32[3,4,32,512]{3,2,1,0:T(8,128)}, f32[9,4,16,128]{3,2,1,0:T(8,128)S(1)}, f32[14,16,128]{2,1,0:T(8,128)S(1)}, f32[3,136,8,128]{3,2,1,0:T(8,128)...) custom-call(s32[1]{0:T(128)} %bitcast.parity_ref, f32[3,8,128]{2,1,0:T(8,128)S(1)} %get-tuple-element.29.shift_ref, ...), custom_call_target="tpu_custom_call" | custom-call | tf_op jit(solution)/shard_map/pallas_call | solution.py:586
  41.5 0.0 collective-permute-done.3.odd_ref
  41.5 0.0 collective-permute-done.2.even_ref
  41.5 2.4 %krylov.4 = (f32[4,6,384,128]{3,2,1,0:T(8,128)S(1)}, f32[32,4,128]{2,1,0:T(4,128)S(1)}) custom-call(s32[1]{0:T(128)} %bitcast.parity_ref, f32[4,128,128]{2,1,0:T(8,128)S(1)} %get-tuple-element.37.mine_ref, f32[4,128,128]{2,1,0:T(8,128)S(1)} %collective-permute-done.2.even_ref, f32[4,128,128]{2,1,0:T(8,128)S(1)} %collective-permute-done.3.odd_ref, ...), custom_call_target="tpu_custom_call" | custom-call | tf_op jit(solution)/shard_map/krylov/pallas_call | solution.py:611
  43.9 14.5 %all_to_all.16.gram_ref = f32[32,4,128]{2,1,0:T(4,128)S(1)} all-to-all(f32[32,4,128]{2,1,0:T(4,128)S(1)} %get-tuple-element.43), channel_id=1, replica_groups=mesh['rows'=32] {'rows'}, dimensions={0} | all-to-all | bytes 131072 | tf_op jit(solution)/shard_map/all_to_all | solution.py:620
  58.4 0.6 shard_map.62
  59.0 0.9 %collective-permute-start.7 = (f32[4,128,128]{2,1,0:T(8,128)S(1)}, f32[4,128,128]{2,1,0:T(8,128)S(1)}, u32[]{:S(2)}, u32[]{:S(2)}) collective-permute-start(f32[4,128,128]{2,1,0:T(8,128)S(1)} %get-tuple-element.45.mine_ref), channel_id=1, source_target_pairs={{1,2},{3,4},{5,6},{7,8},{9,10},{11,12},{13,14},{15,16},{17,18},{19... | collective-permute-start | bytes 786440 | tf_op jit(solution)/shard_map/ppermute | solution.py:520
  59.9 1.8 %collective-permute-start.6 = (f32[4,128,128]{2,1,0:T(8,128)S(1)}, f32[4,128,128]{2,1,0:T(8,128)S(1)}, u32[]{:S(2)}, u32[]{:S(2)}) collective-permute-start(f32[4,128,128]{2,1,0:T(8,128)S(1)} %get-tuple-element.45.mine_ref), channel_id=1, source_target_pairs={{0,1},{1,0},{2,3},{3,2},{4,5},{5,4},{6,7},{7,6},{8,9},{9,8},{10,11... | collective-permute-start | bytes 786440 | tf_op jit(solution)/shard_map/ppermute | solution.py:520
  61.8 1.6 %shard_map.63 = (f32[3,4,32,512]{3,2,1,0:T(8,128)}, f32[9,4,16,128]{3,2,1,0:T(8,128)S(1)}, f32[14,16,128]{2,1,0:T(8,128)S(1)}, f32[3,136,8,128]{3,2,1,0:T(8,128)S(1)}, f32[6,128,128]{2,1,0:T(8,128)S(1)}) custom-call(s32[1]{0:T(128)} %bitcast.parity_ref, f32[3,8,128]{2,1,0:T(8,128)S(1)} %get-tuple-element.29.shift_ref, ...), custom_call_target="tpu_custom_call", output_to_operand_aliasing={{0}: (6, {})} | custom-call | tf_op jit(solution)/shard_map/pallas_call | solution.py:586
  63.3 0.0 collective-permute-done.7.odd_ref
  63.3 0.0 collective-permute-done.6.even_ref
  63.3 2.5 %krylov.5 = (f32[4,6,384,128]{3,2,1,0:T(8,128)S(1)}, f32[32,4,128]{2,1,0:T(4,128)S(1)}) custom-call(s32[1]{0:T(128)} %bitcast.parity_ref, f32[4,128,128]{2,1,0:T(8,128)S(1)} %get-tuple-element.45.mine_ref, f32[4,128,128]{2,1,0:T(8,128)S(1)} %collective-permute-done.6.even_ref, f32[4,128,128]{2,1,0:T(8,128)S(1)} %collective-permute-done.7.odd_ref, ...), custom_call_target="tpu_custom_call" | custom-call | tf_op jit(solution)/shard_map/krylov/pallas_call | solution.py:611
  65.8 15.6 %all_to_all.17.gram_ref = f32[32,4,128]{2,1,0:T(4,128)S(1)} all-to-all(f32[32,4,128]{2,1,0:T(4,128)S(1)} %get-tuple-element.53), channel_id=1, replica_groups=mesh['rows'=32] {'rows'}, dimensions={0} | all-to-all | bytes 131072 | tf_op jit(solution)/shard_map/all_to_all | solution.py:620
  81.4 1.7 %shard_map.64 = (f32[3,4,32,512]{3,2,1,0:T(8,128)}, f32[4,32,512]{2,1,0:T(8,128)}) custom-call(f32[3,8,128]{2,1,0:T(8,128)S(1)} %get-tuple-element.29.shift_ref, f32[32,4,128]{2,1,0:T(4,128)S(1)} %all_to_all.17.gram_ref, f32[4,6,384,128]{3,2,1,0:T(8,128)S(1)} %get-tuple-element.54.z_ref, ...), custom_call_target="tpu_custom_call", output_to_operand_aliasing={{0}: (5, {})} | custom-call | tf_op jit(solution)/shard_map/pallas_call | solution.py:623
Async XLA Ops:
  2.3 5.6 %collective-permute-start.1 = (f32[4,164,128]{2,1,0:T(8,128)S(1)}, f32[4,164,128]{2,1,0:T(8,128)S(1)}, u32[]{:S(2)}, u32[]{:S(2)}) collective-permute-start(f32[4,164,128]{2,1,0:T(8,128)S(1)} %get-tuple-element.30.mine_ref), channel_id=1, source_target_pairs={{1,2},{3,4},{5,6},{7,8},{9,10},{11,12},{13,14},{15,16},{17,18},{19... | collective-permute-start | bytes 1007624 | tf_op jit(solution)/shard_map/ppermute | solution.py:520
  3.0 5.7 %collective-permute-start = (f32[4,164,128]{2,1,0:T(8,128)S(1)}, f32[4,164,128]{2,1,0:T(8,128)S(1)}, u32[]{:S(2)}, u32[]{:S(2)}) collective-permute-start(f32[4,164,128]{2,1,0:T(8,128)S(1)} %get-tuple-element.30.mine_ref), channel_id=1, source_target_pairs={{0,1},{1,0},{2,3},{3,2},{4,5},{5,4},{6,7},{7,6},{8,9},{9,8},{10,11... | collective-permute-start | bytes 1007624 | tf_op jit(solution)/shard_map/ppermute | solution.py:520
  32.7 8.7 %collective-permute-start.3 = (f32[4,128,128]{2,1,0:T(8,128)S(1)}, f32[4,128,128]{2,1,0:T(8,128)S(1)}, u32[]{:S(2)}, u32[]{:S(2)}) collective-permute-start(f32[4,128,128]{2,1,0:T(8,128)S(1)} %get-tuple-element.37.mine_ref), channel_id=1, source_target_pairs={{1,2},{3,4},{5,6},{7,8},{9,10},{11,12},{13,14},{15,16},{17,18},{19... | collective-permute-start | bytes 786440 | tf_op jit(solution)/shard_map/ppermute | solution.py:520
  33.4 8.1 %collective-permute-start.2 = (f32[4,128,128]{2,1,0:T(8,128)S(1)}, f32[4,128,128]{2,1,0:T(8,128)S(1)}, u32[]{:S(2)}, u32[]{:S(2)}) collective-permute-start(f32[4,128,128]{2,1,0:T(8,128)S(1)} %get-tuple-element.37.mine_ref), channel_id=1, source_target_pairs={{0,1},{1,0},{2,3},{3,2},{4,5},{5,4},{6,7},{7,6},{8,9},{9,8},{10,11... | collective-permute-start | bytes 786440 | tf_op jit(solution)/shard_map/ppermute | solution.py:520
  35.3 3.7 %collective-permute-start.5 = (f32[4,36,128]{2,1,0:T(8,128)S(1)}, f32[4,36,128]{2,1,0:T(8,128)S(1)}, u32[]{:S(2)}, u32[]{:S(2)}) collective-permute-start(f32[4,36,128]{2,1,0:T(8,128)S(1)} %get-tuple-element.36.mass_ref.refs_2_), channel_id=1, source_target_pairs={{1,2},{3,4},{5,6},{7,8},{9,10},{11,12},{13,14},{15,16},{17,18},{19... | collective-permute-start | bytes 221192 | tf_op jit(solution)/shard_map/ppermute | solution.py:520
  35.9 4.0 %collective-permute-start.4 = (f32[4,36,128]{2,1,0:T(8,128)S(1)}, f32[4,36,128]{2,1,0:T(8,128)S(1)}, u32[]{:S(2)}, u32[]{:S(2)}) collective-permute-start(f32[4,36,128]{2,1,0:T(8,128)S(1)} %get-tuple-element.36.mass_ref.refs_2_), channel_id=1, source_target_pairs={{0,1},{1,0},{2,3},{3,2},{4,5},{5,4},{6,7},{7,6},{8,9},{9,8},{10,11... | collective-permute-start | bytes 221192 | tf_op jit(solution)/shard_map/ppermute | solution.py:520
  59.0 4.3 %collective-permute-start.7 = (f32[4,128,128]{2,1,0:T(8,128)S(1)}, f32[4,128,128]{2,1,0:T(8,128)S(1)}, u32[]{:S(2)}, u32[]{:S(2)}) collective-permute-start(f32[4,128,128]{2,1,0:T(8,128)S(1)} %get-tuple-element.45.mine_ref), channel_id=1, source_target_pairs={{1,2},{3,4},{5,6},{7,8},{9,10},{11,12},{13,14},{15,16},{17,18},{19... | collective-permute-start | bytes 786440 | tf_op jit(solution)/shard_map/ppermute | solution.py:520
  59.9 3.4 %collective-permute-start.6 = (f32[4,128,128]{2,1,0:T(8,128)S(1)}, f32[4,128,128]{2,1,0:T(8,128)S(1)}, u32[]{:S(2)}, u32[]{:S(2)}) collective-permute-start(f32[4,128,128]{2,1,0:T(8,128)S(1)} %get-tuple-element.45.mine_ref), channel_id=1, source_target_pairs={{0,1},{1,0},{2,3},{3,2},{4,5},{5,4},{6,7},{7,6},{8,9},{9,8},{10,11... | collective-permute-start | bytes 786440 | tf_op jit(solution)/shard_map/ppermute | solution.py:520
